TPU v7x, 256 devices: a whole 4x4x8 slice. The times are simulated.
256 devices in a mesh: batch: 128 (over x_hi, y, z, core), rep: 2 (over x_lo).
Axes of the slice: x: 4 (x_hi: 2, x_lo: 2; x = x_hi * 2 + x_lo), y: 4, z: 8, core: 2. Of those that a mesh axis runs over, the one named last changes fastest.
Arguments:
- image_embed: bfloat16 [16384, 1024], P('batch'), may hold values from -2 to 2
- text_embed: bfloat16 [16384, 1024], P(('batch', 'rep')), may hold values from -2 to 2
- logit_scale: float32 [1], replicated, may hold values from 50 to 100
Outputs:
- mean_loss: float32 [], replicated
- image_grad: float32 [16384, 1024], P(('batch', 'rep'))
- text_grad: float32 [16384, 1024], P(('batch', 'rep'))
All inputs are finite; a program needn't handle non-finite values.
Results may differ from a plain program's by a relative error of at most 0.0025.
Values may be sent and summed in bfloat16 or wider, within the bound.
No kernel may reach another device: no remote copies, remote signals or barrier semaphores. Data moves between devices by JAX's collectives and lax.ppermute only.
A program may use at most 128 MiB of HBM per device.

v0:
```python
import jax
import jax.numpy as jnp
from jax import lax
from jax.experimental import pallas as pl
from jax.experimental.pallas import tpu as pltpu
from jax.sharding import Mesh
from jax.sharding import PartitionSpec as P


BATCH = ("xh", "y", "z", "c")
BATCH_REP = ("xh", "y", "z", "c", "xl")
PLANE = ("xh", "y", "xl")
LINE = ("z", "c")
WIRE_SCALE = 8.0
ROWS = 64
LINE_Z = 8
PLANE_N = 16
HALF = LINE_Z * ROWS
BLOCK = 2 * HALF
LANES = 128
TILES = BLOCK // LANES
STEP = 256
FAR_FIRST = (4, 3, 5, 2, 6, 1, 7)
NT = (((1,), (1,)), ((), ()))
NN = (((1,), (0,)), ((), ()))
TN = (((0,), (0,)), ((), ()))


def exchanged(message, axis):
    return lax.all_to_all(message, axis, 0, 0, tiled=True)


def shifted(array, by):
    return lax.ppermute(array, "z", [(k, (k + by) % LINE_Z) for k in range(LINE_Z)])


def swapped(array):
    return lax.ppermute(array, "c", [(0, 1), (1, 0)])


def as_column(line):
    return jnp.transpose(jnp.broadcast_to(line, (LANES, LANES)))[:ROWS, :1]


def as_line(column):
    return jnp.transpose(jnp.broadcast_to(column, (LANES, LANES)))[:1]


def placed(slots, pos):
    turned = [pltpu.roll(slots[at : at + LINE_Z], pos[1], 0) for at in (0, LINE_Z)]
    return jnp.where(
        pos[0] == 0, jnp.concatenate(turned, axis=0), jnp.concatenate(turned[::-1], axis=0)
    )


def relative(slots, pos):
    back = lax.rem(LINE_Z - pos[1], LINE_Z)
    turned = [pltpu.roll(slots[at : at + LINE_Z], back, 0) for at in (0, LINE_Z)]
    return jnp.where(
        pos[0] == 0, jnp.concatenate(turned, axis=0), jnp.concatenate(turned[::-1], axis=0)
    )


def scores_kernel(pos, scale, own_text, text, *refs):
    blocks, (scores, image, row_message, col_part) = refs[: 2 * LINE_Z], refs[2 * LINE_Z :]
    for k in range(2 * LINE_Z):
        image[k * ROWS : (k + 1) * ROWS, :] = blocks[k][...]
    scale_value = scale[0]
    diag = scale_value * jnp.sum(
        blocks[0][...].astype(jnp.float32) * own_text[...].astype(jnp.float32)
    )
    text_rows = text[...]
    col_max = col_sum = None
    lines = []
    for i in range(BLOCK // STEP):
        span = slice(i * STEP, (i + 1) * STEP)
        part = scale_value * lax.dot_general(
            image[span, :], text_rows, NT, preferred_element_type=jnp.float32
        )
        scores[span, :] = part
        biggest = jnp.max(part, axis=1, keepdims=True)
        lse = biggest + jnp.log(jnp.sum(jnp.exp(part - biggest), axis=1, keepdims=True))
        for t in range(STEP // LANES):
            line = as_line(lse[t * LANES : (t + 1) * LANES])
            lines += [line, pltpu.roll(line, ROWS, 1)]
        top = jnp.max(part, axis=0, keepdims=True)
        new = top if i == 0 else jnp.maximum(col_max, top)
        total = jnp.sum(jnp.exp(part - new), axis=0, keepdims=True)
        col_sum = total if i == 0 else col_sum * jnp.exp(col_max - new) + total
        col_max = new
    slots = placed(jnp.concatenate(lines, axis=0), pos)
    lanes = lax.broadcasted_iota(jnp.int32, slots.shape, 1)
    message = jnp.where(lanes < ROWS, slots, diag)
    row_message[...] = jnp.broadcast_to(message[None], row_message.shape)
    col_lse = col_max + jnp.log(col_sum)
    for i in range(TILES):
        col_part[i : i + 1, :] = col_lse[:, i * LANES : (i + 1) * LANES]


def joined(stats):
    biggest = jnp.max(stats, axis=0)
    return biggest + jnp.log(jnp.sum(jnp.exp(stats - biggest[None]), axis=0))


def rows_kernel(pos, heard, col_part, row_lse, col_message):
    lse = joined(heard[...])
    lanes = lax.broadcasted_iota(jnp.int32, lse.shape, 1)
    diag = jnp.sum(heard[...], axis=0)[:TILES, ROWS : ROWS + 1]
    extra = jnp.sum(jnp.where(lanes < ROWS, lse, 0.0)) - 2.0 * diag
    row_lse[...] = relative(lse, pos)
    message = jnp.concatenate([col_part[...], jnp.broadcast_to(extra, (TILES, LANES))], axis=0)
    col_message[...] = jnp.broadcast_to(message[None], col_message.shape)


def weights_kernel(pos, scores, row_lse, heard, weights, loss_message, rows_loss):
    col_lse = joined(heard[:, :TILES, :])
    rows_loss[...] = jnp.sum(heard[:, TILES:, :], axis=0)
    loss_message[...] = jnp.full(loss_message.shape, jnp.sum(col_lse))
    col_line = jnp.concatenate([col_lse[i : i + 1] for i in range(TILES)], axis=1)
    for k in range(2 * LINE_Z):
        span = slice(k * ROWS, (k + 1) * ROWS)
        part = scores[span, :]
        both = jnp.exp(part - as_column(row_lse[k : k + 1, :])) + jnp.exp(part - col_line)
        if k == 0:
            row_ids = lax.broadcasted_iota(jnp.int32, part.shape, 0)
            column_ids = lax.broadcasted_iota(jnp.int32, part.shape, 1) - pos[2] * ROWS
            both = both - 2.0 * (row_ids == column_ids).astype(jnp.float32)
        weights[span, :] = both.astype(jnp.bfloat16)


def call(kernel, outs, spec, *args):
    vmem = pl.BlockSpec(memory_space=pltpu.VMEM)
    smem = pl.BlockSpec(memory_space=pltpu.SMEM)
    return pl.pallas_call(
        kernel,
        out_shape=[jax.ShapeDtypeStruct(*o) for o in outs],
        in_specs=[smem if s == "s" else vmem for s in spec],
        out_specs=[vmem] * len(outs),
        compiler_params=pltpu.CompilerParams(vmem_limit_bytes=48 * 1024 * 1024),
    )(*args)


def parts(image_embed, text_embed, logit_scale):
    f32, f16, bf16 = jnp.float32, jnp.float16, jnp.bfloat16
    width = text_embed.shape[1]
    pos = jnp.stack(
        [lax.axis_index("c"), lax.axis_index("z"), lax.axis_index(PLANE)]
    ).astype(jnp.int32)
    own_image = lax.dynamic_slice_in_dim(image_embed, lax.axis_index("xl") * ROWS, ROWS, 0)

    text_all = exchanged(
        jnp.broadcast_to(text_embed[None], (PLANE_N, *text_embed.shape)), PLANE
    ).reshape(BLOCK, width)
    near = [own_image] + [None] * (LINE_Z - 1)
    for k in FAR_FIRST:
        near[k] = shifted(own_image, -k)
    far = [None] * LINE_Z
    for k in range(LINE_Z):
        far[k] = swapped(near[k])

    message = (PLANE_N, 2 * TILES, LANES)
    scores, image_all, row_message, col_part = call(
        scores_kernel,
        [((BLOCK, BLOCK), f32), ((BLOCK, width), bf16), (message, f32), ((TILES, LANES), f32)],
        "ss" + "v" * (2 + 2 * LINE_Z),
        pos, logit_scale, text_embed, text_all, *near, *far,
    )
    row_lse, col_message = call(
        rows_kernel,
        [((2 * LINE_Z, LANES), f32), (message, f32)],
        "svv",
        pos, exchanged(row_message, LINE), col_part,
    )
    weights, loss_message, rows_loss = call(
        weights_kernel,
        [((BLOCK, BLOCK), bf16), ((PLANE_N, TILES, LANES), f32), ((TILES, LANES), f32)],
        "svvv",
        pos, scores, row_lse, exchanged(col_message, PLANE),
    )
    heard = exchanged(loss_message, LINE)
    mean_loss = (rows_loss[0, 0] + jnp.sum(heard[:, 0, 0])) / (2 * ROWS * 256)

    other = lax.dot_general(weights[HALF:], text_all, NN, preferred_element_type=f32)
    arrived = swapped((WIRE_SCALE * other).astype(f16))
    text_part = lax.dot_general(weights, image_all, TN, preferred_element_type=f32)
    text_part = (WIRE_SCALE * text_part).astype(f16).reshape(PLANE_N, ROWS, width)
    text_sum = exchanged(text_part, PLANE).astype(f32).sum(axis=0)
    image_part = WIRE_SCALE * lax.dot_general(
        weights[:HALF], text_all, NN, preferred_element_type=f32
    ) + arrived.astype(f32)
    image_part = image_part.reshape(LINE_Z, ROWS, width)
    back = {}
    for k in FAR_FIRST:
        back[k] = shifted(image_part[k].astype(f16), k)
    image_sum = image_part[0]
    for k in range(1, LINE_Z):
        image_sum = image_sum + back[k].astype(f32)
    factor = logit_scale[0] * (0.5 / WIRE_SCALE)
    return (mean_loss, factor * image_sum, factor * text_sum)


def solution(mesh):
    split = Mesh(mesh.devices.reshape(2, 4, LINE_Z, 2, mesh.shape["rep"]), BATCH_REP)
    return jax.shard_map(
        parts,
        mesh=split,
        in_specs=(P(BATCH, None), P(BATCH_REP, None), P()),
        out_specs=(P(), P(BATCH_REP, None), P(BATCH_REP, None)),
        check_vma=False,
    )
```

profile of v0, /device:TPU:33, one launch (start us, length us, event | category | flops | bytes accessed | tf_op | source)
XLA Modules:
  0.0 147.2 jit_solution(16445991416810810252)
XLA Ops:
  0.6 2.5 %broadcast_in_dim.2 = bf16[16,64,1024]{2,1,0:T(8,128)(2,1)} broadcast(bf16[64,1024]{1,0:T(8,128)(2,1)} %own_text.1), dimensions={1,2} | broadcast | bytes 2228224 | tf_op jit(solution)/shard_map/broadcast_in_dim | solution.py:152
  3.2 6.9 %all-to-all-start = ((bf16[16,64,1024]{2,1,0:T(8,128)(2,1)}), bf16[16,64,1024]{2,1,0:T(8,128)(2,1)}, u32[]{:S(2)}, u32[]{:S(2)}) async-start(bf16[16,64,1024]{2,1,0:T(8,128)(2,1)} %broadcast_in_dim.2), calls=%async_computation | async-start | bytes 4194304 | tf_op jit(solution)/shard_map/all_to_all | solution.py:30
  10.2 1.0 collective-permute-start.7
  11.2 1.6 %collective-permute-start.6 = (bf16[64,1024]{1,0:T(8,128)(2,1)S(1)}, bf16[64,1024]{1,0:T(8,128)(2,1)S(1)}, u32[]{:S(2)}, u32[]{:S(2)}) collective-permute-start(bf16[64,1024]{1,0:T(8,128)(2,1)S(1)} %constant_dynamic-slice_fusion.refs_0_), channel_id=1, source_target_pairs={{0,4},{4,8},{8,12},{12,16},{16,20},{20,24},{24,28},{28,0},{1,5},{5... | collective-permute-start | bytes 393224 | tf_op jit(solution)/shard_map/ppermute | solution.py:34
  12.8 4.2 %collective-permute-start.5 = (bf16[64,1024]{1,0:T(8,128)(2,1)S(1)}, bf16[64,1024]{1,0:T(8,128)(2,1)S(1)}, u32[]{:S(2)}, u32[]{:S(2)}) collective-permute-start(bf16[64,1024]{1,0:T(8,128)(2,1)S(1)} %constant_dynamic-slice_fusion.refs_0_), channel_id=1, source_target_pairs={{0,8},{4,12},{8,16},{12,20},{16,24},{20,28},{24,0},{28,4},{1,9},{5... | collective-permute-start | bytes 393224 | tf_op jit(solution)/shard_map/ppermute | solution.py:34
  17.0 1.6 %collective-permute-start.4 = (bf16[64,1024]{1,0:T(8,128)(2,1)S(1)}, bf16[64,1024]{1,0:T(8,128)(2,1)S(1)}, u32[]{:S(2)}, u32[]{:S(2)}) collective-permute-start(bf16[64,1024]{1,0:T(8,128)(2,1)S(1)} %constant_dynamic-slice_fusion.refs_0_), channel_id=1, source_target_pairs={{0,12},{4,16},{8,20},{12,24},{16,28},{20,0},{24,4},{28,8},{1,13},{... | collective-permute-start | bytes 393224 | tf_op jit(solution)/shard_map/ppermute | solution.py:34
  18.7 1.2 collective-permute-start.3
  19.9 3.0 %collective-permute-start.2 = (bf16[64,1024]{1,0:T(8,128)(2,1)S(1)}, bf16[64,1024]{1,0:T(8,128)(2,1)S(1)}, u32[]{:S(2)}, u32[]{:S(2)}) collective-permute-start(bf16[64,1024]{1,0:T(8,128)(2,1)S(1)} %constant_dynamic-slice_fusion.refs_0_), channel_id=1, source_target_pairs={{0,20},{4,24},{8,28},{12,0},{16,4},{20,8},{24,12},{28,16},{1,21},{... | collective-permute-start | bytes 393224 | tf_op jit(solution)/shard_map/ppermute | solution.py:34
  22.9 1.9 %collective-permute-start.1 = (bf16[64,1024]{1,0:T(8,128)(2,1)S(1)}, bf16[64,1024]{1,0:T(8,128)(2,1)S(1)}, u32[]{:S(2)}, u32[]{:S(2)}) collective-permute-start(bf16[64,1024]{1,0:T(8,128)(2,1)S(1)} %constant_dynamic-slice_fusion.refs_0_), channel_id=1, source_target_pairs={{0,24},{4,28},{8,0},{12,4},{16,8},{20,12},{24,16},{28,20},{1,25},{... | collective-permute-start | bytes 393224 | tf_op jit(solution)/shard_map/ppermute | solution.py:34
  24.8 1.4 collective-permute-done.5.refs_6_
  26.7 11.1 %collective-permute-done.4.refs_5_ = bf16[64,1024]{1,0:T(8,128)(2,1)S(1)} collective-permute-done((bf16[64,1024]{1,0:T(8,128)(2,1)S(1)}, bf16[64,1024]{1,0:T(8,128)(2,1)S(1)}, u32[]{:S(2)}, u32[]{:S(2)}) %collective-permute-start.4) | collective-permute-done | bytes 131104 | tf_op jit(solution)/shard_map/ppermute | solution.py:34
  37.9 1.5 %collective-permute-start.14 = (bf16[64,1024]{1,0:T(8,128)(2,1)S(1)}, bf16[64,1024]{1,0:T(8,128)(2,1)S(1)}, u32[]{:S(2)}, u32[]{:S(2)}) collective-permute-start(bf16[64,1024]{1,0:T(8,128)(2,1)S(1)} %collective-permute-done.6.refs_7_), channel_id=1, source_target_pairs={{0,2},{2,0},{1,3},{3,1},{4,6},{6,4},{5,7},{7,5},{8,10},{10,8},{9,1... | collective-permute-start | bytes 393224 | tf_op jit(solution)/shard_map/ppermute | solution.py:38
  40.2 5.6 %collective-permute-start.11 = (bf16[64,1024]{1,0:T(8,128)(2,1)S(1)}, bf16[64,1024]{1,0:T(8,128)(2,1)S(1)}, u32[]{:S(2)}, u32[]{:S(2)}) collective-permute-start(bf16[64,1024]{1,0:T(8,128)(2,1)S(1)} %collective-permute-done.3.refs_4_), channel_id=1, source_target_pairs={{0,2},{2,0},{1,3},{3,1},{4,6},{6,4},{5,7},{7,5},{8,10},{10,8},{9,1... | collective-permute-start | bytes 393224 | tf_op jit(solution)/shard_map/ppermute | solution.py:38
  45.8 1.0 collective-permute-done.refs_1_
  48.9 6.7 %shard_map.58 = (f32[1024,1024]{1,0:T(8,128)}, bf16[1024,1024]{1,0:T(8,128)(2,1)S(1)}, f32[16,16,128]{2,1,0:T(8,128)S(1)}, f32[8,128]{1,0:T(8,128)S(1)}) custom-call(s32[3]{0:T(128)S(1)} %pad_add_fusion.pos, f32[1]{0:T(128)S(6)} %copy.6.scale, bf16[64,1024]{1,0:T(8,128)(2,1)S(1)} %copy-done.1, bf16[1024,1024]{1,0:T(8,128)(2,1)} %bitcast.3.text, ...), custom_call_target="tpu_custom_call" | custom-call | tf_op jit(solution)/shard_map/pallas_call | solution.py:134
  55.6 1.3 copy-done.2
  56.9 11.4 %all_to_all.25.heard = f32[16,16,128]{2,1,0:T(8,128)S(1)} all-to-all(f32[16,16,128]{2,1,0:T(8,128)S(1)} %get-tuple-element.13), channel_id=1, replica_groups=mesh['xh'=2,'y'=4,'z'=8,'c'=2,'xl'=2] {'z','c'}, dimensions={0} | all-to-all | bytes 262144 | tf_op jit(solution)/shard_map/all_to_all | solution.py:30
  69.1 13.8 %all_to_all.26.heard = f32[16,16,128]{2,1,0:T(8,128)S(1)} all-to-all(f32[16,16,128]{2,1,0:T(8,128)S(1)} %get-tuple-element.16), channel_id=1, replica_groups=mesh['xh'=2,'y'=4,'z'=8,'c'=2,'xl'=2] {'xh','y','xl'}, dimensions={0} | all-to-all | bytes 262144 | tf_op jit(solution)/shard_map/all_to_all | solution.py:30
  82.9 3.6 %shard_map.60 = (bf16[1024,1024]{1,0:T(8,128)(2,1)S(1)}, f32[16,8,128]{2,1,0:T(8,128)}, f32[8,128]{1,0:T(8,128)S(1)}) custom-call(s32[3]{0:T(128)S(1)} %pad_add_fusion.pos, f32[1024,1024]{1,0:T(8,128)} %get-tuple-element.12.scores, f32[16,128]{1,0:T(8,128)S(1)} %get-tuple-element.15.row_lse, f32[16,16,128]{2,1,0:T(8,128)S(1)} %all_to_all.26.heard), custom_call_target="tpu_custom_call" | custom-call | tf_op jit(solution)/shard_map/pallas_call | solution.py:134
  86.5 5.5 %all-to-all-start.3 = ((f32[16,8,128]{2,1,0:T(8,128)}), f32[16,8,128]{2,1,0:T(8,128)S(1)}, u32[]{:S(2)}, u32[]{:S(2)}) async-start(f32[16,8,128]{2,1,0:T(8,128)} %get-tuple-element.18), calls=%async_computation.3 | async-start | bytes 131072 | tf_op jit(solution)/shard_map/all_to_all | solution.py:30
  92.0 4.0 %multiply_convert_fusion.1 = f16[512,1024]{1,0:T(8,128)(2,1)} fusion(bf16[1024,1024]{1,0:T(8,128)(2,1)} %bitcast.3.text, bf16[1024,1024]{1,0:T(8,128)(2,1)S(1)} %get-tuple-element.19), kind=kOutput, calls=%fused_computation.3 | convolution fusion | flops 1074790400 | bytes 4194304 | tf_op jit(solution)/shard_map/dot_general | solution.py:183
  96.4 3.8 %multiply_convert_fusion = f16[1024,1024]{1,0:T(8,128)(2,1)} fusion(bf16[1024,1024]{1,0:T(8,128)(2,1)S(1)} %get-tuple-element.19, bf16[1024,1024]{1,0:T(8,128)(2,1)S(1)} %copy-done.3), kind=kOutput, calls=%fused_computation.1 | convolution fusion | flops 2149580800 | bytes 6291456 | tf_op jit(solution)/shard_map/dot_general | solution.py:185
  100.2 4.4 %all-to-all-start.4 = ((f16[16,64,1024]{2,1,0:T(8,128)(2,1)}), f16[16,64,1024]{2,1,0:T(8,128)(2,1)}, u32[]{:S(2)}, u32[]{:S(2)}) async-start(f16[16,64,1024]{2,1,0:T(8,128)(2,1)} %bitcast.11), calls=%async_computation.4 | async-start | bytes 4194304 | tf_op jit(solution)/shard_map/all_to_all | solution.py:30
  104.7 4.3 %fusion.10 = (f16[512,1024]{1,0:T(8,128)(2,1)S(1)}, f32[512,1024]{1,0:T(8,128)}) fusion(f16[512,1024]{1,0:T(8,128)(2,1)S(1)} %collective-permute-done.15, bf16[1024,1024]{1,0:T(8,128)(2,1)} %bitcast.3.text, bf16[1024,1024]{1,0:T(8,128)(2,1)S(1)} %get-tuple-element.19), kind=kOutput, calls=%fused_computation.19 | convolution fusion | flops 1075838976 | bytes 7340032 | tf_op jit(solution)/shard_map/dot_general | solution.py:188
  109.2 1.3 collective-permute-start.16
  110.7 2.5 %collective-permute-start.21 = (f16[64,1024]{1,0:T(8,128)(2,1)S(1)}, f16[64,1024]{1,0:T(8,128)(2,1)S(1)}, u32[]{:S(2)}, u32[]{:S(2)}) collective-permute-start(f16[64,1024]{1,0:T(8,128)(2,1)S(1)} %get-tuple-element.23), channel_id=1, source_target_pairs={{0,24},{4,28},{8,0},{12,4},{16,8},{20,12},{24,16},{28,20},{1,25},{... | collective-permute-start | bytes 393224 | tf_op jit(solution)/shard_map/ppermute | solution.py:34
  113.2 4.1 %collective-permute-start.20 = (f16[64,1024]{1,0:T(8,128)(2,1)S(1)}, f16[64,1024]{1,0:T(8,128)(2,1)S(1)}, u32[]{:S(2)}, u32[]{:S(2)}) collective-permute-start(f16[64,1024]{1,0:T(8,128)(2,1)S(1)} %get-tuple-element.24), channel_id=1, source_target_pairs={{0,20},{4,24},{8,28},{12,0},{16,4},{20,8},{24,12},{28,16},{1,21},{... | collective-permute-start | bytes 393224 | tf_op jit(solution)/shard_map/ppermute | solution.py:34
  117.5 4.1 %collective-permute-start.18 = (f16[64,1024]{1,0:T(8,128)(2,1)S(1)}, f16[64,1024]{1,0:T(8,128)(2,1)S(1)}, u32[]{:S(2)}, u32[]{:S(2)}) collective-permute-start(f16[64,1024]{1,0:T(8,128)(2,1)S(1)} %get-tuple-element.26), channel_id=1, source_target_pairs={{0,12},{4,16},{8,20},{12,24},{16,28},{20,0},{24,4},{28,8},{1,13},{... | collective-permute-start | bytes 393224 | tf_op jit(solution)/shard_map/ppermute | solution.py:34
  124.3 14.8 %collective-permute-done.20 = f16[64,1024]{1,0:T(8,128)(2,1)S(1)} collective-permute-done((f16[64,1024]{1,0:T(8,128)(2,1)S(1)}, f16[64,1024]{1,0:T(8,128)(2,1)S(1)}, u32[]{:S(2)}, u32[]{:S(2)}) %collective-permute-start.20) | collective-permute-done | bytes 131104 | tf_op jit(solution)/shard_map/ppermute | solution.py:34
  139.0 2.4 %collective-permute-done.17 = f16[64,1024]{1,0:T(8,128)(2,1)S(1)} collective-permute-done((f16[64,1024]{1,0:T(8,128)(2,1)S(1)}, f16[64,1024]{1,0:T(8,128)(2,1)S(1)}, u32[]{:S(2)}, u32[]{:S(2)}) %collective-permute-start.17) | collective-permute-done | bytes 131104 | tf_op jit(solution)/shard_map/ppermute | solution.py:34
  141.4 1.8 %fusion.8 = f32[64,1024]{1,0:T(8,128)} fusion(f32[512,1024]{1,0:T(8,128)} %get-tuple-element.29, f16[64,1024]{1,0:T(8,128)(2,1)S(1)} %collective-permute-done.22, f16[64,1024]{1,0:T(8,128)(2,1)S(1)} %collective-permute-done.21, f16[64,1024]{1,0:T(8,128)(2,1)S(1)} %collective-permute-done.20, f16[64,1024]{1,0:T(8,128)(2,1)S(1)} %collective-permute-done.19, ...), kind=kLoop, calls=%fused_computation.13 | loop fusion | flops 983040 | bytes 1441796 | tf_op jit(solution)/shard_map/mul | solution.py:199
  143.3 2.1 %convert_reduce_fusion = f32[64,1024]{1,0:T(8,128)S(1)} fusion(f16[16,64,1024]{2,1,0:T(8,128)(2,1)} %all-to-all-done.4), kind=kLoop, calls=%fused_computation | loop fusion | flops 2031616 | bytes 2359296 | tf_op jit(solution)/shard_map/reduce_sum | solution.py:187
  (45 shorter events, 6.7 us)
Async XLA Ops:
  0.6 9.5 %copy-start = (bf16[128,1024]{1,0:T(8,128)(2,1)S(1)}, bf16[128,1024]{1,0:T(8,128)(2,1)}, u32[]{:S(2)}) copy-start(bf16[128,1024]{1,0:T(8,128)(2,1)} %param.3) | copy-start | bytes 786436
  3.2 45.7 %copy-start.1 = (bf16[64,1024]{1,0:T(8,128)(2,1)S(1)}, bf16[64,1024]{1,0:T(8,128)(2,1)}, u32[]{:S(2)}) copy-start(bf16[64,1024]{1,0:T(8,128)(2,1)} %own_text.1) | copy-start | bytes 393220
  3.2 45.7 %all-to-all-start = ((bf16[16,64,1024]{2,1,0:T(8,128)(2,1)}), bf16[16,64,1024]{2,1,0:T(8,128)(2,1)}, u32[]{:S(2)}, u32[]{:S(2)}) async-start(bf16[16,64,1024]{2,1,0:T(8,128)(2,1)} %broadcast_in_dim.2), calls=%async_computation | async-start | bytes 4194304 | tf_op jit(solution)/shard_map/all_to_all | solution.py:30
  10.2 9.7 %collective-permute-start.7 = (bf16[64,1024]{1,0:T(8,128)(2,1)S(1)}, bf16[64,1024]{1,0:T(8,128)(2,1)S(1)}, u32[]{:S(2)}, u32[]{:S(2)}) collective-permute-start(bf16[64,1024]{1,0:T(8,128)(2,1)S(1)} %constant_dynamic-slice_fusion.refs_0_), channel_id=1, source_target_pairs={{0,2},{2,0},{1,3},{3,1},{4,6},{6,4},{5,7},{7,5},{8,10},{10,8},{9,1... | collective-permute-start | bytes 393224 | tf_op jit(solution)/shard_map/ppermute | solution.py:38
  11.2 11.7 %collective-permute-start.6 = (bf16[64,1024]{1,0:T(8,128)(2,1)S(1)}, bf16[64,1024]{1,0:T(8,128)(2,1)S(1)}, u32[]{:S(2)}, u32[]{:S(2)}) collective-permute-start(bf16[64,1024]{1,0:T(8,128)(2,1)S(1)} %constant_dynamic-slice_fusion.refs_0_), channel_id=1, source_target_pairs={{0,4},{4,8},{8,12},{12,16},{16,20},{20,24},{24,28},{28,0},{1,5},{5... | collective-permute-start | bytes 393224 | tf_op jit(solution)/shard_map/ppermute | solution.py:34
  12.8 13.4 %collective-permute-start.5 = (bf16[64,1024]{1,0:T(8,128)(2,1)S(1)}, bf16[64,1024]{1,0:T(8,128)(2,1)S(1)}, u32[]{:S(2)}, u32[]{:S(2)}) collective-permute-start(bf16[64,1024]{1,0:T(8,128)(2,1)S(1)} %constant_dynamic-slice_fusion.refs_0_), channel_id=1, source_target_pairs={{0,8},{4,12},{8,16},{12,20},{16,24},{20,28},{24,0},{28,4},{1,9},{5... | collective-permute-start | bytes 393224 | tf_op jit(solution)/shard_map/ppermute | solution.py:34
  17.0 20.8 %collective-permute-start.4 = (bf16[64,1024]{1,0:T(8,128)(2,1)S(1)}, bf16[64,1024]{1,0:T(8,128)(2,1)S(1)}, u32[]{:S(2)}, u32[]{:S(2)}) collective-permute-start(bf16[64,1024]{1,0:T(8,128)(2,1)S(1)} %constant_dynamic-slice_fusion.refs_0_), channel_id=1, source_target_pairs={{0,12},{4,16},{8,20},{12,24},{16,28},{20,0},{24,4},{28,8},{1,13},{... | collective-permute-start | bytes 393224 | tf_op jit(solution)/shard_map/ppermute | solution.py:34
  18.7 20.7 %collective-permute-start.3 = (bf16[64,1024]{1,0:T(8,128)(2,1)S(1)}, bf16[64,1024]{1,0:T(8,128)(2,1)S(1)}, u32[]{:S(2)}, u32[]{:S(2)}) collective-permute-start(bf16[64,1024]{1,0:T(8,128)(2,1)S(1)} %constant_dynamic-slice_fusion.refs_0_), channel_id=1, source_target_pairs={{0,16},{4,20},{8,24},{12,28},{16,0},{20,4},{24,8},{28,12},{1,17},{... | collective-permute-start | bytes 393224 | tf_op jit(solution)/shard_map/ppermute | solution.py:34
  19.9 19.5 %collective-permute-start.2 = (bf16[64,1024]{1,0:T(8,128)(2,1)S(1)}, bf16[64,1024]{1,0:T(8,128)(2,1)S(1)}, u32[]{:S(2)}, u32[]{:S(2)}) collective-permute-start(bf16[64,1024]{1,0:T(8,128)(2,1)S(1)} %constant_dynamic-slice_fusion.refs_0_), channel_id=1, source_target_pairs={{0,20},{4,24},{8,28},{12,0},{16,4},{20,8},{24,12},{28,16},{1,21},{... | collective-permute-start | bytes 393224 | tf_op jit(solution)/shard_map/ppermute | solution.py:34
  22.9 17.3 %collective-permute-start.1 = (bf16[64,1024]{1,0:T(8,128)(2,1)S(1)}, bf16[64,1024]{1,0:T(8,128)(2,1)S(1)}, u32[]{:S(2)}, u32[]{:S(2)}) collective-permute-start(bf16[64,1024]{1,0:T(8,128)(2,1)S(1)} %constant_dynamic-slice_fusion.refs_0_), channel_id=1, source_target_pairs={{0,24},{4,28},{8,0},{12,4},{16,8},{20,12},{24,16},{28,20},{1,25},{... | collective-permute-start | bytes 393224 | tf_op jit(solution)/shard_map/ppermute | solution.py:34
  26.3 20.5 %collective-permute-start = (bf16[64,1024]{1,0:T(8,128)(2,1)S(1)}, bf16[64,1024]{1,0:T(8,128)(2,1)S(1)}, u32[]{:S(2)}, u32[]{:S(2)}) collective-permute-start(bf16[64,1024]{1,0:T(8,128)(2,1)S(1)} %constant_dynamic-slice_fusion.refs_0_), channel_id=1, source_target_pairs={{0,28},{4,0},{8,4},{12,8},{16,12},{20,16},{24,20},{28,24},{1,29},{... | collective-permute-start | bytes 393224 | tf_op jit(solution)/shard_map/ppermute | solution.py:34
  37.9 9.4 %collective-permute-start.14 = (bf16[64,1024]{1,0:T(8,128)(2,1)S(1)}, bf16[64,1024]{1,0:T(8,128)(2,1)S(1)}, u32[]{:S(2)}, u32[]{:S(2)}) collective-permute-start(bf16[64,1024]{1,0:T(8,128)(2,1)S(1)} %collective-permute-done.6.refs_7_), channel_id=1, source_target_pairs={{0,2},{2,0},{1,3},{3,1},{4,6},{6,4},{5,7},{7,5},{8,10},{10,8},{9,1... | collective-permute-start | bytes 393224 | tf_op jit(solution)/shard_map/ppermute | solution.py:38
  39.4 7.9 %collective-permute-start.13 = (bf16[64,1024]{1,0:T(8,128)(2,1)S(1)}, bf16[64,1024]{1,0:T(8,128)(2,1)S(1)}, u32[]{:S(2)}, u32[]{:S(2)}) collective-permute-start(bf16[64,1024]{1,0:T(8,128)(2,1)S(1)} %collective-permute-done.5.refs_6_), channel_id=1, source_target_pairs={{0,2},{2,0},{1,3},{3,1},{4,6},{6,4},{5,7},{7,5},{8,10},{10,8},{9,1... | collective-permute-start | bytes 393224 | tf_op jit(solution)/shard_map/ppermute | solution.py:38
  39.4 9.1 %collective-permute-start.12 = (bf16[64,1024]{1,0:T(8,128)(2,1)S(1)}, bf16[64,1024]{1,0:T(8,128)(2,1)S(1)}, u32[]{:S(2)}, u32[]{:S(2)}) collective-permute-start(bf16[64,1024]{1,0:T(8,128)(2,1)S(1)} %collective-permute-done.4.refs_5_), channel_id=1, source_target_pairs={{0,2},{2,0},{1,3},{3,1},{4,6},{6,4},{5,7},{7,5},{8,10},{10,8},{9,1... | collective-permute-start | bytes 393224 | tf_op jit(solution)/shard_map/ppermute | solution.py:38
  40.2 8.4 %collective-permute-start.11 = (bf16[64,1024]{1,0:T(8,128)(2,1)S(1)}, bf16[64,1024]{1,0:T(8,128)(2,1)S(1)}, u32[]{:S(2)}, u32[]{:S(2)}) collective-permute-start(bf16[64,1024]{1,0:T(8,128)(2,1)S(1)} %collective-permute-done.3.refs_4_), channel_id=1, source_target_pairs={{0,2},{2,0},{1,3},{3,1},{4,6},{6,4},{5,7},{7,5},{8,10},{10,8},{9,1... | collective-permute-start | bytes 393224 | tf_op jit(solution)/shard_map/ppermute | solution.py:38
  46.8 1.8 %collective-permute-start.10 = (bf16[64,1024]{1,0:T(8,128)(2,1)S(1)}, bf16[64,1024]{1,0:T(8,128)(2,1)S(1)}, u32[]{:S(2)}, u32[]{:S(2)}) collective-permute-start(bf16[64,1024]{1,0:T(8,128)(2,1)S(1)} %collective-permute-done.2.refs_3_), channel_id=1, source_target_pairs={{0,2},{2,0},{1,3},{3,1},{4,6},{6,4},{5,7},{7,5},{8,10},{10,8},{9,1... | collective-permute-start | bytes 393224 | tf_op jit(solution)/shard_map/ppermute | solution.py:38
  47.3 1.3 collective-permute-start.9
  47.3 1.6 %collective-permute-start.8 = (bf16[64,1024]{1,0:T(8,128)(2,1)S(1)}, bf16[64,1024]{1,0:T(8,128)(2,1)S(1)}, u32[]{:S(2)}, u32[]{:S(2)}) collective-permute-start(bf16[64,1024]{1,0:T(8,128)(2,1)S(1)} %collective-permute-done.refs_1_), channel_id=1, source_target_pairs={{0,2},{2,0},{1,3},{3,1},{4,6},{6,4},{5,7},{7,5},{8,10},{10,8},{9,1... | collective-permute-start | bytes 393224 | tf_op jit(solution)/shard_map/ppermute | solution.py:38
  55.6 1.3 copy-start.2
  86.5 13.7 %all-to-all-start.3 = ((f32[16,8,128]{2,1,0:T(8,128)}), f32[16,8,128]{2,1,0:T(8,128)S(1)}, u32[]{:S(2)}, u32[]{:S(2)}) async-start(f32[16,8,128]{2,1,0:T(8,128)} %get-tuple-element.18), calls=%async_computation.3 | async-start | bytes 131072 | tf_op jit(solution)/shard_map/all_to_all | solution.py:30
  92.0 4.4 %copy-start.3 = (bf16[1024,1024]{1,0:T(8,128)(2,1)S(1)}, bf16[1024,1024]{1,0:T(8,128)(2,1)}, u32[]{:S(2)}) copy-start(bf16[1024,1024]{1,0:T(8,128)(2,1)} %copy-done.2) | copy-start | bytes 6291460
  96.0 8.6 %collective-permute-start.15 = (f16[512,1024]{1,0:T(8,128)(2,1)}, f16[512,1024]{1,0:T(8,128)(2,1)S(1)}, u32[]{:S(2)}, u32[]{:S(2)}) collective-permute-start(f16[512,1024]{1,0:T(8,128)(2,1)} %multiply_convert_fusion.1), channel_id=1, source_target_pairs={{0,2},{2,0},{1,3},{3,1},{4,6},{6,4},{5,7},{7,5},{8,10},{10,8},{9,1... | collective-permute-start | bytes 3145736 | tf_op jit(solution)/shard_map/ppermute | solution.py:38
  100.2 43.1 %all-to-all-start.4 = ((f16[16,64,1024]{2,1,0:T(8,128)(2,1)}), f16[16,64,1024]{2,1,0:T(8,128)(2,1)}, u32[]{:S(2)}, u32[]{:S(2)}) async-start(f16[16,64,1024]{2,1,0:T(8,128)(2,1)} %bitcast.11), calls=%async_computation.4 | async-start | bytes 4194304 | tf_op jit(solution)/shard_map/all_to_all | solution.py:30
  109.2 8.3 %collective-permute-start.16 = (f16[64,1024]{1,0:T(8,128)(2,1)S(1)}, f16[64,1024]{1,0:T(8,128)(2,1)S(1)}, u32[]{:S(2)}, u32[]{:S(2)}) collective-permute-start(f16[64,1024]{1,0:T(8,128)(2,1)S(1)} %get-tuple-element.21), channel_id=1, source_target_pairs={{0,4},{4,8},{8,12},{12,16},{16,20},{20,24},{24,28},{28,0},{1,5},{5... | collective-permute-start | bytes 393224 | tf_op jit(solution)/shard_map/ppermute | solution.py:34
  110.5 11.1 %collective-permute-start.22 = (f16[64,1024]{1,0:T(8,128)(2,1)S(1)}, f16[64,1024]{1,0:T(8,128)(2,1)S(1)}, u32[]{:S(2)}, u32[]{:S(2)}) collective-permute-start(f16[64,1024]{1,0:T(8,128)(2,1)S(1)} %get-tuple-element.22), channel_id=1, source_target_pairs={{0,28},{4,0},{8,4},{12,8},{16,12},{20,16},{24,20},{28,24},{1,29},{... | collective-permute-start | bytes 393224 | tf_op jit(solution)/shard_map/ppermute | solution.py:34
  110.7 13.5 %collective-permute-start.21 = (f16[64,1024]{1,0:T(8,128)(2,1)S(1)}, f16[64,1024]{1,0:T(8,128)(2,1)S(1)}, u32[]{:S(2)}, u32[]{:S(2)}) collective-permute-start(f16[64,1024]{1,0:T(8,128)(2,1)S(1)} %get-tuple-element.23), channel_id=1, source_target_pairs={{0,24},{4,28},{8,0},{12,4},{16,8},{20,12},{24,16},{28,20},{1,25},{... | collective-permute-start | bytes 393224 | tf_op jit(solution)/shard_map/ppermute | solution.py:34
  113.2 25.8 %collective-permute-start.20 = (f16[64,1024]{1,0:T(8,128)(2,1)S(1)}, f16[64,1024]{1,0:T(8,128)(2,1)S(1)}, u32[]{:S(2)}, u32[]{:S(2)}) collective-permute-start(f16[64,1024]{1,0:T(8,128)(2,1)S(1)} %get-tuple-element.24), channel_id=1, source_target_pairs={{0,20},{4,24},{8,28},{12,0},{16,4},{20,8},{24,12},{28,16},{1,21},{... | collective-permute-start | bytes 393224 | tf_op jit(solution)/shard_map/ppermute | solution.py:34
  117.4 21.7 %collective-permute-start.19 = (f16[64,1024]{1,0:T(8,128)(2,1)S(1)}, f16[64,1024]{1,0:T(8,128)(2,1)S(1)}, u32[]{:S(2)}, u32[]{:S(2)}) collective-permute-start(f16[64,1024]{1,0:T(8,128)(2,1)S(1)} %get-tuple-element.25), channel_id=1, source_target_pairs={{0,16},{4,20},{8,24},{12,28},{16,0},{20,4},{24,8},{28,12},{1,17},{... | collective-permute-start | bytes 393224 | tf_op jit(solution)/shard_map/ppermute | solution.py:34
  117.5 21.5 %collective-permute-start.18 = (f16[64,1024]{1,0:T(8,128)(2,1)S(1)}, f16[64,1024]{1,0:T(8,128)(2,1)S(1)}, u32[]{:S(2)}, u32[]{:S(2)}) collective-permute-start(f16[64,1024]{1,0:T(8,128)(2,1)S(1)} %get-tuple-element.26), channel_id=1, source_target_pairs={{0,12},{4,16},{8,20},{12,24},{16,28},{20,0},{24,4},{28,8},{1,13},{... | collective-permute-start | bytes 393224 | tf_op jit(solution)/shard_map/ppermute | solution.py:34
  121.6 19.9 %collective-permute-start.17 = (f16[64,1024]{1,0:T(8,128)(2,1)S(1)}, f16[64,1024]{1,0:T(8,128)(2,1)S(1)}, u32[]{:S(2)}, u32[]{:S(2)}) collective-permute-start(f16[64,1024]{1,0:T(8,128)(2,1)S(1)} %get-tuple-element.27), channel_id=1, source_target_pairs={{0,8},{4,12},{8,16},{12,20},{16,24},{20,28},{24,0},{28,4},{1,9},{5... | collective-permute-start | bytes 393224 | tf_op jit(solution)/shard_map/ppermute | solution.py:34
where the time goes:
time: 148 us; the launch traced here: 147 us
  starting transfers between devices  53.9 us (36%)
  waiting for transfers between devices  31.1 us (21%)
  blocking collectives  25.2 us (17%)
  matrix products  12.1 us (8%)
  Pallas kernels  11.1 us (8%)
  other arithmetic  5.34 us (4%)
  local copies, waits for them, and re-layouts  4.6 us (3%)
  between operations  3.83 us (3%)
    ppermute x14, waiting for transfers between devices, shifted(): lax.ppermute(array, 'z', [(k, (k + by) % LINE_Z) for k in range(LINE_Z)])  30.8 us
    ppermute x14, starting transfers between devices, shifted(): lax.ppermute(array, 'z', [(k, (k + by) % LINE_Z) for k in range(LINE_Z)])  26.7 us
    all_to_all x2, blocking collectives, exchanged(): return lax.all_to_all(message, axis, 0, 0, tiled=True)  25.2 us
    all_to_all x3, starting transfers between devices, exchanged(): return lax.all_to_all(message, axis, 0, 0, tiled=True)  16.9 us
    pallas_call x3, Pallas kernels, call(): pl.pallas_call(kernel, out_shape=[jax.ShapeDtypeStruct(*o) for o in outs]...  11.1 us
    ppermute x9, starting transfers between devices, swapped(): return lax.ppermute(array, 'c', [(0, 1), (1, 0)])  10.3 us
    dot_general x1, matrix products, parts(): lax.dot_general(weights[:HALF], text_all, NN, preferred_element_type=f32)  4.32 us
    dot_general x1, matrix products, parts(): lax.dot_general(weights[HALF:], text_all, NN, preferred_element_type=f32)  3.98 us
  transfers between devices with their start and end apart: 26, of which 7 were waited for; matrix products, arithmetic and copies ran while one was open for 10% of the time, Pallas kernels for 0%

commit v1 on v0

v1 whole, which is shorter than its diff:
```python
import jax
import jax.numpy as jnp
from jax import lax
from jax.experimental import pallas as pl
from jax.experimental.pallas import tpu as pltpu
from jax.sharding import Mesh
from jax.sharding import PartitionSpec as P


BATCH = ("xh", "y", "z", "c")
BATCH_REP = ("xh", "y", "z", "c", "xl")
PLANE = ("xh", "y", "xl")
LINE = ("z", "c")
WIRE_SCALE = 8.0
VMEM_LIMIT = 24 * 1024 * 1024
ROWS = 64
LINE_Z = 8
PLANE_N = 16
HALF = LINE_Z * ROWS
BLOCK = 2 * HALF
LANES = 128
TILES = BLOCK // LANES
STEP = 256
FAR_FIRST = (4, 3, 5, 2, 6, 1, 7)
NT = (((1,), (1,)), ((), ()))
NN = (((1,), (0,)), ((), ()))
TN = (((0,), (0,)), ((), ()))


def exchanged(message, axis):
    return lax.all_to_all(message, axis, 0, 0, tiled=True)


def shifted(array, by):
    return lax.ppermute(array, "z", [(k, (k + by) % LINE_Z) for k in range(LINE_Z)])


def swapped(array):
    return lax.ppermute(array, "c", [(0, 1), (1, 0)])


def as_column(line):
    return jnp.transpose(jnp.broadcast_to(line, (LANES, LANES)))[:ROWS, :1]


def as_line(column):
    return jnp.transpose(jnp.broadcast_to(column, (LANES, LANES)))[:1]


def placed(slots, pos):
    lanes = lax.broadcasted_iota(jnp.int32, (LINE_Z, LANES), 1)
    both = jnp.where(lanes < ROWS, slots[:LINE_Z], pltpu.roll(slots[LINE_Z:], ROWS, 1))
    return pltpu.roll(jnp.where(pos[0] == 0, both, pltpu.roll(both, ROWS, 1)), pos[1], 0)


def relative(both, pos):
    both = pltpu.roll(both, lax.rem(LINE_Z - pos[1], LINE_Z), 0)
    turned = pltpu.roll(both, ROWS, 1)
    same = pos[0] == 0
    return jnp.concatenate(
        [jnp.where(same, both, turned), jnp.where(same, turned, both)], axis=0
    )


def scores_kernel(pos, scale, own_text, text, *refs):
    blocks, rest = refs[: 2 * LINE_Z], refs[2 * LINE_Z :]
    scores, image, row_message, col_part, diag_part = rest
    for k in range(2 * LINE_Z):
        image[k * ROWS : (k + 1) * ROWS, :] = blocks[k][...]
    scale_value = scale[0]
    diag = scale_value * jnp.sum(
        blocks[0][...].astype(jnp.float32) * own_text[...].astype(jnp.float32)
    )
    text_rows = text[...]
    col_max = col_sum = None
    lines = []
    for i in range(BLOCK // STEP):
        span = slice(i * STEP, (i + 1) * STEP)
        part = scale_value * lax.dot_general(
            image[span, :], text_rows, NT, preferred_element_type=jnp.float32
        )
        scores[span, :] = part
        biggest = jnp.max(part, axis=1, keepdims=True)
        lse = biggest + jnp.log(jnp.sum(jnp.exp(part - biggest), axis=1, keepdims=True))
        for t in range(STEP // LANES):
            line = as_line(lse[t * LANES : (t + 1) * LANES])
            lines += [line, pltpu.roll(line, ROWS, 1)]
        top = jnp.max(part, axis=0, keepdims=True)
        new = top if i == 0 else jnp.maximum(col_max, top)
        total = jnp.sum(jnp.exp(part - new), axis=0, keepdims=True)
        col_sum = total if i == 0 else col_sum * jnp.exp(col_max - new) + total
        col_max = new
    message = placed(jnp.concatenate(lines, axis=0), pos)
    diag_part[...] = jnp.full(diag_part.shape, diag)
    row_message[...] = jnp.broadcast_to(message[None], row_message.shape)
    col_lse = col_max + jnp.log(col_sum)
    for i in range(TILES):
        col_part[i : i + 1, :] = col_lse[:, i * LANES : (i + 1) * LANES]


def joined(stats):
    biggest = jnp.max(stats, axis=0)
    return biggest + jnp.log(jnp.sum(jnp.exp(stats - biggest[None]), axis=0))


def rows_kernel(pos, heard, col_part, diag_part, row_lse, col_message):
    lse = joined(heard[...])
    row_lse[...] = relative(lse, pos)
    extra = lax.broadcasted_iota(jnp.int32, (TILES, LANES), 0)
    extra = jnp.where(extra == 0, jnp.sum(lse), diag_part[...])
    message = jnp.concatenate([col_part[...], extra], axis=0)
    col_message[...] = jnp.broadcast_to(message[None], col_message.shape)


def weights_kernel(pos, scores, row_lse, heard, text, weights, near, other, loss_part, rows_loss):
    step = pl.program_id(0)
    col_lse = joined(heard[:, :TILES, :])
    extra = jnp.sum(heard[:, TILES:, :], axis=0)
    rows_loss[...] = jnp.broadcast_to(extra[:1], rows_loss.shape)
    loss_part[...] = jnp.sum(col_lse) - 2.0 * jnp.broadcast_to(extra[1:2], loss_part.shape)
    col_line = jnp.concatenate([col_lse[i : i + 1] for i in range(TILES)], axis=1)
    row_ids = lax.broadcasted_iota(jnp.int32, (ROWS, BLOCK), 0)
    column_ids = lax.broadcasted_iota(jnp.int32, (ROWS, BLOCK), 1) - pos[2] * ROWS
    own_pairs = jnp.where(row_ids == column_ids, jnp.where(step == 0, 2.0, 0.0), 0.0)
    for k in range(STEP // ROWS):
        span = slice(k * ROWS, (k + 1) * ROWS)
        part = scores[span, :]
        column = as_column(row_lse[pl.ds(step * (STEP // ROWS) + k, 1), :])
        both = jnp.exp(part - column) + jnp.exp(part - col_line)
        if k == 0:
            both = both - own_pairs
        weights[span, :] = both.astype(jnp.bfloat16)
    out = WIRE_SCALE * lax.dot_general(
        weights[...], text[...], NN, preferred_element_type=jnp.float32
    )

    @pl.when(step < HALF // STEP)
    def _():
        near[...] = out

    @pl.when(step >= HALF // STEP)
    def _():
        other[...] = out


def weights_call(pos, scores, row_lse, heard, text):
    half_steps = HALF // STEP
    whole = lambda *shape: pl.BlockSpec(shape, lambda i: (0,) * len(shape))
    rows = pl.BlockSpec((STEP, BLOCK), lambda i: (i, 0))
    width = text.shape[1]
    f32 = jnp.float32
    return pl.pallas_call(
        weights_kernel,
        grid=(BLOCK // STEP,),
        in_specs=[
            pl.BlockSpec(memory_space=pltpu.SMEM),
            rows,
            whole(*row_lse.shape),
            whole(*heard.shape),
            whole(*text.shape),
        ],
        out_specs=[
            rows,
            pl.BlockSpec((STEP, width), lambda i: (jnp.minimum(i, half_steps - 1), 0)),
            pl.BlockSpec((STEP, width), lambda i: (jnp.maximum(i - half_steps, 0), 0)),
            whole(TILES, LANES),
            whole(TILES, LANES),
        ],
        out_shape=[
            jax.ShapeDtypeStruct((BLOCK, BLOCK), jnp.bfloat16),
            jax.ShapeDtypeStruct((HALF, width), f32),
            jax.ShapeDtypeStruct((HALF, width), f32),
            jax.ShapeDtypeStruct((TILES, LANES), f32),
            jax.ShapeDtypeStruct((TILES, LANES), f32),
        ],
        compiler_params=pltpu.CompilerParams(vmem_limit_bytes=VMEM_LIMIT),
        name="weights_kernel",
    )(pos, scores, row_lse, heard, text)


def call(kernel, outs, spec, *args, out_spec=None, scratch=()):
    kinds = {
        "v": pl.BlockSpec(memory_space=pltpu.VMEM),
        "s": pl.BlockSpec(memory_space=pltpu.SMEM),
        "a": pl.BlockSpec(memory_space=pl.ANY),
    }
    return pl.pallas_call(
        kernel,
        out_shape=[jax.ShapeDtypeStruct(*o) for o in outs],
        in_specs=[kinds[k] for k in spec],
        out_specs=[kinds[k] for k in out_spec or "v" * len(outs)],
        scratch_shapes=scratch,
        compiler_params=pltpu.CompilerParams(vmem_limit_bytes=VMEM_LIMIT),
    )(*args)


def parts(image_embed, text_embed, logit_scale):
    f32, f16, bf16 = jnp.float32, jnp.float16, jnp.bfloat16
    width = text_embed.shape[1]
    pos = jnp.stack(
        [lax.axis_index("c"), lax.axis_index("z"), lax.axis_index(PLANE)]
    ).astype(jnp.int32)
    own_image = lax.dynamic_slice_in_dim(image_embed, lax.axis_index("xl") * ROWS, ROWS, 0)

    text_all = exchanged(
        jnp.broadcast_to(text_embed[None], (PLANE_N, ROWS, width)), PLANE
    ).reshape(BLOCK, width)
    near = [own_image] + [None] * (LINE_Z - 1)
    for k, by in ((1, -1), (7, 1), (2, -2), (6, 2), (4, 4)):
        near[k] = shifted(own_image, by)
    near[3] = shifted(near[1], -2)
    near[5] = shifted(near[7], 2)
    far = []
    for block in near:
        far.append(swapped(block))

    message = (PLANE_N, 2 * TILES, LANES)
    scores, image_all, row_message, col_part, diag_part = call(
        scores_kernel,
        [
            ((BLOCK, BLOCK), f32),
            ((BLOCK, width), bf16),
            ((PLANE_N, TILES, LANES), f32),
            ((TILES, LANES), f32),
            ((TILES, LANES), f32),
        ],
        "ss" + "v" * (2 + 2 * LINE_Z),
        pos, logit_scale, text_embed, text_all, *near, *far,
    )
    row_lse, col_message = call(
        rows_kernel,
        [((2 * LINE_Z, LANES), f32), (message, f32)],
        "svvv",
        pos, exchanged(row_message, LINE), col_part, diag_part,
    )
    weights, near_part, other_part, loss_sum, rows_loss = weights_call(
        pos, scores, row_lse, exchanged(col_message, PLANE), text_all
    )
    arrived = swapped(other_part)
    for bit in (1, 2, 4):
        loss_sum = loss_sum + lax.ppermute(
            loss_sum, "z", [(k, k ^ bit) for k in range(LINE_Z)]
        )
    loss_sum = loss_sum + swapped(loss_sum)
    mean_loss = ((rows_loss + loss_sum) * (1.0 / (2 * ROWS * 256)))[0, 0]

    text_part = lax.dot_general(weights, image_all, TN, preferred_element_type=f32)
    text_part = (WIRE_SCALE * text_part).astype(f16).reshape(PLANE_N, ROWS, width)
    text_back = exchanged(text_part, PLANE)
    image_part = [
        near_part[k * ROWS : (k + 1) * ROWS] + arrived[k * ROWS : (k + 1) * ROWS]
        for k in range(LINE_Z)
    ]
    image_sum = image_part[0]
    for k in FAR_FIRST:
        image_sum = image_sum + shifted(image_part[k].astype(f16), k).astype(f32)
    text_sum = text_back[0].astype(f32)
    for k in range(1, PLANE_N):
        text_sum = text_sum + text_back[k].astype(f32)
    factor = logit_scale[0] * (0.5 / WIRE_SCALE)
    return (mean_loss, factor * image_sum, factor * text_sum)


def solution(mesh):
    split = Mesh(mesh.devices.reshape(2, 4, LINE_Z, 2, mesh.shape["rep"]), BATCH_REP)
    return jax.shard_map(
        parts,
        mesh=split,
        in_specs=(P(BATCH, None), P(BATCH_REP, None), P()),
        out_specs=(P(), P(BATCH_REP, None), P(BATCH_REP, None)),
        check_vma=False,
    )
```

time: 148 us -> 142 us (0.959)
  the two profiles are of different devices: /device:TPU:33 before, /device:TPU:1 now
where the time goes in v1:
time: 142 us; the launch traced here: 139 us
  starting transfers between devices  55.7 us (39%)
  waiting for transfers between devices  29.3 us (21%)
  blocking collectives  26.3 us (19%)
  Pallas kernels  11.6 us (8%)
  other arithmetic  6.68 us (5%)
  local copies, waits for them, and re-layouts  4.68 us (3%)
  matrix products  3.78 us (3%)
    ppermute x14, starting transfers between devices, shifted(): lax.ppermute(array, 'z', [(k, (k + by) % LINE_Z) for k in range(LINE_Z)])  28.7 us
    all_to_all x2, blocking collectives, exchanged(): return lax.all_to_all(message, axis, 0, 0, tiled=True)  26.3 us
    ppermute x14, waiting for transfers between devices, shifted(): lax.ppermute(array, 'z', [(k, (k + by) % LINE_Z) for k in range(LINE_Z)])  17.9 us
    ppermute x10, starting transfers between devices, swapped(): return lax.ppermute(array, 'c', [(0, 1), (1, 0)])  12.9 us
    all_to_all x2, starting transfers between devices, exchanged(): return lax.all_to_all(message, axis, 0, 0, tiled=True)  12.3 us
    ppermute x3, waiting for transfers between devices, parts(): lax.ppermute(loss_sum, 'z', [(k, k ^ bit) for k in range(LINE_Z)])  10.8 us
    pallas_call x1, Pallas kernels, weights_call(): pl.pallas_call(weights_kernel, grid=(BLOCK // STEP,), in_specs=[pl.BlockS...  6.1 us
    pallas_call x2, Pallas kernels, call(): pl.pallas_call(kernel, out_shape=[jax.ShapeDtypeStruct(*o) for o in outs]...  5.46 us
  transfers between devices with their start and end apart: 29, of which 12 were waited for; matrix products, arithmetic and copies ran while one was open for 6% of the time, Pallas kernels for 0%

profile of v1, /device:TPU:1, one launch (start us, length us, event | category | flops | bytes accessed | tf_op | source)
XLA Modules:
  0.0 139.5 jit_solution(2025864493238224322)
XLA Ops:
  0.6 2.6 %broadcast_in_dim.2 = bf16[16,64,1024]{2,1,0:T(8,128)(2,1)} broadcast(bf16[64,1024]{1,0:T(8,128)(2,1)} %own_text.1), dimensions={1,2} | broadcast | bytes 2228224 | tf_op jit(solution)/shard_map/broadcast_in_dim | solution.py:206
  3.2 7.7 %all-to-all-start = ((bf16[16,64,1024]{2,1,0:T(8,128)(2,1)}), bf16[16,64,1024]{2,1,0:T(8,128)(2,1)S(1)}, u32[]{:S(2)}, u32[]{:S(2)}) async-start(bf16[16,64,1024]{2,1,0:T(8,128)(2,1)} %broadcast_in_dim.2), calls=%async_computation | async-start | bytes 4194304 | tf_op jit(solution)/shard_map/all_to_all | solution.py:31
  12.0 3.0 %collective-permute-start.6 = (bf16[64,1024]{1,0:T(8,128)(2,1)S(1)}, bf16[64,1024]{1,0:T(8,128)(2,1)S(1)}, u32[]{:S(2)}, u32[]{:S(2)}) collective-permute-start(bf16[64,1024]{1,0:T(8,128)(2,1)S(1)} %constant_dynamic-slice_fusion.refs_0_), channel_id=1, source_target_pairs={{0,8},{4,12},{8,16},{12,20},{16,24},{20,28},{24,0},{28,4},{1,9},{5... | collective-permute-start | bytes 393224 | tf_op jit(solution)/shard_map/ppermute | solution.py:35
  15.0 1.6 %collective-permute-start.4 = (bf16[64,1024]{1,0:T(8,128)(2,1)S(1)}, bf16[64,1024]{1,0:T(8,128)(2,1)S(1)}, u32[]{:S(2)}, u32[]{:S(2)}) collective-permute-start(bf16[64,1024]{1,0:T(8,128)(2,1)S(1)} %constant_dynamic-slice_fusion.refs_0_), channel_id=1, source_target_pairs={{0,4},{4,8},{8,12},{12,16},{16,20},{20,24},{24,28},{28,0},{1,5},{5... | collective-permute-start | bytes 393224 | tf_op jit(solution)/shard_map/ppermute | solution.py:35
  16.6 4.2 %collective-permute-start.3 = (bf16[64,1024]{1,0:T(8,128)(2,1)S(1)}, bf16[64,1024]{1,0:T(8,128)(2,1)S(1)}, u32[]{:S(2)}, u32[]{:S(2)}) collective-permute-start(bf16[64,1024]{1,0:T(8,128)(2,1)S(1)} %constant_dynamic-slice_fusion.refs_0_), channel_id=1, source_target_pairs={{0,16},{4,20},{8,24},{12,28},{16,0},{20,4},{24,8},{28,12},{1,17},{... | collective-permute-start | bytes 393224 | tf_op jit(solution)/shard_map/ppermute | solution.py:35
  20.8 1.9 %collective-permute-start = (bf16[64,1024]{1,0:T(8,128)(2,1)S(1)}, bf16[64,1024]{1,0:T(8,128)(2,1)S(1)}, u32[]{:S(2)}, u32[]{:S(2)}) collective-permute-start(bf16[64,1024]{1,0:T(8,128)(2,1)S(1)} %constant_dynamic-slice_fusion.refs_0_), channel_id=1, source_target_pairs={{0,28},{4,0},{8,4},{12,8},{16,12},{20,16},{24,20},{28,24},{1,29},{... | collective-permute-start | bytes 393224 | tf_op jit(solution)/shard_map/ppermute | solution.py:35
  24.0 1.5 %collective-permute-start.13 = (bf16[64,1024]{1,0:T(8,128)(2,1)S(1)}, bf16[64,1024]{1,0:T(8,128)(2,1)S(1)}, u32[]{:S(2)}, u32[]{:S(2)}) collective-permute-start(bf16[64,1024]{1,0:T(8,128)(2,1)S(1)} %collective-permute-done.6.refs_6_), channel_id=1, source_target_pairs={{0,2},{2,0},{1,3},{3,1},{4,6},{6,4},{5,7},{7,5},{8,10},{10,8},{9,1... | collective-permute-start | bytes 393224 | tf_op jit(solution)/shard_map/ppermute | solution.py:39
  25.5 1.5 %collective-permute-done.4.refs_7_ = bf16[64,1024]{1,0:T(8,128)(2,1)S(1)} collective-permute-done((bf16[64,1024]{1,0:T(8,128)(2,1)S(1)}, bf16[64,1024]{1,0:T(8,128)(2,1)S(1)}, u32[]{:S(2)}, u32[]{:S(2)}) %collective-permute-start.4) | collective-permute-done | bytes 131104 | tf_op jit(solution)/shard_map/ppermute | solution.py:35
  27.7 4.4 %collective-permute-done.3.refs_4_ = bf16[64,1024]{1,0:T(8,128)(2,1)S(1)} collective-permute-done((bf16[64,1024]{1,0:T(8,128)(2,1)S(1)}, bf16[64,1024]{1,0:T(8,128)(2,1)S(1)}, u32[]{:S(2)}, u32[]{:S(2)}) %collective-permute-start.3) | collective-permute-done | bytes 131104 | tf_op jit(solution)/shard_map/ppermute | solution.py:35
  32.1 4.6 %collective-permute-start.5 = (bf16[64,1024]{1,0:T(8,128)(2,1)S(1)}, bf16[64,1024]{1,0:T(8,128)(2,1)}, u32[]{:S(2)}, u32[]{:S(2)}) collective-permute-start(bf16[64,1024]{1,0:T(8,128)(2,1)S(1)} %collective-permute-done.4.refs_7_), channel_id=1, source_target_pairs={{0,8},{4,12},{8,16},{12,20},{16,24},{20,28},{24,0},{28,4},{1,9},{5... | collective-permute-start | bytes 393224 | tf_op jit(solution)/shard_map/ppermute | solution.py:35
  42.0 1.9 %collective-permute-start.10 = (bf16[64,1024]{1,0:T(8,128)(2,1)}, bf16[64,1024]{1,0:T(8,128)(2,1)}, u32[]{:S(2)}, u32[]{:S(2)}) collective-permute-start(bf16[64,1024]{1,0:T(8,128)(2,1)} %collective-permute-done.2.refs_3_), channel_id=1, source_target_pairs={{0,2},{2,0},{1,3},{3,1},{4,6},{6,4},{5,7},{7,5},{8,10},{10,8},{9,1... | collective-permute-start | bytes 393224 | tf_op jit(solution)/shard_map/ppermute | solution.py:39
  46.2 4.8 %shard_map.58 = (f32[1024,1024]{1,0:T(8,128)S(1)}, bf16[1024,1024]{1,0:T(8,128)(2,1)S(1)}, f32[16,8,128]{2,1,0:T(8,128)S(1)}, f32[8,128]{1,0:T(8,128)S(1)}, f32[8,128]{1,0:T(8,128)S(1)}) custom-call(s32[3]{0:T(128)S(1)} %pad_add_fusion.pos, f32[1]{0:T(128)S(6)} %copy.6.scale, bf16[64,1024]{1,0:T(8,128)(2,1)S(1)} %copy-done.3, ...), custom_call_target="tpu_custom_call" | custom-call | tf_op jit(solution)/shard_map/pallas_call | solution.py:187
  50.9 13.5 %all_to_all.20.heard = f32[16,8,128]{2,1,0:T(8,128)S(1)} all-to-all(f32[16,8,128]{2,1,0:T(8,128)S(1)} %get-tuple-element.16), channel_id=1, replica_groups=mesh['xh'=2,'y'=4,'z'=8,'c'=2,'xl'=2] {'z','c'}, dimensions={0} | all-to-all | bytes 131072 | tf_op jit(solution)/shard_map/all_to_all | solution.py:31
  65.2 12.8 %all_to_all.21.heard = f32[16,16,128]{2,1,0:T(8,128)S(1)} all-to-all(f32[16,16,128]{2,1,0:T(8,128)S(1)} %get-tuple-element.20), channel_id=1, replica_groups=mesh['xh'=2,'y'=4,'z'=8,'c'=2,'xl'=2] {'xh','y','xl'}, dimensions={0} | all-to-all | bytes 262144 | tf_op jit(solution)/shard_map/all_to_all | solution.py:31
  78.0 6.1 %weights_kernel.1 = (bf16[1024,1024]{1,0:T(8,128)(2,1)S(1)}, f32[512,1024]{1,0:T(8,128)S(1)}, f32[512,1024]{1,0:T(8,128)}, f32[8,128]{1,0:T(8,128)S(1)}, f32[8,128]{1,0:T(8,128)S(1)}) custom-call(s32[3]{0:T(128)S(1)} %pad_add_fusion.pos, f32[1024,1024]{1,0:T(8,128)S(1)} %get-tuple-element.15.scores, f32[16,128]{1,0:T(8,128)S(1)} %get-tuple-element.19.row_lse, ...), custom_call_target="tpu_custom_call" | custom-call | tf_op jit(solution)/shard_map/weights_kernel/pallas_call | solution.py:152
  84.1 1.5 %collective-permute-start.19 = (f32[512,1024]{1,0:T(8,128)}, f32[512,1024]{1,0:T(8,128)}, u32[]{:S(2)}, u32[]{:S(2)}) collective-permute-start(f32[512,1024]{1,0:T(8,128)} %get-tuple-element.24), channel_id=1, source_target_pairs={{0,2},{2,0},{1,3},{3,1},{4,6},{6,4},{5,7},{7,5},{8,10},{10,8},{9,1... | collective-permute-start | bytes 6291464 | tf_op jit(solution)/shard_map/ppermute | solution.py:39
  85.6 3.8 %multiply_convert_fusion = f16[1024,1024]{1,0:T(8,128)(2,1)} fusion(bf16[1024,1024]{1,0:T(8,128)(2,1)S(1)} %get-tuple-element.25, bf16[1024,1024]{1,0:T(8,128)(2,1)S(1)} %get-tuple-element.26), kind=kOutput, calls=%fused_computation | convolution fusion | flops 2149580800 | bytes 6291456 | tf_op jit(solution)/shard_map/dot_general | solution.py:247
  89.4 4.6 %all-to-all-start.3 = ((f16[16,64,1024]{2,1,0:T(8,128)(2,1)}), f16[16,64,1024]{2,1,0:T(8,128)(2,1)}, u32[]{:S(2)}, u32[]{:S(2)}) async-start(f16[16,64,1024]{2,1,0:T(8,128)(2,1)} %bitcast.18), calls=%async_computation.3 | async-start | bytes 4194304 | tf_op jit(solution)/shard_map/all_to_all | solution.py:31
  94.4 2.1 %collective-permute-done.15 = f32[8,128]{1,0:T(8,128)S(1)} collective-permute-done((f32[8,128]{1,0:T(8,128)S(1)}, f32[8,128]{1,0:T(8,128)S(1)}, u32[]{:S(2)}, u32[]{:S(2)}) %collective-permute-start.15) | collective-permute-done | bytes 4128 | tf_op jit(solution)/shard_map/ppermute | solution.py:241
  97.0 3.2 %collective-permute-done.16 = f32[8,128]{1,0:T(8,128)S(1)} collective-permute-done((f32[8,128]{1,0:T(8,128)S(1)}, f32[8,128]{1,0:T(8,128)S(1)}, u32[]{:S(2)}, u32[]{:S(2)}) %collective-permute-start.16) | collective-permute-done | bytes 4128 | tf_op jit(solution)/shard_map/ppermute | solution.py:241
  101.1 5.5 %collective-permute-done.17 = f32[8,128]{1,0:T(8,128)S(1)} collective-permute-done((f32[8,128]{1,0:T(8,128)S(1)}, f32[8,128]{1,0:T(8,128)S(1)}, u32[]{:S(2)}, u32[]{:S(2)}) %collective-permute-start.17) | collective-permute-done | bytes 4128 | tf_op jit(solution)/shard_map/ppermute | solution.py:241
  106.6 3.1 %collective-permute-start.18 = (f32[8,128]{1,0:T(8,128)S(1)}, f32[8,128]{1,0:T(8,128)S(1)}, u32[]{:S(2)}, u32[]{:S(2)}) collective-permute-start(f32[8,128]{1,0:T(8,128)S(1)} %add.124), channel_id=1, source_target_pairs={{0,2},{2,0},{1,3},{3,1},{4,6},{6,4},{5,7},{7,5},{8,10},{10,8},{9,1... | collective-permute-start | bytes 12296 | tf_op jit(solution)/shard_map/ppermute | solution.py:39
  109.7 1.9 %fusion.6 = (f16[64,1024]{1,0:T(8,128)(2,1)S(1)}, f16[64,1024]{1,0:T(8,128)(2,1)S(1)}, f16[64,1024]{1,0:T(8,128)(2,1)S(1)}, f16[64,1024]{1,0:T(8,128)(2,1)S(1)},...) fusion(f32[512,1024]{1,0:T(8,128)} %collective-permute-done.19, ...), kind=kLoop, calls=%fused_computation.14 | loop fusion | flops 917504 | bytes 4587520 | tf_op jit(solution)/shard_map/convert_element_type | solution.py:256
  112.5 2.1 %collective-permute-start.26 = (f16[64,1024]{1,0:T(8,128)(2,1)S(1)}, f16[64,1024]{1,0:T(8,128)(2,1)S(1)}, u32[]{:S(2)}, u32[]{:S(2)}) collective-permute-start(f16[64,1024]{1,0:T(8,128)(2,1)S(1)} %get-tuple-element.28), channel_id=1, source_target_pairs={{0,28},{4,0},{8,4},{12,8},{16,12},{20,16},{24,20},{28,24},{1,29},{... | collective-permute-start | bytes 393224 | tf_op jit(solution)/shard_map/ppermute | solution.py:35
  115.2 2.3 %collective-permute-start.24 = (f16[64,1024]{1,0:T(8,128)(2,1)S(1)}, f16[64,1024]{1,0:T(8,128)(2,1)S(1)}, u32[]{:S(2)}, u32[]{:S(2)}) collective-permute-start(f16[64,1024]{1,0:T(8,128)(2,1)S(1)} %get-tuple-element.30), channel_id=1, source_target_pairs={{0,24},{4,28},{8,0},{12,4},{16,8},{20,12},{24,16},{28,20},{1,25},{... | collective-permute-start | bytes 393224 | tf_op jit(solution)/shard_map/ppermute | solution.py:35
  117.6 3.6 %collective-permute-done.20 = f16[64,1024]{1,0:T(8,128)(2,1)S(1)} collective-permute-done((f16[64,1024]{1,0:T(8,128)(2,1)S(1)}, f16[64,1024]{1,0:T(8,128)(2,1)S(1)}, u32[]{:S(2)}, u32[]{:S(2)}) %collective-permute-start.20) | collective-permute-done | bytes 131104 | tf_op jit(solution)/shard_map/ppermute | solution.py:35
  121.1 3.3 %collective-permute-start.22 = (f16[64,1024]{1,0:T(8,128)(2,1)S(1)}, f16[64,1024]{1,0:T(8,128)(2,1)}, u32[]{:S(2)}, u32[]{:S(2)}) collective-permute-start(f16[64,1024]{1,0:T(8,128)(2,1)S(1)} %get-tuple-element.32), channel_id=1, source_target_pairs={{0,20},{4,24},{8,28},{12,0},{16,4},{20,8},{24,12},{28,16},{1,21},{... | collective-permute-start | bytes 393224 | tf_op jit(solution)/shard_map/ppermute | solution.py:35
  124.5 2.8 %collective-permute-start.21 = (f16[64,1024]{1,0:T(8,128)(2,1)S(1)}, f16[64,1024]{1,0:T(8,128)(2,1)}, u32[]{:S(2)}, u32[]{:S(2)}) collective-permute-start(f16[64,1024]{1,0:T(8,128)(2,1)S(1)} %get-tuple-element.33), channel_id=1, source_target_pairs={{0,12},{4,16},{8,20},{12,24},{16,28},{20,0},{24,4},{28,8},{1,13},{... | collective-permute-start | bytes 393224 | tf_op jit(solution)/shard_map/ppermute | solution.py:35
  127.2 2.7 %fusion.15 = f32[64,1024]{1,0:T(8,128)} fusion(f16[16,64,1024]{2,1,0:T(8,128)(2,1)} %all-to-all-done.3, f32[]{:T(128)} %bitcast.5), kind=kLoop, calls=%fused_computation.25 | loop fusion | flops 2097152 | bytes 2359300 | tf_op jit(solution)/shard_map/mul | solution.py:261
  130.0 2.2 %collective-permute-done.24 = f16[64,1024]{1,0:T(8,128)(2,1)S(1)} collective-permute-done((f16[64,1024]{1,0:T(8,128)(2,1)S(1)}, f16[64,1024]{1,0:T(8,128)(2,1)S(1)}, u32[]{:S(2)}, u32[]{:S(2)}) %collective-permute-start.24) | collective-permute-done | bytes 131104 | tf_op jit(solution)/shard_map/ppermute | solution.py:35
  133.5 4.0 %collective-permute-done.21 = f16[64,1024]{1,0:T(8,128)(2,1)} collective-permute-done((f16[64,1024]{1,0:T(8,128)(2,1)S(1)}, f16[64,1024]{1,0:T(8,128)(2,1)}, u32[]{:S(2)}, u32[]{:S(2)}) %collective-permute-start.21) | collective-permute-done | bytes 131104 | tf_op jit(solution)/shard_map/ppermute | solution.py:35
  137.5 2.0 %fusion.14 = f32[64,1024]{1,0:T(8,128)} fusion(f32[512,1024]{1,0:T(8,128)} %collective-permute-done.19, f16[64,1024]{1,0:T(8,128)(2,1)S(1)} %collective-permute-done.26, f16[64,1024]{1,0:T(8,128)(2,1)S(1)} %collective-permute-done.25, f16[64,1024]{1,0:T(8,128)(2,1)S(1)} %collective-permute-done.24, f16[64,1024]{1,0:T(8,128)(2,1)} %collective-permute-done.23, ...), kind=kLoop, calls=%fused_computation.23 | loop fusion | flops 1048576 | bytes 1703940 | tf_op jit(solution)/shard_map/mul | solution.py:261
  (55 shorter events, 15.2 us)
Async XLA Ops:
  0.6 10.3 %copy-start = (bf16[128,1024]{1,0:T(8,128)(2,1)S(1)}, bf16[128,1024]{1,0:T(8,128)(2,1)}, u32[]{:S(2)}) copy-start(bf16[128,1024]{1,0:T(8,128)(2,1)} %param.3) | copy-start | bytes 786436
  3.2 42.0 %copy-start.3 = (bf16[64,1024]{1,0:T(8,128)(2,1)S(1)}, bf16[64,1024]{1,0:T(8,128)(2,1)}, u32[]{:S(2)}) copy-start(bf16[64,1024]{1,0:T(8,128)(2,1)} %own_text.1) | copy-start | bytes 393220
  3.2 42.0 %all-to-all-start = ((bf16[16,64,1024]{2,1,0:T(8,128)(2,1)}), bf16[16,64,1024]{2,1,0:T(8,128)(2,1)S(1)}, u32[]{:S(2)}, u32[]{:S(2)}) async-start(bf16[16,64,1024]{2,1,0:T(8,128)(2,1)} %broadcast_in_dim.2), calls=%async_computation | async-start | bytes 4194304 | tf_op jit(solution)/shard_map/all_to_all | solution.py:31
  11.0 11.8 %collective-permute-start.7 = (bf16[64,1024]{1,0:T(8,128)(2,1)S(1)}, bf16[64,1024]{1,0:T(8,128)(2,1)S(1)}, u32[]{:S(2)}, u32[]{:S(2)}) collective-permute-start(bf16[64,1024]{1,0:T(8,128)(2,1)S(1)} %constant_dynamic-slice_fusion.refs_0_), channel_id=1, source_target_pairs={{0,2},{2,0},{1,3},{3,1},{4,6},{6,4},{5,7},{7,5},{8,10},{10,8},{9,1... | collective-permute-start | bytes 393224 | tf_op jit(solution)/shard_map/ppermute | solution.py:39
  12.0 12.0 %collective-permute-start.6 = (bf16[64,1024]{1,0:T(8,128)(2,1)S(1)}, bf16[64,1024]{1,0:T(8,128)(2,1)S(1)}, u32[]{:S(2)}, u32[]{:S(2)}) collective-permute-start(bf16[64,1024]{1,0:T(8,128)(2,1)S(1)} %constant_dynamic-slice_fusion.refs_0_), channel_id=1, source_target_pairs={{0,8},{4,12},{8,16},{12,20},{16,24},{20,28},{24,0},{28,4},{1,9},{5... | collective-permute-start | bytes 393224 | tf_op jit(solution)/shard_map/ppermute | solution.py:35
  15.0 12.0 %collective-permute-start.4 = (bf16[64,1024]{1,0:T(8,128)(2,1)S(1)}, bf16[64,1024]{1,0:T(8,128)(2,1)S(1)}, u32[]{:S(2)}, u32[]{:S(2)}) collective-permute-start(bf16[64,1024]{1,0:T(8,128)(2,1)S(1)} %constant_dynamic-slice_fusion.refs_0_), channel_id=1, source_target_pairs={{0,4},{4,8},{8,12},{12,16},{16,20},{20,24},{24,28},{28,0},{1,5},{5... | collective-permute-start | bytes 393224 | tf_op jit(solution)/shard_map/ppermute | solution.py:35
  16.6 15.4 %collective-permute-start.3 = (bf16[64,1024]{1,0:T(8,128)(2,1)S(1)}, bf16[64,1024]{1,0:T(8,128)(2,1)S(1)}, u32[]{:S(2)}, u32[]{:S(2)}) collective-permute-start(bf16[64,1024]{1,0:T(8,128)(2,1)S(1)} %constant_dynamic-slice_fusion.refs_0_), channel_id=1, source_target_pairs={{0,16},{4,20},{8,24},{12,28},{16,0},{20,4},{24,8},{28,12},{1,17},{... | collective-permute-start | bytes 393224 | tf_op jit(solution)/shard_map/ppermute | solution.py:35
  20.8 15.8 %collective-permute-start = (bf16[64,1024]{1,0:T(8,128)(2,1)S(1)}, bf16[64,1024]{1,0:T(8,128)(2,1)S(1)}, u32[]{:S(2)}, u32[]{:S(2)}) collective-permute-start(bf16[64,1024]{1,0:T(8,128)(2,1)S(1)} %constant_dynamic-slice_fusion.refs_0_), channel_id=1, source_target_pairs={{0,28},{4,0},{8,4},{12,8},{16,12},{20,16},{24,20},{28,24},{1,29},{... | collective-permute-start | bytes 393224 | tf_op jit(solution)/shard_map/ppermute | solution.py:35
  22.8 14.6 %collective-permute-start.1 = (bf16[64,1024]{1,0:T(8,128)(2,1)S(1)}, bf16[64,1024]{1,0:T(8,128)(2,1)S(1)}, u32[]{:S(2)}, u32[]{:S(2)}) collective-permute-start(bf16[64,1024]{1,0:T(8,128)(2,1)S(1)} %constant_dynamic-slice_fusion.refs_0_), channel_id=1, source_target_pairs={{0,24},{4,28},{8,0},{12,4},{16,8},{20,12},{24,16},{28,20},{1,25},{... | collective-permute-start | bytes 393224 | tf_op jit(solution)/shard_map/ppermute | solution.py:35
  24.0 14.6 %collective-permute-start.13 = (bf16[64,1024]{1,0:T(8,128)(2,1)S(1)}, bf16[64,1024]{1,0:T(8,128)(2,1)S(1)}, u32[]{:S(2)}, u32[]{:S(2)}) collective-permute-start(bf16[64,1024]{1,0:T(8,128)(2,1)S(1)} %collective-permute-done.6.refs_6_), channel_id=1, source_target_pairs={{0,2},{2,0},{1,3},{3,1},{4,6},{6,4},{5,7},{7,5},{8,10},{10,8},{9,1... | collective-permute-start | bytes 393224 | tf_op jit(solution)/shard_map/ppermute | solution.py:39
  27.0 11.6 %collective-permute-start.14 = (bf16[64,1024]{1,0:T(8,128)(2,1)S(1)}, bf16[64,1024]{1,0:T(8,128)(2,1)S(1)}, u32[]{:S(2)}, u32[]{:S(2)}) collective-permute-start(bf16[64,1024]{1,0:T(8,128)(2,1)S(1)} %collective-permute-done.4.refs_7_), channel_id=1, source_target_pairs={{0,2},{2,0},{1,3},{3,1},{4,6},{6,4},{5,7},{7,5},{8,10},{10,8},{9,1... | collective-permute-start | bytes 393224 | tf_op jit(solution)/shard_map/ppermute | solution.py:39
  32.1 8.3 %collective-permute-start.5 = (bf16[64,1024]{1,0:T(8,128)(2,1)S(1)}, bf16[64,1024]{1,0:T(8,128)(2,1)}, u32[]{:S(2)}, u32[]{:S(2)}) collective-permute-start(bf16[64,1024]{1,0:T(8,128)(2,1)S(1)} %collective-permute-done.4.refs_7_), channel_id=1, source_target_pairs={{0,8},{4,12},{8,16},{12,20},{16,24},{20,28},{24,0},{28,4},{1,9},{5... | collective-permute-start | bytes 393224 | tf_op jit(solution)/shard_map/ppermute | solution.py:35
  36.7 5.3 %collective-permute-start.2 = (bf16[64,1024]{1,0:T(8,128)(2,1)S(1)}, bf16[64,1024]{1,0:T(8,128)(2,1)}, u32[]{:S(2)}, u32[]{:S(2)}) collective-permute-start(bf16[64,1024]{1,0:T(8,128)(2,1)S(1)} %collective-permute-done.refs_1_), channel_id=1, source_target_pairs={{0,24},{4,28},{8,0},{12,4},{16,8},{20,12},{24,16},{28,20},{1,25},{... | collective-permute-start | bytes 393224 | tf_op jit(solution)/shard_map/ppermute | solution.py:35
  37.3 7.3 %collective-permute-start.8 = (bf16[64,1024]{1,0:T(8,128)(2,1)S(1)}, bf16[64,1024]{1,0:T(8,128)(2,1)}, u32[]{:S(2)}, u32[]{:S(2)}) collective-permute-start(bf16[64,1024]{1,0:T(8,128)(2,1)S(1)} %collective-permute-done.refs_1_), channel_id=1, source_target_pairs={{0,2},{2,0},{1,3},{3,1},{4,6},{6,4},{5,7},{7,5},{8,10},{10,8},{9,1... | collective-permute-start | bytes 393224 | tf_op jit(solution)/shard_map/ppermute | solution.py:39
  38.5 6.1 %collective-permute-start.11 = (bf16[64,1024]{1,0:T(8,128)(2,1)S(1)}, bf16[64,1024]{1,0:T(8,128)(2,1)}, u32[]{:S(2)}, u32[]{:S(2)}) collective-permute-start(bf16[64,1024]{1,0:T(8,128)(2,1)S(1)} %collective-permute-done.3.refs_4_), channel_id=1, source_target_pairs={{0,2},{2,0},{1,3},{3,1},{4,6},{6,4},{5,7},{7,5},{8,10},{10,8},{9,1... | collective-permute-start | bytes 393224 | tf_op jit(solution)/shard_map/ppermute | solution.py:39
  39.3 5.4 %collective-permute-start.9 = (bf16[64,1024]{1,0:T(8,128)(2,1)S(1)}, bf16[64,1024]{1,0:T(8,128)(2,1)}, u32[]{:S(2)}, u32[]{:S(2)}) collective-permute-start(bf16[64,1024]{1,0:T(8,128)(2,1)S(1)} %collective-permute-done.1.refs_2_), channel_id=1, source_target_pairs={{0,2},{2,0},{1,3},{3,1},{4,6},{6,4},{5,7},{7,5},{8,10},{10,8},{9,1... | collective-permute-start | bytes 393224 | tf_op jit(solution)/shard_map/ppermute | solution.py:39
  40.4 4.2 %collective-permute-start.12 = (bf16[64,1024]{1,0:T(8,128)(2,1)}, bf16[64,1024]{1,0:T(8,128)(2,1)}, u32[]{:S(2)}, u32[]{:S(2)}) collective-permute-start(bf16[64,1024]{1,0:T(8,128)(2,1)} %collective-permute-done.5.refs_5_), channel_id=1, source_target_pairs={{0,2},{2,0},{1,3},{3,1},{4,6},{6,4},{5,7},{7,5},{8,10},{10,8},{9,1... | collective-permute-start | bytes 393224 | tf_op jit(solution)/shard_map/ppermute | solution.py:39
  42.0 3.3 %collective-permute-start.10 = (bf16[64,1024]{1,0:T(8,128)(2,1)}, bf16[64,1024]{1,0:T(8,128)(2,1)}, u32[]{:S(2)}, u32[]{:S(2)}) collective-permute-start(bf16[64,1024]{1,0:T(8,128)(2,1)} %collective-permute-done.2.refs_3_), channel_id=1, source_target_pairs={{0,2},{2,0},{1,3},{3,1},{4,6},{6,4},{5,7},{7,5},{8,10},{10,8},{9,1... | collective-permute-start | bytes 393224 | tf_op jit(solution)/shard_map/ppermute | solution.py:39
  84.1 25.6 %collective-permute-start.19 = (f32[512,1024]{1,0:T(8,128)}, f32[512,1024]{1,0:T(8,128)}, u32[]{:S(2)}, u32[]{:S(2)}) collective-permute-start(f32[512,1024]{1,0:T(8,128)} %get-tuple-element.24), channel_id=1, source_target_pairs={{0,2},{2,0},{1,3},{3,1},{4,6},{6,4},{5,7},{7,5},{8,10},{10,8},{9,1... | collective-permute-start | bytes 6291464 | tf_op jit(solution)/shard_map/ppermute | solution.py:39
  89.4 20.3 %copy-start.2 = (f32[512,1024]{1,0:T(8,128)S(1)}, f32[512,1024]{1,0:T(8,128)}, u32[]{:S(2)}) copy-start(f32[512,1024]{1,0:T(8,128)} %copy-done.1) | copy-start | bytes 6291460
  89.4 37.8 %all-to-all-start.3 = ((f16[16,64,1024]{2,1,0:T(8,128)(2,1)}), f16[16,64,1024]{2,1,0:T(8,128)(2,1)}, u32[]{:S(2)}, u32[]{:S(2)}) async-start(f16[16,64,1024]{2,1,0:T(8,128)(2,1)} %bitcast.18), calls=%async_computation.3 | async-start | bytes 4194304 | tf_op jit(solution)/shard_map/all_to_all | solution.py:31
  94.0 2.5 %collective-permute-start.15 = (f32[8,128]{1,0:T(8,128)S(1)}, f32[8,128]{1,0:T(8,128)S(1)}, u32[]{:S(2)}, u32[]{:S(2)}) collective-permute-start(f32[8,128]{1,0:T(8,128)S(1)} %get-tuple-element.22), channel_id=1, source_target_pairs={{0,4},{4,0},{8,12},{12,8},{16,20},{20,16},{24,28},{28,24},{1,5},{5... | collective-permute-start | bytes 12296 | tf_op jit(solution)/shard_map/ppermute | solution.py:241
  96.5 3.8 %collective-permute-start.16 = (f32[8,128]{1,0:T(8,128)S(1)}, f32[8,128]{1,0:T(8,128)S(1)}, u32[]{:S(2)}, u32[]{:S(2)}) collective-permute-start(f32[8,128]{1,0:T(8,128)S(1)} %add.122), channel_id=1, source_target_pairs={{0,8},{4,12},{8,0},{12,4},{16,24},{20,28},{24,16},{28,20},{1,9},{5... | collective-permute-start | bytes 12296 | tf_op jit(solution)/shard_map/ppermute | solution.py:241
  100.3 6.4 %collective-permute-start.17 = (f32[8,128]{1,0:T(8,128)S(1)}, f32[8,128]{1,0:T(8,128)S(1)}, u32[]{:S(2)}, u32[]{:S(2)}) collective-permute-start(f32[8,128]{1,0:T(8,128)S(1)} %add.123), channel_id=1, source_target_pairs={{0,16},{4,20},{8,24},{12,28},{16,0},{20,4},{24,8},{28,12},{1,17},{... | collective-permute-start | bytes 12296 | tf_op jit(solution)/shard_map/ppermute | solution.py:241
  106.6 8.0 %collective-permute-start.18 = (f32[8,128]{1,0:T(8,128)S(1)}, f32[8,128]{1,0:T(8,128)S(1)}, u32[]{:S(2)}, u32[]{:S(2)}) collective-permute-start(f32[8,128]{1,0:T(8,128)S(1)} %add.124), channel_id=1, source_target_pairs={{0,2},{2,0},{1,3},{3,1},{4,6},{6,4},{5,7},{7,5},{8,10},{10,8},{9,1... | collective-permute-start | bytes 12296 | tf_op jit(solution)/shard_map/ppermute | solution.py:39
  111.6 9.6 %collective-permute-start.20 = (f16[64,1024]{1,0:T(8,128)(2,1)S(1)}, f16[64,1024]{1,0:T(8,128)(2,1)S(1)}, u32[]{:S(2)}, u32[]{:S(2)}) collective-permute-start(f16[64,1024]{1,0:T(8,128)(2,1)S(1)} %get-tuple-element.27), channel_id=1, source_target_pairs={{0,16},{4,20},{8,24},{12,28},{16,0},{20,4},{24,8},{28,12},{1,17},{... | collective-permute-start | bytes 393224 | tf_op jit(solution)/shard_map/ppermute | solution.py:35
  112.5 11.9 %collective-permute-start.26 = (f16[64,1024]{1,0:T(8,128)(2,1)S(1)}, f16[64,1024]{1,0:T(8,128)(2,1)S(1)}, u32[]{:S(2)}, u32[]{:S(2)}) collective-permute-start(f16[64,1024]{1,0:T(8,128)(2,1)S(1)} %get-tuple-element.28), channel_id=1, source_target_pairs={{0,28},{4,0},{8,4},{12,8},{16,12},{20,16},{24,20},{28,24},{1,29},{... | collective-permute-start | bytes 393224 | tf_op jit(solution)/shard_map/ppermute | solution.py:35
  115.2 14.8 %collective-permute-start.25 = (f16[64,1024]{1,0:T(8,128)(2,1)S(1)}, f16[64,1024]{1,0:T(8,128)(2,1)S(1)}, u32[]{:S(2)}, u32[]{:S(2)}) collective-permute-start(f16[64,1024]{1,0:T(8,128)(2,1)S(1)} %get-tuple-element.29), channel_id=1, source_target_pairs={{0,4},{4,8},{8,12},{12,16},{16,20},{20,24},{24,28},{28,0},{1,5},{5... | collective-permute-start | bytes 393224 | tf_op jit(solution)/shard_map/ppermute | solution.py:35
  115.2 16.9 %collective-permute-start.24 = (f16[64,1024]{1,0:T(8,128)(2,1)S(1)}, f16[64,1024]{1,0:T(8,128)(2,1)S(1)}, u32[]{:S(2)}, u32[]{:S(2)}) collective-permute-start(f16[64,1024]{1,0:T(8,128)(2,1)S(1)} %get-tuple-element.30), channel_id=1, source_target_pairs={{0,24},{4,28},{8,0},{12,4},{16,8},{20,12},{24,16},{28,20},{1,25},{... | collective-permute-start | bytes 393224 | tf_op jit(solution)/shard_map/ppermute | solution.py:35
  117.4 14.7 %collective-permute-start.23 = (f16[64,1024]{1,0:T(8,128)(2,1)S(1)}, f16[64,1024]{1,0:T(8,128)(2,1)}, u32[]{:S(2)}, u32[]{:S(2)}) collective-permute-start(f16[64,1024]{1,0:T(8,128)(2,1)S(1)} %get-tuple-element.31), channel_id=1, source_target_pairs={{0,8},{4,12},{8,16},{12,20},{16,24},{20,28},{24,0},{28,4},{1,9},{5... | collective-permute-start | bytes 393224 | tf_op jit(solution)/shard_map/ppermute | solution.py:35
  121.1 12.3 %collective-permute-start.22 = (f16[64,1024]{1,0:T(8,128)(2,1)S(1)}, f16[64,1024]{1,0:T(8,128)(2,1)}, u32[]{:S(2)}, u32[]{:S(2)}) collective-permute-start(f16[64,1024]{1,0:T(8,128)(2,1)S(1)} %get-tuple-element.32), channel_id=1, source_target_pairs={{0,20},{4,24},{8,28},{12,0},{16,4},{20,8},{24,12},{28,16},{1,21},{... | collective-permute-start | bytes 393224 | tf_op jit(solution)/shard_map/ppermute | solution.py:35
  124.5 13.0 %collective-permute-start.21 = (f16[64,1024]{1,0:T(8,128)(2,1)S(1)}, f16[64,1024]{1,0:T(8,128)(2,1)}, u32[]{:S(2)}, u32[]{:S(2)}) collective-permute-start(f16[64,1024]{1,0:T(8,128)(2,1)S(1)} %get-tuple-element.33), channel_id=1, source_target_pairs={{0,12},{4,16},{8,20},{12,24},{16,28},{20,0},{24,4},{28,8},{1,13},{... | collective-permute-start | bytes 393224 | tf_op jit(solution)/shard_map/ppermute | solution.py:35
  (3 other events, 6.9 us)

commit v2 on v1

--- a/solution.py
+++ b/solution.py
@@ -237,28 +237,37 @@
         pos, scores, row_lse, exchanged(col_message, PLANE), text_all
     )
     arrived = swapped(other_part)
+    loss_sum = loss_sum + swapped(loss_sum)
     for bit in (1, 2, 4):
         loss_sum = loss_sum + lax.ppermute(
             loss_sum, "z", [(k, k ^ bit) for k in range(LINE_Z)]
         )
-    loss_sum = loss_sum + swapped(loss_sum)
     mean_loss = ((rows_loss + loss_sum) * (1.0 / (2 * ROWS * 256)))[0, 0]
 
     text_part = lax.dot_general(weights, image_all, TN, preferred_element_type=f32)
     text_part = (WIRE_SCALE * text_part).astype(f16).reshape(PLANE_N, ROWS, width)
     text_back = exchanged(text_part, PLANE)
+    factor = logit_scale[0] * (0.5 / WIRE_SCALE)
     image_part = [
         near_part[k * ROWS : (k + 1) * ROWS] + arrived[k * ROWS : (k + 1) * ROWS]
         for k in range(LINE_Z)
     ]
-    image_sum = image_part[0]
+    leaving = [part.astype(f16) for part in image_part]
+    back = {}
     for k in FAR_FIRST:
-        image_sum = image_sum + shifted(image_part[k].astype(f16), k).astype(f32)
+        back[k] = shifted(leaving[k], k)
     text_sum = text_back[0].astype(f32)
     for k in range(1, PLANE_N):
         text_sum = text_sum + text_back[k].astype(f32)
-    factor = logit_scale[0] * (0.5 / WIRE_SCALE)
-    return (mean_loss, factor * image_sum, factor * text_sum)
+    text_grad = factor * text_sum
+    image_sum = image_part[0]
+    for k in FAR_FIRST[:5]:
+        image_sum = image_sum + back[k].astype(f32)
+    image_sum = lax.optimization_barrier(image_sum)
+    for k in FAR_FIRST[5:]:
+        image_sum = image_sum + back[k].astype(f32)
+    image_grad = factor * image_sum
+    return (mean_loss, image_grad, text_grad)
 
 
 def solution(mesh):

time: 142 us -> 140 us (0.986); the launches traced: 139 us -> 139 us
  starting transfers between devices: 55.7 us -> 51 us
  waiting for transfers between devices: 29.3 us -> 33.9 us
    all_to_all x2, waiting for transfers between devices: 0.01 us -> 7.57 us  [exchanged(): return lax.all_to_all(message, axis, 0, 0, tiled=True)]
    ppermute x14, waiting for transfers between devices: 17.9 us -> 13.7 us  [shifted(): lax.ppermute(array, 'z', [(k, (k + by) % LINE_Z) for k in range(LINE_Z)])]
    ppermute x10, starting transfers between devices: 12.9 us -> 9.93 us  [swapped(): return lax.ppermute(array, 'c', [(0, 1), (1, 0)])]
    ppermute x14, starting transfers between devices: 28.7 us -> 27.1 us  [shifted(): lax.ppermute(array, 'z', [(k, (k + by) % LINE_Z) for k in range(LINE_Z)])]
  transfers between devices with their start and end apart: 29 -> 29, of which waited for: 12 -> 11; matrix products, arithmetic and copies ran while one was open for 6% -> 7% of each run, Pallas kernels for 0% -> 0%
where the time goes in v2:
time: 140 us; the launch traced here: 139 us
  starting transfers between devices  51 us (36%)
  waiting for transfers between devices  33.9 us (24%)
  blocking collectives  26.3 us (19%)
  Pallas kernels  11.6 us (8%)
  other arithmetic  6.68 us (5%)
  local copies, waits for them, and re-layouts  4.68 us (3%)
  matrix products  3.78 us (3%)
  between operations  1.41 us (1%)
    ppermute x14, starting transfers between devices, shifted(): lax.ppermute(array, 'z', [(k, (k + by) % LINE_Z) for k in range(LINE_Z)])  27.1 us
    all_to_all x2, blocking collectives, exchanged(): return lax.all_to_all(message, axis, 0, 0, tiled=True)  26.3 us
    ppermute x14, waiting for transfers between devices, shifted(): lax.ppermute(array, 'z', [(k, (k + by) % LINE_Z) for k in range(LINE_Z)])  13.7 us
    all_to_all x2, starting transfers between devices, exchanged(): return lax.all_to_all(message, axis, 0, 0, tiled=True)  12.3 us
    ppermute x3, waiting for transfers between devices, parts(): lax.ppermute(loss_sum, 'z', [(k, k ^ bit) for k in range(LINE_Z)])  10.8 us
    ppermute x10, starting transfers between devices, swapped(): return lax.ppermute(array, 'c', [(0, 1), (1, 0)])  9.93 us
    all_to_all x2, waiting for transfers between devices, exchanged(): return lax.all_to_all(message, axis, 0, 0, tiled=True)  7.57 us
    pallas_call x1, Pallas kernels, weights_call(): pl.pallas_call(weights_kernel, grid=(BLOCK // STEP,), in_specs=[pl.BlockS...  6.1 us
  transfers between devices with their start and end apart: 29, of which 11 were waited for; matrix products, arithmetic and copies ran while one was open for 7% of the time, Pallas kernels for 0%

profile of v2, /device:TPU:1, one launch (start us, length us, event | category | flops | bytes accessed | tf_op | source)
XLA Modules:
  0.0 139.3 jit_solution(10283301088040582463)
XLA Ops:
  0.6 2.6 %broadcast_in_dim.2 = bf16[16,64,1024]{2,1,0:T(8,128)(2,1)} broadcast(bf16[64,1024]{1,0:T(8,128)(2,1)} %own_text.1), dimensions={1,2} | broadcast | bytes 2228224 | tf_op jit(solution)/shard_map/broadcast_in_dim | solution.py:206
  3.2 7.7 %all-to-all-start = ((bf16[16,64,1024]{2,1,0:T(8,128)(2,1)}), bf16[16,64,1024]{2,1,0:T(8,128)(2,1)S(1)}, u32[]{:S(2)}, u32[]{:S(2)}) async-start(bf16[16,64,1024]{2,1,0:T(8,128)(2,1)} %broadcast_in_dim.2), calls=%async_computation | async-start | bytes 4194304 | tf_op jit(solution)/shard_map/all_to_all | solution.py:31
  12.0 3.0 %collective-permute-start.6 = (bf16[64,1024]{1,0:T(8,128)(2,1)S(1)}, bf16[64,1024]{1,0:T(8,128)(2,1)S(1)}, u32[]{:S(2)}, u32[]{:S(2)}) collective-permute-start(bf16[64,1024]{1,0:T(8,128)(2,1)S(1)} %constant_dynamic-slice_fusion.refs_0_), channel_id=1, source_target_pairs={{0,8},{4,12},{8,16},{12,20},{16,24},{20,28},{24,0},{28,4},{1,9},{5... | collective-permute-start | bytes 393224 | tf_op jit(solution)/shard_map/ppermute | solution.py:35
  15.0 1.6 %collective-permute-start.4 = (bf16[64,1024]{1,0:T(8,128)(2,1)S(1)}, bf16[64,1024]{1,0:T(8,128)(2,1)S(1)}, u32[]{:S(2)}, u32[]{:S(2)}) collective-permute-start(bf16[64,1024]{1,0:T(8,128)(2,1)S(1)} %constant_dynamic-slice_fusion.refs_0_), channel_id=1, source_target_pairs={{0,4},{4,8},{8,12},{12,16},{16,20},{20,24},{24,28},{28,0},{1,5},{5... | collective-permute-start | bytes 393224 | tf_op jit(solution)/shard_map/ppermute | solution.py:35
  16.6 4.2 %collective-permute-start.3 = (bf16[64,1024]{1,0:T(8,128)(2,1)S(1)}, bf16[64,1024]{1,0:T(8,128)(2,1)S(1)}, u32[]{:S(2)}, u32[]{:S(2)}) collective-permute-start(bf16[64,1024]{1,0:T(8,128)(2,1)S(1)} %constant_dynamic-slice_fusion.refs_0_), channel_id=1, source_target_pairs={{0,16},{4,20},{8,24},{12,28},{16,0},{20,4},{24,8},{28,12},{1,17},{... | collective-permute-start | bytes 393224 | tf_op jit(solution)/shard_map/ppermute | solution.py:35
  20.8 1.9 %collective-permute-start = (bf16[64,1024]{1,0:T(8,128)(2,1)S(1)}, bf16[64,1024]{1,0:T(8,128)(2,1)S(1)}, u32[]{:S(2)}, u32[]{:S(2)}) collective-permute-start(bf16[64,1024]{1,0:T(8,128)(2,1)S(1)} %constant_dynamic-slice_fusion.refs_0_), channel_id=1, source_target_pairs={{0,28},{4,0},{8,4},{12,8},{16,12},{20,16},{24,20},{28,24},{1,29},{... | collective-permute-start | bytes 393224 | tf_op jit(solution)/shard_map/ppermute | solution.py:35
  22.8 1.2 collective-permute-start.1
  24.0 1.5 %collective-permute-start.13 = (bf16[64,1024]{1,0:T(8,128)(2,1)S(1)}, bf16[64,1024]{1,0:T(8,128)(2,1)S(1)}, u32[]{:S(2)}, u32[]{:S(2)}) collective-permute-start(bf16[64,1024]{1,0:T(8,128)(2,1)S(1)} %collective-permute-done.6.refs_6_), channel_id=1, source_target_pairs={{0,2},{2,0},{1,3},{3,1},{4,6},{6,4},{5,7},{7,5},{8,10},{10,8},{9,1... | collective-permute-start | bytes 393224 | tf_op jit(solution)/shard_map/ppermute | solution.py:39
  25.5 1.5 %collective-permute-done.4.refs_7_ = bf16[64,1024]{1,0:T(8,128)(2,1)S(1)} collective-permute-done((bf16[64,1024]{1,0:T(8,128)(2,1)S(1)}, bf16[64,1024]{1,0:T(8,128)(2,1)S(1)}, u32[]{:S(2)}, u32[]{:S(2)}) %collective-permute-start.4) | collective-permute-done | bytes 131104 | tf_op jit(solution)/shard_map/ppermute | solution.py:35
  27.7 4.4 %collective-permute-done.3.refs_4_ = bf16[64,1024]{1,0:T(8,128)(2,1)S(1)} collective-permute-done((bf16[64,1024]{1,0:T(8,128)(2,1)S(1)}, bf16[64,1024]{1,0:T(8,128)(2,1)S(1)}, u32[]{:S(2)}, u32[]{:S(2)}) %collective-permute-start.3) | collective-permute-done | bytes 131104 | tf_op jit(solution)/shard_map/ppermute | solution.py:35
  32.1 4.6 %collective-permute-start.5 = (bf16[64,1024]{1,0:T(8,128)(2,1)S(1)}, bf16[64,1024]{1,0:T(8,128)(2,1)}, u32[]{:S(2)}, u32[]{:S(2)}) collective-permute-start(bf16[64,1024]{1,0:T(8,128)(2,1)S(1)} %collective-permute-done.4.refs_7_), channel_id=1, source_target_pairs={{0,8},{4,12},{8,16},{12,20},{16,24},{20,28},{24,0},{28,4},{1,9},{5... | collective-permute-start | bytes 393224 | tf_op jit(solution)/shard_map/ppermute | solution.py:35
  40.4 1.5 %collective-permute-start.12 = (bf16[64,1024]{1,0:T(8,128)(2,1)}, bf16[64,1024]{1,0:T(8,128)(2,1)}, u32[]{:S(2)}, u32[]{:S(2)}) collective-permute-start(bf16[64,1024]{1,0:T(8,128)(2,1)} %collective-permute-done.5.refs_5_), channel_id=1, source_target_pairs={{0,2},{2,0},{1,3},{3,1},{4,6},{6,4},{5,7},{7,5},{8,10},{10,8},{9,1... | collective-permute-start | bytes 393224 | tf_op jit(solution)/shard_map/ppermute | solution.py:39
  42.0 1.9 %collective-permute-start.10 = (bf16[64,1024]{1,0:T(8,128)(2,1)}, bf16[64,1024]{1,0:T(8,128)(2,1)}, u32[]{:S(2)}, u32[]{:S(2)}) collective-permute-start(bf16[64,1024]{1,0:T(8,128)(2,1)} %collective-permute-done.2.refs_3_), channel_id=1, source_target_pairs={{0,2},{2,0},{1,3},{3,1},{4,6},{6,4},{5,7},{7,5},{8,10},{10,8},{9,1... | collective-permute-start | bytes 393224 | tf_op jit(solution)/shard_map/ppermute | solution.py:39
  46.2 4.8 %shard_map.58 = (f32[1024,1024]{1,0:T(8,128)S(1)}, bf16[1024,1024]{1,0:T(8,128)(2,1)S(1)}, f32[16,8,128]{2,1,0:T(8,128)S(1)}, f32[8,128]{1,0:T(8,128)S(1)}, f32[8,128]{1,0:T(8,128)S(1)}) custom-call(s32[3]{0:T(128)S(1)} %pad_add_fusion.pos, f32[1]{0:T(128)S(6)} %copy.6.scale, bf16[64,1024]{1,0:T(8,128)(2,1)S(1)} %copy-done.3, ...), custom_call_target="tpu_custom_call" | custom-call | tf_op jit(solution)/shard_map/pallas_call | solution.py:187
  50.9 13.5 %all_to_all.20.heard = f32[16,8,128]{2,1,0:T(8,128)S(1)} all-to-all(f32[16,8,128]{2,1,0:T(8,128)S(1)} %get-tuple-element.16), channel_id=1, replica_groups=mesh['xh'=2,'y'=4,'z'=8,'c'=2,'xl'=2] {'z','c'}, dimensions={0} | all-to-all | bytes 131072 | tf_op jit(solution)/shard_map/all_to_all | solution.py:31
  65.2 12.8 %all_to_all.21.heard = f32[16,16,128]{2,1,0:T(8,128)S(1)} all-to-all(f32[16,16,128]{2,1,0:T(8,128)S(1)} %get-tuple-element.20), channel_id=1, replica_groups=mesh['xh'=2,'y'=4,'z'=8,'c'=2,'xl'=2] {'xh','y','xl'}, dimensions={0} | all-to-all | bytes 262144 | tf_op jit(solution)/shard_map/all_to_all | solution.py:31
  78.0 6.1 %weights_kernel.1 = (bf16[1024,1024]{1,0:T(8,128)(2,1)S(1)}, f32[512,1024]{1,0:T(8,128)S(1)}, f32[512,1024]{1,0:T(8,128)}, f32[8,128]{1,0:T(8,128)S(1)}, f32[8,128]{1,0:T(8,128)S(1)}) custom-call(s32[3]{0:T(128)S(1)} %pad_add_fusion.pos, f32[1024,1024]{1,0:T(8,128)S(1)} %get-tuple-element.15.scores, f32[16,128]{1,0:T(8,128)S(1)} %get-tuple-element.19.row_lse, ...), custom_call_target="tpu_custom_call" | custom-call | tf_op jit(solution)/shard_map/weights_kernel/pallas_call | solution.py:152
  84.1 1.5 %collective-permute-start.19 = (f32[512,1024]{1,0:T(8,128)}, f32[512,1024]{1,0:T(8,128)}, u32[]{:S(2)}, u32[]{:S(2)}) collective-permute-start(f32[512,1024]{1,0:T(8,128)} %get-tuple-element.24), channel_id=1, source_target_pairs={{0,2},{2,0},{1,3},{3,1},{4,6},{6,4},{5,7},{7,5},{8,10},{10,8},{9,1... | collective-permute-start | bytes 6291464 | tf_op jit(solution)/shard_map/ppermute | solution.py:39
  85.6 3.8 %multiply_convert_fusion = f16[1024,1024]{1,0:T(8,128)(2,1)} fusion(bf16[1024,1024]{1,0:T(8,128)(2,1)S(1)} %get-tuple-element.25, bf16[1024,1024]{1,0:T(8,128)(2,1)S(1)} %get-tuple-element.26), kind=kOutput, calls=%fused_computation | convolution fusion | flops 2149580800 | bytes 6291456 | tf_op jit(solution)/shard_map/dot_general | solution.py:247
  89.4 4.6 %all-to-all-start.3 = ((f16[16,64,1024]{2,1,0:T(8,128)(2,1)}), f16[16,64,1024]{2,1,0:T(8,128)(2,1)}, u32[]{:S(2)}, u32[]{:S(2)}) async-start(f16[16,64,1024]{2,1,0:T(8,128)(2,1)} %bitcast.18), calls=%async_computation.3 | async-start | bytes 4194304 | tf_op jit(solution)/shard_map/all_to_all | solution.py:31
  95.6 2.1 %collective-permute-done.16 = f32[8,128]{1,0:T(8,128)S(1)} collective-permute-done((f32[8,128]{1,0:T(8,128)S(1)}, f32[8,128]{1,0:T(8,128)S(1)}, u32[]{:S(2)}, u32[]{:S(2)}) %collective-permute-start.16) | collective-permute-done | bytes 4128 | tf_op jit(solution)/shard_map/ppermute | solution.py:242
  98.2 3.2 %collective-permute-done.17 = f32[8,128]{1,0:T(8,128)S(1)} collective-permute-done((f32[8,128]{1,0:T(8,128)S(1)}, f32[8,128]{1,0:T(8,128)S(1)}, u32[]{:S(2)}, u32[]{:S(2)}) %collective-permute-start.17) | collective-permute-done | bytes 4128 | tf_op jit(solution)/shard_map/ppermute | solution.py:242
  102.3 5.5 %collective-permute-done.18 = f32[8,128]{1,0:T(8,128)S(1)} collective-permute-done((f32[8,128]{1,0:T(8,128)S(1)}, f32[8,128]{1,0:T(8,128)S(1)}, u32[]{:S(2)}, u32[]{:S(2)}) %collective-permute-start.18) | collective-permute-done | bytes 4128 | tf_op jit(solution)/shard_map/ppermute | solution.py:242
  108.3 1.9 %fusion.1 = (f16[64,1024]{1,0:T(8,128)(2,1)S(1)}, f16[64,1024]{1,0:T(8,128)(2,1)S(1)}, f16[64,1024]{1,0:T(8,128)(2,1)S(1)}, f16[64,1024]{1,0:T(8,128)(2,1)S(1)},...) fusion(f32[512,1024]{1,0:T(8,128)} %collective-permute-done.19, ...), kind=kLoop, calls=%fused_computation.4 | loop fusion | flops 917504 | bytes 4587520 | tf_op jit(solution)/shard_map/convert_element_type | solution.py:255
  110.8 1.8 %collective-permute-start.23 = (f16[64,1024]{1,0:T(8,128)(2,1)S(1)}, f16[64,1024]{1,0:T(8,128)(2,1)S(1)}, u32[]{:S(2)}, u32[]{:S(2)}) collective-permute-start(f16[64,1024]{1,0:T(8,128)(2,1)S(1)} %get-tuple-element.30), channel_id=1, source_target_pairs={{0,8},{4,12},{8,16},{12,20},{16,24},{20,28},{24,0},{28,4},{1,9},{5... | collective-permute-start | bytes 393224 | tf_op jit(solution)/shard_map/ppermute | solution.py:35
  113.6 2.4 %collective-permute-start.21 = (f16[64,1024]{1,0:T(8,128)(2,1)S(1)}, f16[64,1024]{1,0:T(8,128)(2,1)}, u32[]{:S(2)}, u32[]{:S(2)}) collective-permute-start(f16[64,1024]{1,0:T(8,128)(2,1)S(1)} %get-tuple-element.32), channel_id=1, source_target_pairs={{0,12},{4,16},{8,20},{12,24},{16,28},{20,0},{24,4},{28,8},{1,13},{... | collective-permute-start | bytes 393224 | tf_op jit(solution)/shard_map/ppermute | solution.py:35
  115.9 1.4 %collective-permute-start.20 = (f16[64,1024]{1,0:T(8,128)(2,1)S(1)}, f16[64,1024]{1,0:T(8,128)(2,1)}, u32[]{:S(2)}, u32[]{:S(2)}) collective-permute-start(f16[64,1024]{1,0:T(8,128)(2,1)S(1)} %get-tuple-element.33), channel_id=1, source_target_pairs={{0,16},{4,20},{8,24},{12,28},{16,0},{20,4},{24,8},{28,12},{1,17},{... | collective-permute-start | bytes 393224 | tf_op jit(solution)/shard_map/ppermute | solution.py:35
  117.4 7.6 %all-to-all-done.3 = f16[16,64,1024]{2,1,0:T(8,128)(2,1)} async-done(((f16[16,64,1024]{2,1,0:T(8,128)(2,1)}), f16[16,64,1024]{2,1,0:T(8,128)(2,1)}, u32[]{:S(2)}, u32[]{:S(2)}) %all-to-all-start.3) | async-done | bytes 2097184 | tf_op jit(solution)/shard_map/all_to_all | solution.py:31
  124.9 2.7 %fusion.12 = f32[64,1024]{1,0:T(8,128)} fusion(f16[16,64,1024]{2,1,0:T(8,128)(2,1)} %all-to-all-done.3, f32[]{:T(128)} %bitcast.5), kind=kLoop, calls=%fused_computation.22 | loop fusion | flops 2097152 | bytes 2359300 | tf_op jit(solution)/shard_map/mul | solution.py:262
  128.1 2.3 %collective-permute-start.26 = (f16[64,1024]{1,0:T(8,128)(2,1)S(1)}, f16[64,1024]{1,0:T(8,128)(2,1)S(1)}, u32[]{:S(2)}, u32[]{:S(2)}) collective-permute-start(f16[64,1024]{1,0:T(8,128)(2,1)S(1)} %get-tuple-element.28), channel_id=1, source_target_pairs={{0,28},{4,0},{8,4},{12,8},{16,12},{20,16},{24,20},{28,24},{1,29},{... | collective-permute-start | bytes 393224 | tf_op jit(solution)/shard_map/ppermute | solution.py:35
  130.4 1.2 fusion.11
  131.7 6.9 %collective-permute-done.25 = f16[64,1024]{1,0:T(8,128)(2,1)S(1)} collective-permute-done((f16[64,1024]{1,0:T(8,128)(2,1)S(1)}, f16[64,1024]{1,0:T(8,128)(2,1)S(1)}, u32[]{:S(2)}, u32[]{:S(2)}) %collective-permute-start.25) | collective-permute-done | bytes 131104 | tf_op jit(solution)/shard_map/ppermute | solution.py:35
  (56 shorter events, 14.1 us)
Async XLA Ops:
  0.6 10.3 %copy-start = (bf16[128,1024]{1,0:T(8,128)(2,1)S(1)}, bf16[128,1024]{1,0:T(8,128)(2,1)}, u32[]{:S(2)}) copy-start(bf16[128,1024]{1,0:T(8,128)(2,1)} %param.3) | copy-start | bytes 786436
  3.2 42.0 %copy-start.3 = (bf16[64,1024]{1,0:T(8,128)(2,1)S(1)}, bf16[64,1024]{1,0:T(8,128)(2,1)}, u32[]{:S(2)}) copy-start(bf16[64,1024]{1,0:T(8,128)(2,1)} %own_text.1) | copy-start | bytes 393220
  3.2 42.0 %all-to-all-start = ((bf16[16,64,1024]{2,1,0:T(8,128)(2,1)}), bf16[16,64,1024]{2,1,0:T(8,128)(2,1)S(1)}, u32[]{:S(2)}, u32[]{:S(2)}) async-start(bf16[16,64,1024]{2,1,0:T(8,128)(2,1)} %broadcast_in_dim.2), calls=%async_computation | async-start | bytes 4194304 | tf_op jit(solution)/shard_map/all_to_all | solution.py:31
  11.0 11.8 %collective-permute-start.7 = (bf16[64,1024]{1,0:T(8,128)(2,1)S(1)}, bf16[64,1024]{1,0:T(8,128)(2,1)S(1)}, u32[]{:S(2)}, u32[]{:S(2)}) collective-permute-start(bf16[64,1024]{1,0:T(8,128)(2,1)S(1)} %constant_dynamic-slice_fusion.refs_0_), channel_id=1, source_target_pairs={{0,2},{2,0},{1,3},{3,1},{4,6},{6,4},{5,7},{7,5},{8,10},{10,8},{9,1... | collective-permute-start | bytes 393224 | tf_op jit(solution)/shard_map/ppermute | solution.py:39
  12.0 12.0 %collective-permute-start.6 = (bf16[64,1024]{1,0:T(8,128)(2,1)S(1)}, bf16[64,1024]{1,0:T(8,128)(2,1)S(1)}, u32[]{:S(2)}, u32[]{:S(2)}) collective-permute-start(bf16[64,1024]{1,0:T(8,128)(2,1)S(1)} %constant_dynamic-slice_fusion.refs_0_), channel_id=1, source_target_pairs={{0,8},{4,12},{8,16},{12,20},{16,24},{20,28},{24,0},{28,4},{1,9},{5... | collective-permute-start | bytes 393224 | tf_op jit(solution)/shard_map/ppermute | solution.py:35
  15.0 12.0 %collective-permute-start.4 = (bf16[64,1024]{1,0:T(8,128)(2,1)S(1)}, bf16[64,1024]{1,0:T(8,128)(2,1)S(1)}, u32[]{:S(2)}, u32[]{:S(2)}) collective-permute-start(bf16[64,1024]{1,0:T(8,128)(2,1)S(1)} %constant_dynamic-slice_fusion.refs_0_), channel_id=1, source_target_pairs={{0,4},{4,8},{8,12},{12,16},{16,20},{20,24},{24,28},{28,0},{1,5},{5... | collective-permute-start | bytes 393224 | tf_op jit(solution)/shard_map/ppermute | solution.py:35
  16.6 15.4 %collective-permute-start.3 = (bf16[64,1024]{1,0:T(8,128)(2,1)S(1)}, bf16[64,1024]{1,0:T(8,128)(2,1)S(1)}, u32[]{:S(2)}, u32[]{:S(2)}) collective-permute-start(bf16[64,1024]{1,0:T(8,128)(2,1)S(1)} %constant_dynamic-slice_fusion.refs_0_), channel_id=1, source_target_pairs={{0,16},{4,20},{8,24},{12,28},{16,0},{20,4},{24,8},{28,12},{1,17},{... | collective-permute-start | bytes 393224 | tf_op jit(solution)/shard_map/ppermute | solution.py:35
  20.8 15.8 %collective-permute-start = (bf16[64,1024]{1,0:T(8,128)(2,1)S(1)}, bf16[64,1024]{1,0:T(8,128)(2,1)S(1)}, u32[]{:S(2)}, u32[]{:S(2)}) collective-permute-start(bf16[64,1024]{1,0:T(8,128)(2,1)S(1)} %constant_dynamic-slice_fusion.refs_0_), channel_id=1, source_target_pairs={{0,28},{4,0},{8,4},{12,8},{16,12},{20,16},{24,20},{28,24},{1,29},{... | collective-permute-start | bytes 393224 | tf_op jit(solution)/shard_map/ppermute | solution.py:35
  22.8 14.6 %collective-permute-start.1 = (bf16[64,1024]{1,0:T(8,128)(2,1)S(1)}, bf16[64,1024]{1,0:T(8,128)(2,1)S(1)}, u32[]{:S(2)}, u32[]{:S(2)}) collective-permute-start(bf16[64,1024]{1,0:T(8,128)(2,1)S(1)} %constant_dynamic-slice_fusion.refs_0_), channel_id=1, source_target_pairs={{0,24},{4,28},{8,0},{12,4},{16,8},{20,12},{24,16},{28,20},{1,25},{... | collective-permute-start | bytes 393224 | tf_op jit(solution)/shard_map/ppermute | solution.py:35
  24.0 14.6 %collective-permute-start.13 = (bf16[64,1024]{1,0:T(8,128)(2,1)S(1)}, bf16[64,1024]{1,0:T(8,128)(2,1)S(1)}, u32[]{:S(2)}, u32[]{:S(2)}) collective-permute-start(bf16[64,1024]{1,0:T(8,128)(2,1)S(1)} %collective-permute-done.6.refs_6_), channel_id=1, source_target_pairs={{0,2},{2,0},{1,3},{3,1},{4,6},{6,4},{5,7},{7,5},{8,10},{10,8},{9,1... | collective-permute-start | bytes 393224 | tf_op jit(solution)/shard_map/ppermute | solution.py:39
  27.0 11.6 %collective-permute-start.14 = (bf16[64,1024]{1,0:T(8,128)(2,1)S(1)}, bf16[64,1024]{1,0:T(8,128)(2,1)S(1)}, u32[]{:S(2)}, u32[]{:S(2)}) collective-permute-start(bf16[64,1024]{1,0:T(8,128)(2,1)S(1)} %collective-permute-done.4.refs_7_), channel_id=1, source_target_pairs={{0,2},{2,0},{1,3},{3,1},{4,6},{6,4},{5,7},{7,5},{8,10},{10,8},{9,1... | collective-permute-start | bytes 393224 | tf_op jit(solution)/shard_map/ppermute | solution.py:39
  32.1 8.3 %collective-permute-start.5 = (bf16[64,1024]{1,0:T(8,128)(2,1)S(1)}, bf16[64,1024]{1,0:T(8,128)(2,1)}, u32[]{:S(2)}, u32[]{:S(2)}) collective-permute-start(bf16[64,1024]{1,0:T(8,128)(2,1)S(1)} %collective-permute-done.4.refs_7_), channel_id=1, source_target_pairs={{0,8},{4,12},{8,16},{12,20},{16,24},{20,28},{24,0},{28,4},{1,9},{5... | collective-permute-start | bytes 393224 | tf_op jit(solution)/shard_map/ppermute | solution.py:35
  36.7 5.3 %collective-permute-start.2 = (bf16[64,1024]{1,0:T(8,128)(2,1)S(1)}, bf16[64,1024]{1,0:T(8,128)(2,1)}, u32[]{:S(2)}, u32[]{:S(2)}) collective-permute-start(bf16[64,1024]{1,0:T(8,128)(2,1)S(1)} %collective-permute-done.refs_1_), channel_id=1, source_target_pairs={{0,24},{4,28},{8,0},{12,4},{16,8},{20,12},{24,16},{28,20},{1,25},{... | collective-permute-start | bytes 393224 | tf_op jit(solution)/shard_map/ppermute | solution.py:35
  37.3 7.3 %collective-permute-start.8 = (bf16[64,1024]{1,0:T(8,128)(2,1)S(1)}, bf16[64,1024]{1,0:T(8,128)(2,1)}, u32[]{:S(2)}, u32[]{:S(2)}) collective-permute-start(bf16[64,1024]{1,0:T(8,128)(2,1)S(1)} %collective-permute-done.refs_1_), channel_id=1, source_target_pairs={{0,2},{2,0},{1,3},{3,1},{4,6},{6,4},{5,7},{7,5},{8,10},{10,8},{9,1... | collective-permute-start | bytes 393224 | tf_op jit(solution)/shard_map/ppermute | solution.py:39
  38.5 6.1 %collective-permute-start.11 = (bf16[64,1024]{1,0:T(8,128)(2,1)S(1)}, bf16[64,1024]{1,0:T(8,128)(2,1)}, u32[]{:S(2)}, u32[]{:S(2)}) collective-permute-start(bf16[64,1024]{1,0:T(8,128)(2,1)S(1)} %collective-permute-done.3.refs_4_), channel_id=1, source_target_pairs={{0,2},{2,0},{1,3},{3,1},{4,6},{6,4},{5,7},{7,5},{8,10},{10,8},{9,1... | collective-permute-start | bytes 393224 | tf_op jit(solution)/shard_map/ppermute | solution.py:39
  39.3 5.4 %collective-permute-start.9 = (bf16[64,1024]{1,0:T(8,128)(2,1)S(1)}, bf16[64,1024]{1,0:T(8,128)(2,1)}, u32[]{:S(2)}, u32[]{:S(2)}) collective-permute-start(bf16[64,1024]{1,0:T(8,128)(2,1)S(1)} %collective-permute-done.1.refs_2_), channel_id=1, source_target_pairs={{0,2},{2,0},{1,3},{3,1},{4,6},{6,4},{5,7},{7,5},{8,10},{10,8},{9,1... | collective-permute-start | bytes 393224 | tf_op jit(solution)/shard_map/ppermute | solution.py:39
  40.4 4.2 %collective-permute-start.12 = (bf16[64,1024]{1,0:T(8,128)(2,1)}, bf16[64,1024]{1,0:T(8,128)(2,1)}, u32[]{:S(2)}, u32[]{:S(2)}) collective-permute-start(bf16[64,1024]{1,0:T(8,128)(2,1)} %collective-permute-done.5.refs_5_), channel_id=1, source_target_pairs={{0,2},{2,0},{1,3},{3,1},{4,6},{6,4},{5,7},{7,5},{8,10},{10,8},{9,1... | collective-permute-start | bytes 393224 | tf_op jit(solution)/shard_map/ppermute | solution.py:39
  42.0 3.3 %collective-permute-start.10 = (bf16[64,1024]{1,0:T(8,128)(2,1)}, bf16[64,1024]{1,0:T(8,128)(2,1)}, u32[]{:S(2)}, u32[]{:S(2)}) collective-permute-start(bf16[64,1024]{1,0:T(8,128)(2,1)} %collective-permute-done.2.refs_3_), channel_id=1, source_target_pairs={{0,2},{2,0},{1,3},{3,1},{4,6},{6,4},{5,7},{7,5},{8,10},{10,8},{9,1... | collective-permute-start | bytes 393224 | tf_op jit(solution)/shard_map/ppermute | solution.py:39
  84.1 24.3 %collective-permute-start.19 = (f32[512,1024]{1,0:T(8,128)}, f32[512,1024]{1,0:T(8,128)}, u32[]{:S(2)}, u32[]{:S(2)}) collective-permute-start(f32[512,1024]{1,0:T(8,128)} %get-tuple-element.24), channel_id=1, source_target_pairs={{0,2},{2,0},{1,3},{3,1},{4,6},{6,4},{5,7},{7,5},{8,10},{10,8},{9,1... | collective-permute-start | bytes 6291464 | tf_op jit(solution)/shard_map/ppermute | solution.py:39
  89.4 18.9 %copy-start.2 = (f32[512,1024]{1,0:T(8,128)S(1)}, f32[512,1024]{1,0:T(8,128)}, u32[]{:S(2)}) copy-start(f32[512,1024]{1,0:T(8,128)} %copy-done.1) | copy-start | bytes 6291460
  89.4 35.5 %all-to-all-start.3 = ((f16[16,64,1024]{2,1,0:T(8,128)(2,1)}), f16[16,64,1024]{2,1,0:T(8,128)(2,1)}, u32[]{:S(2)}, u32[]{:S(2)}) async-start(f16[16,64,1024]{2,1,0:T(8,128)(2,1)} %bitcast.18), calls=%async_computation.3 | async-start | bytes 4194304 | tf_op jit(solution)/shard_map/all_to_all | solution.py:31
  94.0 1.3 collective-permute-start.15
  95.2 2.5 %collective-permute-start.16 = (f32[8,128]{1,0:T(8,128)S(1)}, f32[8,128]{1,0:T(8,128)S(1)}, u32[]{:S(2)}, u32[]{:S(2)}) collective-permute-start(f32[8,128]{1,0:T(8,128)S(1)} %add.122), channel_id=1, source_target_pairs={{0,4},{4,0},{8,12},{12,8},{16,20},{20,16},{24,28},{28,24},{1,5},{5... | collective-permute-start | bytes 12296 | tf_op jit(solution)/shard_map/ppermute | solution.py:242
  97.7 3.8 %collective-permute-start.17 = (f32[8,128]{1,0:T(8,128)S(1)}, f32[8,128]{1,0:T(8,128)S(1)}, u32[]{:S(2)}, u32[]{:S(2)}) collective-permute-start(f32[8,128]{1,0:T(8,128)S(1)} %add.123), channel_id=1, source_target_pairs={{0,8},{4,12},{8,0},{12,4},{16,24},{20,28},{24,16},{28,20},{1,9},{5... | collective-permute-start | bytes 12296 | tf_op jit(solution)/shard_map/ppermute | solution.py:242
  101.4 6.4 %collective-permute-start.18 = (f32[8,128]{1,0:T(8,128)S(1)}, f32[8,128]{1,0:T(8,128)S(1)}, u32[]{:S(2)}, u32[]{:S(2)}) collective-permute-start(f32[8,128]{1,0:T(8,128)S(1)} %add.124), channel_id=1, source_target_pairs={{0,16},{4,20},{8,24},{12,28},{16,0},{20,4},{24,8},{28,12},{1,17},{... | collective-permute-start | bytes 12296 | tf_op jit(solution)/shard_map/ppermute | solution.py:242
  110.2 17.4 %collective-permute-start.24 = (f16[64,1024]{1,0:T(8,128)(2,1)S(1)}, f16[64,1024]{1,0:T(8,128)(2,1)S(1)}, u32[]{:S(2)}, u32[]{:S(2)}) collective-permute-start(f16[64,1024]{1,0:T(8,128)(2,1)S(1)} %get-tuple-element.29), channel_id=1, source_target_pairs={{0,24},{4,28},{8,0},{12,4},{16,8},{20,12},{24,16},{28,20},{1,25},{... | collective-permute-start | bytes 393224 | tf_op jit(solution)/shard_map/ppermute | solution.py:35
  110.8 17.3 %collective-permute-start.23 = (f16[64,1024]{1,0:T(8,128)(2,1)S(1)}, f16[64,1024]{1,0:T(8,128)(2,1)S(1)}, u32[]{:S(2)}, u32[]{:S(2)}) collective-permute-start(f16[64,1024]{1,0:T(8,128)(2,1)S(1)} %get-tuple-element.30), channel_id=1, source_target_pairs={{0,8},{4,12},{8,16},{12,20},{16,24},{20,28},{24,0},{28,4},{1,9},{5... | collective-permute-start | bytes 393224 | tf_op jit(solution)/shard_map/ppermute | solution.py:35
  112.7 17.8 %collective-permute-start.22 = (f16[64,1024]{1,0:T(8,128)(2,1)S(1)}, f16[64,1024]{1,0:T(8,128)(2,1)}, u32[]{:S(2)}, u32[]{:S(2)}) collective-permute-start(f16[64,1024]{1,0:T(8,128)(2,1)S(1)} %get-tuple-element.31), channel_id=1, source_target_pairs={{0,20},{4,24},{8,28},{12,0},{16,4},{20,8},{24,12},{28,16},{1,21},{... | collective-permute-start | bytes 393224 | tf_op jit(solution)/shard_map/ppermute | solution.py:35
  113.6 16.9 %collective-permute-start.21 = (f16[64,1024]{1,0:T(8,128)(2,1)S(1)}, f16[64,1024]{1,0:T(8,128)(2,1)}, u32[]{:S(2)}, u32[]{:S(2)}) collective-permute-start(f16[64,1024]{1,0:T(8,128)(2,1)S(1)} %get-tuple-element.32), channel_id=1, source_target_pairs={{0,12},{4,16},{8,20},{12,24},{16,28},{20,0},{24,4},{28,8},{1,13},{... | collective-permute-start | bytes 393224 | tf_op jit(solution)/shard_map/ppermute | solution.py:35
  115.9 14.5 %collective-permute-start.20 = (f16[64,1024]{1,0:T(8,128)(2,1)S(1)}, f16[64,1024]{1,0:T(8,128)(2,1)}, u32[]{:S(2)}, u32[]{:S(2)}) collective-permute-start(f16[64,1024]{1,0:T(8,128)(2,1)S(1)} %get-tuple-element.33), channel_id=1, source_target_pairs={{0,16},{4,20},{8,24},{12,28},{16,0},{20,4},{24,8},{28,12},{1,17},{... | collective-permute-start | bytes 393224 | tf_op jit(solution)/shard_map/ppermute | solution.py:35
  127.6 10.9 %collective-permute-start.25 = (f16[64,1024]{1,0:T(8,128)(2,1)S(1)}, f16[64,1024]{1,0:T(8,128)(2,1)S(1)}, u32[]{:S(2)}, u32[]{:S(2)}) collective-permute-start(f16[64,1024]{1,0:T(8,128)(2,1)S(1)} %get-tuple-element.27), channel_id=1, source_target_pairs={{0,4},{4,8},{8,12},{12,16},{16,20},{20,24},{24,28},{28,0},{1,5},{5... | collective-permute-start | bytes 393224 | tf_op jit(solution)/shard_map/ppermute | solution.py:35
  128.1 10.5 %collective-permute-start.26 = (f16[64,1024]{1,0:T(8,128)(2,1)S(1)}, f16[64,1024]{1,0:T(8,128)(2,1)S(1)}, u32[]{:S(2)}, u32[]{:S(2)}) collective-permute-start(f16[64,1024]{1,0:T(8,128)(2,1)S(1)} %get-tuple-element.28), channel_id=1, source_target_pairs={{0,28},{4,0},{8,4},{12,8},{16,12},{20,16},{24,20},{28,24},{1,29},{... | collective-permute-start | bytes 393224 | tf_op jit(solution)/shard_map/ppermute | solution.py:35
  (3 other events, 6.9 us)

commit v3 on v2

--- a/solution.py
+++ b/solution.py
@@ -33,6 +33,10 @@
 
 def shifted(array, by):
     return lax.ppermute(array, "z", [(k, (k + by) % LINE_Z) for k in range(LINE_Z)])
+
+
+def across(array, bit):
+    return lax.ppermute(array, "z", [(k, k ^ bit) for k in range(LINE_Z)])
 
 
 def swapped(array):
@@ -112,70 +116,41 @@
     col_message[...] = jnp.broadcast_to(message[None], col_message.shape)
 
 
-def weights_kernel(pos, scores, row_lse, heard, text, weights, near, other, loss_part, rows_loss):
-    step = pl.program_id(0)
+def weights_kernel(
+    pos, scores, row_lse, heard, text, weights, near, other_out, loss_part, rows_loss, other, sems
+):
     col_lse = joined(heard[:, :TILES, :])
     extra = jnp.sum(heard[:, TILES:, :], axis=0)
     rows_loss[...] = jnp.broadcast_to(extra[:1], rows_loss.shape)
     loss_part[...] = jnp.sum(col_lse) - 2.0 * jnp.broadcast_to(extra[1:2], loss_part.shape)
     col_line = jnp.concatenate([col_lse[i : i + 1] for i in range(TILES)], axis=1)
-    row_ids = lax.broadcasted_iota(jnp.int32, (ROWS, BLOCK), 0)
-    column_ids = lax.broadcasted_iota(jnp.int32, (ROWS, BLOCK), 1) - pos[2] * ROWS
-    own_pairs = jnp.where(row_ids == column_ids, jnp.where(step == 0, 2.0, 0.0), 0.0)
-    for k in range(STEP // ROWS):
-        span = slice(k * ROWS, (k + 1) * ROWS)
-        part = scores[span, :]
-        column = as_column(row_lse[pl.ds(step * (STEP // ROWS) + k, 1), :])
-        both = jnp.exp(part - column) + jnp.exp(part - col_line)
-        if k == 0:
-            both = both - own_pairs
-        weights[span, :] = both.astype(jnp.bfloat16)
-    out = WIRE_SCALE * lax.dot_general(
-        weights[...], text[...], NN, preferred_element_type=jnp.float32
-    )
-
-    @pl.when(step < HALF // STEP)
-    def _():
-        near[...] = out
-
-    @pl.when(step >= HALF // STEP)
-    def _():
-        other[...] = out
-
-
-def weights_call(pos, scores, row_lse, heard, text):
+    text_rows = text[...]
+    copies = []
     half_steps = HALF // STEP
-    whole = lambda *shape: pl.BlockSpec(shape, lambda i: (0,) * len(shape))
-    rows = pl.BlockSpec((STEP, BLOCK), lambda i: (i, 0))
-    width = text.shape[1]
-    f32 = jnp.float32
-    return pl.pallas_call(
-        weights_kernel,
-        grid=(BLOCK // STEP,),
-        in_specs=[
-            pl.BlockSpec(memory_space=pltpu.SMEM),
-            rows,
-            whole(*row_lse.shape),
-            whole(*heard.shape),
-            whole(*text.shape),
-        ],
-        out_specs=[
-            rows,
-            pl.BlockSpec((STEP, width), lambda i: (jnp.minimum(i, half_steps - 1), 0)),
-            pl.BlockSpec((STEP, width), lambda i: (jnp.maximum(i - half_steps, 0), 0)),
-            whole(TILES, LANES),
-            whole(TILES, LANES),
-        ],
-        out_shape=[
-            jax.ShapeDtypeStruct((BLOCK, BLOCK), jnp.bfloat16),
-            jax.ShapeDtypeStruct((HALF, width), f32),
-            jax.ShapeDtypeStruct((HALF, width), f32),
-            jax.ShapeDtypeStruct((TILES, LANES), f32),
-            jax.ShapeDtypeStruct((TILES, LANES), f32),
-        ],
-        compiler_params=pltpu.CompilerParams(vmem_limit_bytes=VMEM_LIMIT),
-        name="weights_kernel",
-    )(pos, scores, row_lse, heard, text)
+    for step in [*range(half_steps, 2 * half_steps), *range(half_steps)]:
+        blocks = []
+        for k in range(STEP // ROWS * step, STEP // ROWS * (step + 1)):
+            part = scores[k * ROWS : (k + 1) * ROWS, :]
+            both = jnp.exp(part - as_column(row_lse[k : k + 1, :])) + jnp.exp(part - col_line)
+            if k == 0:
+                row_ids = lax.broadcasted_iota(jnp.int32, part.shape, 0)
+                column_ids = lax.broadcasted_iota(jnp.int32, part.shape, 1) - pos[2] * ROWS
+                both = both - 2.0 * (row_ids == column_ids).astype(jnp.float32)
+            blocks.append(both.astype(jnp.bfloat16))
+        rows = jnp.concatenate(blocks, axis=0)
+        weights[step * STEP : (step + 1) * STEP, :] = rows
+        out = WIRE_SCALE * lax.dot_general(rows, text_rows, NN, preferred_element_type=jnp.float32)
+        span = slice(step % half_steps * STEP, (step % half_steps + 1) * STEP)
+        if step < half_steps:
+            near[span, :] = out
+        else:
+            other[span, :] = out
+            copies.append(
+                pltpu.make_async_copy(other.at[span, :], other_out.at[span, :], sems.at[len(copies)])
+            )
+            copies[-1].start()
+    for copy in copies:
+        copy.wait()
 
 
 def call(kernel, outs, spec, *args, out_spec=None, scratch=()):
@@ -233,16 +208,26 @@
         "svvv",
         pos, exchanged(row_message, LINE), col_part, diag_part,
     )
-    weights, near_part, other_part, loss_sum, rows_loss = weights_call(
-        pos, scores, row_lse, exchanged(col_message, PLANE), text_all
+    weights, near_part, other_part, loss_sum, rows_loss = call(
+        weights_kernel,
+        [
+            ((BLOCK, BLOCK), bf16),
+            ((HALF, width), f32),
+            ((HALF, width), f32),
+            ((TILES, LANES), f32),
+            ((TILES, LANES), f32),
+        ],
+        "svvvv",
+        pos, scores, row_lse, exchanged(col_message, PLANE), text_all,
+        out_spec="vvavv",
+        scratch=[pltpu.VMEM((HALF, width), f32), pltpu.SemaphoreType.DMA((HALF // STEP,))],
     )
     arrived = swapped(other_part)
     loss_sum = loss_sum + swapped(loss_sum)
-    for bit in (1, 2, 4):
-        loss_sum = loss_sum + lax.ppermute(
-            loss_sum, "z", [(k, k ^ bit) for k in range(LINE_Z)]
-        )
-    mean_loss = ((rows_loss + loss_sum) * (1.0 / (2 * ROWS * 256)))[0, 0]
+    for bit in (1, 2):
+        loss_sum = loss_sum + across(loss_sum, bit)
+    crossed = across(loss_sum, 4)
+    mean_loss = ((rows_loss + (loss_sum + crossed)) * (1.0 / (2 * ROWS * 256)))[0, 0]
 
     text_part = lax.dot_general(weights, image_all, TN, preferred_element_type=f32)
     text_part = (WIRE_SCALE * text_part).astype(f16).reshape(PLANE_N, ROWS, width)

time: 140 us -> 137 us (0.979)
  Pallas kernels: 11.6 us -> 8.81 us
    pallas_call x1 -> x0, Pallas kernels: 6.1 us -> none  [weights_call(): pl.pallas_call(weights_kernel, grid=(BLOCK // STEP,), in_specs=[pl.BlockS...]
    pallas_call x2 -> x3, Pallas kernels: 5.46 us -> 8.81 us  [call(): pl.pallas_call(kernel, out_shape=[jax.ShapeDtypeStruct(*o) for o in outs]...]
  transfers between devices with their start and end apart: 29 -> 29, of which waited for: 11 -> 12; matrix products, arithmetic and copies ran while one was open for 7% -> 7% of each run, Pallas kernels for 0% -> 0%
where the time goes in v3:
time: 137 us
  starting transfers between devices  51.4 us (38%)
  waiting for transfers between devices  33.9 us (25%)
  blocking collectives  26.3 us (19%)
  Pallas kernels  8.81 us (6%)
  other arithmetic  6.67 us (5%)
  local copies, waits for them, and re-layouts  4.68 us (3%)
  matrix products  3.78 us (3%)
  between operations  1.41 us (1%)
    ppermute x14, starting transfers between devices, shifted(): lax.ppermute(array, 'z', [(k, (k + by) % LINE_Z) for k in range(LINE_Z)])  27.3 us
    all_to_all x2, blocking collectives, exchanged(): return lax.all_to_all(message, axis, 0, 0, tiled=True)  26.3 us
    ppermute x14, waiting for transfers between devices, shifted(): lax.ppermute(array, 'z', [(k, (k + by) % LINE_Z) for k in range(LINE_Z)])  14 us
    all_to_all x2, starting transfers between devices, exchanged(): return lax.all_to_all(message, axis, 0, 0, tiled=True)  12.3 us
    ppermute x3, waiting for transfers between devices, across(): return lax.ppermute(array, 'z', [(k, k ^ bit) for k in range(LINE_Z)])  10.8 us
    ppermute x10, starting transfers between devices, swapped(): return lax.ppermute(array, 'c', [(0, 1), (1, 0)])  10 us
    pallas_call x3, Pallas kernels, call(): pl.pallas_call(kernel, out_shape=[jax.ShapeDtypeStruct(*o) for o in outs]...  8.81 us
    all_to_all x2, waiting for transfers between devices, exchanged(): return lax.all_to_all(message, axis, 0, 0, tiled=True)  7.34 us
  transfers between devices with their start and end apart: 29, of which 12 were waited for; matrix products, arithmetic and copies ran while one was open for 7% of the time, Pallas kernels for 0%

profile of v3, /device:TPU:1, one launch (start us, length us, event | category | flops | bytes accessed | tf_op | source)
XLA Modules:
  0.0 136.9 jit_solution(11909501109801972544)
XLA Ops:
  0.6 2.6 %broadcast_in_dim.2 = bf16[16,64,1024]{2,1,0:T(8,128)(2,1)} broadcast(bf16[64,1024]{1,0:T(8,128)(2,1)} %own_text.1), dimensions={1,2} | broadcast | bytes 2228224 | tf_op jit(solution)/shard_map/broadcast_in_dim | solution.py:181
  3.2 7.7 %all-to-all-start = ((bf16[16,64,1024]{2,1,0:T(8,128)(2,1)}), bf16[16,64,1024]{2,1,0:T(8,128)(2,1)S(1)}, u32[]{:S(2)}, u32[]{:S(2)}) async-start(bf16[16,64,1024]{2,1,0:T(8,128)(2,1)} %broadcast_in_dim.2), calls=%async_computation | async-start | bytes 4194304 | tf_op jit(solution)/shard_map/all_to_all | solution.py:31
  12.0 3.0 %collective-permute-start.6 = (bf16[64,1024]{1,0:T(8,128)(2,1)S(1)}, bf16[64,1024]{1,0:T(8,128)(2,1)S(1)}, u32[]{:S(2)}, u32[]{:S(2)}) collective-permute-start(bf16[64,1024]{1,0:T(8,128)(2,1)S(1)} %constant_dynamic-slice_fusion.refs_0_), channel_id=1, source_target_pairs={{0,8},{4,12},{8,16},{12,20},{16,24},{20,28},{24,0},{28,4},{1,9},{5... | collective-permute-start | bytes 393224 | tf_op jit(solution)/shard_map/ppermute | solution.py:35
  15.0 1.6 %collective-permute-start.4 = (bf16[64,1024]{1,0:T(8,128)(2,1)S(1)}, bf16[64,1024]{1,0:T(8,128)(2,1)S(1)}, u32[]{:S(2)}, u32[]{:S(2)}) collective-permute-start(bf16[64,1024]{1,0:T(8,128)(2,1)S(1)} %constant_dynamic-slice_fusion.refs_0_), channel_id=1, source_target_pairs={{0,4},{4,8},{8,12},{12,16},{16,20},{20,24},{24,28},{28,0},{1,5},{5... | collective-permute-start | bytes 393224 | tf_op jit(solution)/shard_map/ppermute | solution.py:35
  16.6 4.2 %collective-permute-start.3 = (bf16[64,1024]{1,0:T(8,128)(2,1)S(1)}, bf16[64,1024]{1,0:T(8,128)(2,1)S(1)}, u32[]{:S(2)}, u32[]{:S(2)}) collective-permute-start(bf16[64,1024]{1,0:T(8,128)(2,1)S(1)} %constant_dynamic-slice_fusion.refs_0_), channel_id=1, source_target_pairs={{0,16},{4,20},{8,24},{12,28},{16,0},{20,4},{24,8},{28,12},{1,17},{... | collective-permute-start | bytes 393224 | tf_op jit(solution)/shard_map/ppermute | solution.py:35
  20.8 1.9 %collective-permute-start = (bf16[64,1024]{1,0:T(8,128)(2,1)S(1)}, bf16[64,1024]{1,0:T(8,128)(2,1)S(1)}, u32[]{:S(2)}, u32[]{:S(2)}) collective-permute-start(bf16[64,1024]{1,0:T(8,128)(2,1)S(1)} %constant_dynamic-slice_fusion.refs_0_), channel_id=1, source_target_pairs={{0,28},{4,0},{8,4},{12,8},{16,12},{20,16},{24,20},{28,24},{1,29},{... | collective-permute-start | bytes 393224 | tf_op jit(solution)/shard_map/ppermute | solution.py:35
  22.8 1.2 collective-permute-start.1
  24.0 1.5 %collective-permute-start.13 = (bf16[64,1024]{1,0:T(8,128)(2,1)S(1)}, bf16[64,1024]{1,0:T(8,128)(2,1)S(1)}, u32[]{:S(2)}, u32[]{:S(2)}) collective-permute-start(bf16[64,1024]{1,0:T(8,128)(2,1)S(1)} %collective-permute-done.6.refs_6_), channel_id=1, source_target_pairs={{0,2},{2,0},{1,3},{3,1},{4,6},{6,4},{5,7},{7,5},{8,10},{10,8},{9,1... | collective-permute-start | bytes 393224 | tf_op jit(solution)/shard_map/ppermute | solution.py:43
  25.5 1.5 %collective-permute-done.4.refs_7_ = bf16[64,1024]{1,0:T(8,128)(2,1)S(1)} collective-permute-done((bf16[64,1024]{1,0:T(8,128)(2,1)S(1)}, bf16[64,1024]{1,0:T(8,128)(2,1)S(1)}, u32[]{:S(2)}, u32[]{:S(2)}) %collective-permute-start.4) | collective-permute-done | bytes 131104 | tf_op jit(solution)/shard_map/ppermute | solution.py:35
  27.7 4.4 %collective-permute-done.3.refs_4_ = bf16[64,1024]{1,0:T(8,128)(2,1)S(1)} collective-permute-done((bf16[64,1024]{1,0:T(8,128)(2,1)S(1)}, bf16[64,1024]{1,0:T(8,128)(2,1)S(1)}, u32[]{:S(2)}, u32[]{:S(2)}) %collective-permute-start.3) | collective-permute-done | bytes 131104 | tf_op jit(solution)/shard_map/ppermute | solution.py:35
  32.1 4.6 %collective-permute-start.5 = (bf16[64,1024]{1,0:T(8,128)(2,1)S(1)}, bf16[64,1024]{1,0:T(8,128)(2,1)}, u32[]{:S(2)}, u32[]{:S(2)}) collective-permute-start(bf16[64,1024]{1,0:T(8,128)(2,1)S(1)} %collective-permute-done.4.refs_7_), channel_id=1, source_target_pairs={{0,8},{4,12},{8,16},{12,20},{16,24},{20,28},{24,0},{28,4},{1,9},{5... | collective-permute-start | bytes 393224 | tf_op jit(solution)/shard_map/ppermute | solution.py:35
  40.4 1.5 %collective-permute-start.12 = (bf16[64,1024]{1,0:T(8,128)(2,1)}, bf16[64,1024]{1,0:T(8,128)(2,1)}, u32[]{:S(2)}, u32[]{:S(2)}) collective-permute-start(bf16[64,1024]{1,0:T(8,128)(2,1)} %collective-permute-done.5.refs_5_), channel_id=1, source_target_pairs={{0,2},{2,0},{1,3},{3,1},{4,6},{6,4},{5,7},{7,5},{8,10},{10,8},{9,1... | collective-permute-start | bytes 393224 | tf_op jit(solution)/shard_map/ppermute | solution.py:43
  42.0 1.9 %collective-permute-start.10 = (bf16[64,1024]{1,0:T(8,128)(2,1)}, bf16[64,1024]{1,0:T(8,128)(2,1)}, u32[]{:S(2)}, u32[]{:S(2)}) collective-permute-start(bf16[64,1024]{1,0:T(8,128)(2,1)} %collective-permute-done.2.refs_3_), channel_id=1, source_target_pairs={{0,2},{2,0},{1,3},{3,1},{4,6},{6,4},{5,7},{7,5},{8,10},{10,8},{9,1... | collective-permute-start | bytes 393224 | tf_op jit(solution)/shard_map/ppermute | solution.py:43
  46.2 4.8 %shard_map.58 = (f32[1024,1024]{1,0:T(8,128)S(1)}, bf16[1024,1024]{1,0:T(8,128)(2,1)S(1)}, f32[16,8,128]{2,1,0:T(8,128)S(1)}, f32[8,128]{1,0:T(8,128)S(1)}, f32[8,128]{1,0:T(8,128)S(1)}) custom-call(s32[3]{0:T(128)S(1)} %pad_add_fusion.pos, f32[1]{0:T(128)S(6)} %copy.6.scale, bf16[64,1024]{1,0:T(8,128)(2,1)S(1)} %copy-done.3, ...), custom_call_target="tpu_custom_call" | custom-call | tf_op jit(solution)/shard_map/pallas_call | solution.py:162
  50.9 13.5 %all_to_all.20.heard = f32[16,8,128]{2,1,0:T(8,128)S(1)} all-to-all(f32[16,8,128]{2,1,0:T(8,128)S(1)} %get-tuple-element.16), channel_id=1, replica_groups=mesh['xh'=2,'y'=4,'z'=8,'c'=2,'xl'=2] {'z','c'}, dimensions={0} | all-to-all | bytes 131072 | tf_op jit(solution)/shard_map/all_to_all | solution.py:31
  65.2 12.8 %all_to_all.21.heard = f32[16,16,128]{2,1,0:T(8,128)S(1)} all-to-all(f32[16,16,128]{2,1,0:T(8,128)S(1)} %get-tuple-element.20), channel_id=1, replica_groups=mesh['xh'=2,'y'=4,'z'=8,'c'=2,'xl'=2] {'xh','y','xl'}, dimensions={0} | all-to-all | bytes 262144 | tf_op jit(solution)/shard_map/all_to_all | solution.py:31
  78.0 3.3 %shard_map.60 = (bf16[1024,1024]{1,0:T(8,128)(2,1)S(1)}, f32[512,1024]{1,0:T(8,128)S(1)}, f32[512,1024]{1,0:T(8,128)}, f32[8,128]{1,0:T(8,128)S(1)}, f32[8,128]{1,0:T(8,128)S(1)}) custom-call(s32[3]{0:T(128)S(1)} %pad_add_fusion.pos, f32[1024,1024]{1,0:T(8,128)S(1)} %get-tuple-element.15.scores, f32[16,128]{1,0:T(8,128)S(1)} %get-tuple-element.19.row_lse, ...), custom_call_target="tpu_custom_call" | custom-call | tf_op jit(solution)/shard_map/pallas_call | solution.py:162
  81.3 1.6 %collective-permute-start.19 = (f32[512,1024]{1,0:T(8,128)}, f32[512,1024]{1,0:T(8,128)}, u32[]{:S(2)}, u32[]{:S(2)}) collective-permute-start(f32[512,1024]{1,0:T(8,128)} %get-tuple-element.24), channel_id=1, source_target_pairs={{0,2},{2,0},{1,3},{3,1},{4,6},{6,4},{5,7},{7,5},{8,10},{10,8},{9,1... | collective-permute-start | bytes 6291464 | tf_op jit(solution)/shard_map/ppermute | solution.py:43
  83.0 3.8 %multiply_convert_fusion = f16[1024,1024]{1,0:T(8,128)(2,1)} fusion(bf16[1024,1024]{1,0:T(8,128)(2,1)S(1)} %get-tuple-element.25, bf16[1024,1024]{1,0:T(8,128)(2,1)S(1)} %get-tuple-element.26), kind=kOutput, calls=%fused_computation | convolution fusion | flops 2149580800 | bytes 6291456 | tf_op jit(solution)/shard_map/dot_general | solution.py:232
  86.7 4.6 %all-to-all-start.3 = ((f16[16,64,1024]{2,1,0:T(8,128)(2,1)}), f16[16,64,1024]{2,1,0:T(8,128)(2,1)}, u32[]{:S(2)}, u32[]{:S(2)}) async-start(f16[16,64,1024]{2,1,0:T(8,128)(2,1)} %bitcast.18), calls=%async_computation.3 | async-start | bytes 4194304 | tf_op jit(solution)/shard_map/all_to_all | solution.py:31
  92.9 2.1 %collective-permute-done.16 = f32[8,128]{1,0:T(8,128)S(1)} collective-permute-done((f32[8,128]{1,0:T(8,128)S(1)}, f32[8,128]{1,0:T(8,128)S(1)}, u32[]{:S(2)}, u32[]{:S(2)}) %collective-permute-start.16) | collective-permute-done | bytes 4128 | tf_op jit(solution)/shard_map/ppermute | solution.py:39
  95.5 3.2 %collective-permute-done.17 = f32[8,128]{1,0:T(8,128)S(1)} collective-permute-done((f32[8,128]{1,0:T(8,128)S(1)}, f32[8,128]{1,0:T(8,128)S(1)}, u32[]{:S(2)}, u32[]{:S(2)}) %collective-permute-start.17) | collective-permute-done | bytes 4128 | tf_op jit(solution)/shard_map/ppermute | solution.py:39
  99.7 5.5 %collective-permute-done.18 = f32[8,128]{1,0:T(8,128)S(1)} collective-permute-done((f32[8,128]{1,0:T(8,128)S(1)}, f32[8,128]{1,0:T(8,128)S(1)}, u32[]{:S(2)}, u32[]{:S(2)}) %collective-permute-start.18) | collective-permute-done | bytes 4128 | tf_op jit(solution)/shard_map/ppermute | solution.py:39
  105.7 1.9 %fusion.1 = (f16[64,1024]{1,0:T(8,128)(2,1)S(1)}, f16[64,1024]{1,0:T(8,128)(2,1)S(1)}, f16[64,1024]{1,0:T(8,128)(2,1)S(1)}, f16[64,1024]{1,0:T(8,128)(2,1)S(1)},...) fusion(f32[512,1024]{1,0:T(8,128)} %collective-permute-done.19, ...), kind=kLoop, calls=%fused_computation.4 | loop fusion | flops 917504 | bytes 4587520 | tf_op jit(solution)/shard_map/convert_element_type | solution.py:240
  108.4 1.8 %collective-permute-start.23 = (f16[64,1024]{1,0:T(8,128)(2,1)S(1)}, f16[64,1024]{1,0:T(8,128)(2,1)S(1)}, u32[]{:S(2)}, u32[]{:S(2)}) collective-permute-start(f16[64,1024]{1,0:T(8,128)(2,1)S(1)} %get-tuple-element.30), channel_id=1, source_target_pairs={{0,8},{4,12},{8,16},{12,20},{16,24},{20,28},{24,0},{28,4},{1,9},{5... | collective-permute-start | bytes 393224 | tf_op jit(solution)/shard_map/ppermute | solution.py:35
  111.1 2.4 %collective-permute-start.21 = (f16[64,1024]{1,0:T(8,128)(2,1)S(1)}, f16[64,1024]{1,0:T(8,128)(2,1)}, u32[]{:S(2)}, u32[]{:S(2)}) collective-permute-start(f16[64,1024]{1,0:T(8,128)(2,1)S(1)} %get-tuple-element.32), channel_id=1, source_target_pairs={{0,12},{4,16},{8,20},{12,24},{16,28},{20,0},{24,4},{28,8},{1,13},{... | collective-permute-start | bytes 393224 | tf_op jit(solution)/shard_map/ppermute | solution.py:35
  113.5 1.4 %collective-permute-start.20 = (f16[64,1024]{1,0:T(8,128)(2,1)S(1)}, f16[64,1024]{1,0:T(8,128)(2,1)}, u32[]{:S(2)}, u32[]{:S(2)}) collective-permute-start(f16[64,1024]{1,0:T(8,128)(2,1)S(1)} %get-tuple-element.33), channel_id=1, source_target_pairs={{0,16},{4,20},{8,24},{12,28},{16,0},{20,4},{24,8},{28,12},{1,17},{... | collective-permute-start | bytes 393224 | tf_op jit(solution)/shard_map/ppermute | solution.py:35
  114.9 7.3 %all-to-all-done.3 = f16[16,64,1024]{2,1,0:T(8,128)(2,1)} async-done(((f16[16,64,1024]{2,1,0:T(8,128)(2,1)}), f16[16,64,1024]{2,1,0:T(8,128)(2,1)}, u32[]{:S(2)}, u32[]{:S(2)}) %all-to-all-start.3) | async-done | bytes 2097184 | tf_op jit(solution)/shard_map/all_to_all | solution.py:31
  122.3 2.7 %fusion.12 = f32[64,1024]{1,0:T(8,128)} fusion(f16[16,64,1024]{2,1,0:T(8,128)(2,1)} %all-to-all-done.3, f32[]{:T(128)} %bitcast.5), kind=kLoop, calls=%fused_computation.22 | loop fusion | flops 2097152 | bytes 2359300 | tf_op jit(solution)/shard_map/mul | solution.py:247
  125.4 2.3 %collective-permute-start.26 = (f16[64,1024]{1,0:T(8,128)(2,1)S(1)}, f16[64,1024]{1,0:T(8,128)(2,1)S(1)}, u32[]{:S(2)}, u32[]{:S(2)}) collective-permute-start(f16[64,1024]{1,0:T(8,128)(2,1)S(1)} %get-tuple-element.28), channel_id=1, source_target_pairs={{0,28},{4,0},{8,4},{12,8},{16,12},{20,16},{24,20},{28,24},{1,29},{... | collective-permute-start | bytes 393224 | tf_op jit(solution)/shard_map/ppermute | solution.py:35
  127.9 1.2 fusion.11
  129.1 7.0 %collective-permute-done.25 = f16[64,1024]{1,0:T(8,128)(2,1)S(1)} collective-permute-done((f16[64,1024]{1,0:T(8,128)(2,1)S(1)}, f16[64,1024]{1,0:T(8,128)(2,1)S(1)}, u32[]{:S(2)}, u32[]{:S(2)}) %collective-permute-start.25) | collective-permute-done | bytes 131104 | tf_op jit(solution)/shard_map/ppermute | solution.py:35
  (56 shorter events, 14.5 us)
Async XLA Ops:
  0.6 10.3 %copy-start = (bf16[128,1024]{1,0:T(8,128)(2,1)S(1)}, bf16[128,1024]{1,0:T(8,128)(2,1)}, u32[]{:S(2)}) copy-start(bf16[128,1024]{1,0:T(8,128)(2,1)} %param.3) | copy-start | bytes 786436
  3.2 42.0 %copy-start.3 = (bf16[64,1024]{1,0:T(8,128)(2,1)S(1)}, bf16[64,1024]{1,0:T(8,128)(2,1)}, u32[]{:S(2)}) copy-start(bf16[64,1024]{1,0:T(8,128)(2,1)} %own_text.1) | copy-start | bytes 393220
  3.2 42.0 %all-to-all-start = ((bf16[16,64,1024]{2,1,0:T(8,128)(2,1)}), bf16[16,64,1024]{2,1,0:T(8,128)(2,1)S(1)}, u32[]{:S(2)}, u32[]{:S(2)}) async-start(bf16[16,64,1024]{2,1,0:T(8,128)(2,1)} %broadcast_in_dim.2), calls=%async_computation | async-start | bytes 4194304 | tf_op jit(solution)/shard_map/all_to_all | solution.py:31
  11.0 11.8 %collective-permute-start.7 = (bf16[64,1024]{1,0:T(8,128)(2,1)S(1)}, bf16[64,1024]{1,0:T(8,128)(2,1)S(1)}, u32[]{:S(2)}, u32[]{:S(2)}) collective-permute-start(bf16[64,1024]{1,0:T(8,128)(2,1)S(1)} %constant_dynamic-slice_fusion.refs_0_), channel_id=1, source_target_pairs={{0,2},{2,0},{1,3},{3,1},{4,6},{6,4},{5,7},{7,5},{8,10},{10,8},{9,1... | collective-permute-start | bytes 393224 | tf_op jit(solution)/shard_map/ppermute | solution.py:43
  12.0 12.0 %collective-permute-start.6 = (bf16[64,1024]{1,0:T(8,128)(2,1)S(1)}, bf16[64,1024]{1,0:T(8,128)(2,1)S(1)}, u32[]{:S(2)}, u32[]{:S(2)}) collective-permute-start(bf16[64,1024]{1,0:T(8,128)(2,1)S(1)} %constant_dynamic-slice_fusion.refs_0_), channel_id=1, source_target_pairs={{0,8},{4,12},{8,16},{12,20},{16,24},{20,28},{24,0},{28,4},{1,9},{5... | collective-permute-start | bytes 393224 | tf_op jit(solution)/shard_map/ppermute | solution.py:35
  15.0 12.0 %collective-permute-start.4 = (bf16[64,1024]{1,0:T(8,128)(2,1)S(1)}, bf16[64,1024]{1,0:T(8,128)(2,1)S(1)}, u32[]{:S(2)}, u32[]{:S(2)}) collective-permute-start(bf16[64,1024]{1,0:T(8,128)(2,1)S(1)} %constant_dynamic-slice_fusion.refs_0_), channel_id=1, source_target_pairs={{0,4},{4,8},{8,12},{12,16},{16,20},{20,24},{24,28},{28,0},{1,5},{5... | collective-permute-start | bytes 393224 | tf_op jit(solution)/shard_map/ppermute | solution.py:35
  16.6 15.4 %collective-permute-start.3 = (bf16[64,1024]{1,0:T(8,128)(2,1)S(1)}, bf16[64,1024]{1,0:T(8,128)(2,1)S(1)}, u32[]{:S(2)}, u32[]{:S(2)}) collective-permute-start(bf16[64,1024]{1,0:T(8,128)(2,1)S(1)} %constant_dynamic-slice_fusion.refs_0_), channel_id=1, source_target_pairs={{0,16},{4,20},{8,24},{12,28},{16,0},{20,4},{24,8},{28,12},{1,17},{... | collective-permute-start | bytes 393224 | tf_op jit(solution)/shard_map/ppermute | solution.py:35
  20.8 15.8 %collective-permute-start = (bf16[64,1024]{1,0:T(8,128)(2,1)S(1)}, bf16[64,1024]{1,0:T(8,128)(2,1)S(1)}, u32[]{:S(2)}, u32[]{:S(2)}) collective-permute-start(bf16[64,1024]{1,0:T(8,128)(2,1)S(1)} %constant_dynamic-slice_fusion.refs_0_), channel_id=1, source_target_pairs={{0,28},{4,0},{8,4},{12,8},{16,12},{20,16},{24,20},{28,24},{1,29},{... | collective-permute-start | bytes 393224 | tf_op jit(solution)/shard_map/ppermute | solution.py:35
  22.8 14.6 %collective-permute-start.1 = (bf16[64,1024]{1,0:T(8,128)(2,1)S(1)}, bf16[64,1024]{1,0:T(8,128)(2,1)S(1)}, u32[]{:S(2)}, u32[]{:S(2)}) collective-permute-start(bf16[64,1024]{1,0:T(8,128)(2,1)S(1)} %constant_dynamic-slice_fusion.refs_0_), channel_id=1, source_target_pairs={{0,24},{4,28},{8,0},{12,4},{16,8},{20,12},{24,16},{28,20},{1,25},{... | collective-permute-start | bytes 393224 | tf_op jit(solution)/shard_map/ppermute | solution.py:35
  24.0 14.6 %collective-permute-start.13 = (bf16[64,1024]{1,0:T(8,128)(2,1)S(1)}, bf16[64,1024]{1,0:T(8,128)(2,1)S(1)}, u32[]{:S(2)}, u32[]{:S(2)}) collective-permute-start(bf16[64,1024]{1,0:T(8,128)(2,1)S(1)} %collective-permute-done.6.refs_6_), channel_id=1, source_target_pairs={{0,2},{2,0},{1,3},{3,1},{4,6},{6,4},{5,7},{7,5},{8,10},{10,8},{9,1... | collective-permute-start | bytes 393224 | tf_op jit(solution)/shard_map/ppermute | solution.py:43
  27.0 11.6 %collective-permute-start.14 = (bf16[64,1024]{1,0:T(8,128)(2,1)S(1)}, bf16[64,1024]{1,0:T(8,128)(2,1)S(1)}, u32[]{:S(2)}, u32[]{:S(2)}) collective-permute-start(bf16[64,1024]{1,0:T(8,128)(2,1)S(1)} %collective-permute-done.4.refs_7_), channel_id=1, source_target_pairs={{0,2},{2,0},{1,3},{3,1},{4,6},{6,4},{5,7},{7,5},{8,10},{10,8},{9,1... | collective-permute-start | bytes 393224 | tf_op jit(solution)/shard_map/ppermute | solution.py:43
  32.1 8.3 %collective-permute-start.5 = (bf16[64,1024]{1,0:T(8,128)(2,1)S(1)}, bf16[64,1024]{1,0:T(8,128)(2,1)}, u32[]{:S(2)}, u32[]{:S(2)}) collective-permute-start(bf16[64,1024]{1,0:T(8,128)(2,1)S(1)} %collective-permute-done.4.refs_7_), channel_id=1, source_target_pairs={{0,8},{4,12},{8,16},{12,20},{16,24},{20,28},{24,0},{28,4},{1,9},{5... | collective-permute-start | bytes 393224 | tf_op jit(solution)/shard_map/ppermute | solution.py:35
  36.7 5.3 %collective-permute-start.2 = (bf16[64,1024]{1,0:T(8,128)(2,1)S(1)}, bf16[64,1024]{1,0:T(8,128)(2,1)}, u32[]{:S(2)}, u32[]{:S(2)}) collective-permute-start(bf16[64,1024]{1,0:T(8,128)(2,1)S(1)} %collective-permute-done.refs_1_), channel_id=1, source_target_pairs={{0,24},{4,28},{8,0},{12,4},{16,8},{20,12},{24,16},{28,20},{1,25},{... | collective-permute-start | bytes 393224 | tf_op jit(solution)/shard_map/ppermute | solution.py:35
  37.3 7.3 %collective-permute-start.8 = (bf16[64,1024]{1,0:T(8,128)(2,1)S(1)}, bf16[64,1024]{1,0:T(8,128)(2,1)}, u32[]{:S(2)}, u32[]{:S(2)}) collective-permute-start(bf16[64,1024]{1,0:T(8,128)(2,1)S(1)} %collective-permute-done.refs_1_), channel_id=1, source_target_pairs={{0,2},{2,0},{1,3},{3,1},{4,6},{6,4},{5,7},{7,5},{8,10},{10,8},{9,1... | collective-permute-start | bytes 393224 | tf_op jit(solution)/shard_map/ppermute | solution.py:43
  38.5 6.1 %collective-permute-start.11 = (bf16[64,1024]{1,0:T(8,128)(2,1)S(1)}, bf16[64,1024]{1,0:T(8,128)(2,1)}, u32[]{:S(2)}, u32[]{:S(2)}) collective-permute-start(bf16[64,1024]{1,0:T(8,128)(2,1)S(1)} %collective-permute-done.3.refs_4_), channel_id=1, source_target_pairs={{0,2},{2,0},{1,3},{3,1},{4,6},{6,4},{5,7},{7,5},{8,10},{10,8},{9,1... | collective-permute-start | bytes 393224 | tf_op jit(solution)/shard_map/ppermute | solution.py:43
  39.3 5.4 %collective-permute-start.9 = (bf16[64,1024]{1,0:T(8,128)(2,1)S(1)}, bf16[64,1024]{1,0:T(8,128)(2,1)}, u32[]{:S(2)}, u32[]{:S(2)}) collective-permute-start(bf16[64,1024]{1,0:T(8,128)(2,1)S(1)} %collective-permute-done.1.refs_2_), channel_id=1, source_target_pairs={{0,2},{2,0},{1,3},{3,1},{4,6},{6,4},{5,7},{7,5},{8,10},{10,8},{9,1... | collective-permute-start | bytes 393224 | tf_op jit(solution)/shard_map/ppermute | solution.py:43
  40.4 4.2 %collective-permute-start.12 = (bf16[64,1024]{1,0:T(8,128)(2,1)}, bf16[64,1024]{1,0:T(8,128)(2,1)}, u32[]{:S(2)}, u32[]{:S(2)}) collective-permute-start(bf16[64,1024]{1,0:T(8,128)(2,1)} %collective-permute-done.5.refs_5_), channel_id=1, source_target_pairs={{0,2},{2,0},{1,3},{3,1},{4,6},{6,4},{5,7},{7,5},{8,10},{10,8},{9,1... | collective-permute-start | bytes 393224 | tf_op jit(solution)/shard_map/ppermute | solution.py:43
  42.0 3.3 %collective-permute-start.10 = (bf16[64,1024]{1,0:T(8,128)(2,1)}, bf16[64,1024]{1,0:T(8,128)(2,1)}, u32[]{:S(2)}, u32[]{:S(2)}) collective-permute-start(bf16[64,1024]{1,0:T(8,128)(2,1)} %collective-permute-done.2.refs_3_), channel_id=1, source_target_pairs={{0,2},{2,0},{1,3},{3,1},{4,6},{6,4},{5,7},{7,5},{8,10},{10,8},{9,1... | collective-permute-start | bytes 393224 | tf_op jit(solution)/shard_map/ppermute | solution.py:43
  81.3 24.4 %collective-permute-start.19 = (f32[512,1024]{1,0:T(8,128)}, f32[512,1024]{1,0:T(8,128)}, u32[]{:S(2)}, u32[]{:S(2)}) collective-permute-start(f32[512,1024]{1,0:T(8,128)} %get-tuple-element.24), channel_id=1, source_target_pairs={{0,2},{2,0},{1,3},{3,1},{4,6},{6,4},{5,7},{7,5},{8,10},{10,8},{9,1... | collective-permute-start | bytes 6291464 | tf_op jit(solution)/shard_map/ppermute | solution.py:43
  86.7 18.9 %copy-start.2 = (f32[512,1024]{1,0:T(8,128)S(1)}, f32[512,1024]{1,0:T(8,128)}, u32[]{:S(2)}) copy-start(f32[512,1024]{1,0:T(8,128)} %copy-done.1) | copy-start | bytes 6291460
  86.7 35.5 %all-to-all-start.3 = ((f16[16,64,1024]{2,1,0:T(8,128)(2,1)}), f16[16,64,1024]{2,1,0:T(8,128)(2,1)}, u32[]{:S(2)}, u32[]{:S(2)}) async-start(f16[16,64,1024]{2,1,0:T(8,128)(2,1)} %bitcast.18), calls=%async_computation.3 | async-start | bytes 4194304 | tf_op jit(solution)/shard_map/all_to_all | solution.py:31
  91.3 1.3 collective-permute-start.15
  92.6 2.5 %collective-permute-start.16 = (f32[8,128]{1,0:T(8,128)S(1)}, f32[8,128]{1,0:T(8,128)S(1)}, u32[]{:S(2)}, u32[]{:S(2)}) collective-permute-start(f32[8,128]{1,0:T(8,128)S(1)} %add.122), channel_id=1, source_target_pairs={{0,4},{4,0},{8,12},{12,8},{16,20},{20,16},{24,28},{28,24},{1,5},{5... | collective-permute-start | bytes 12296 | tf_op jit(solution)/shard_map/ppermute | solution.py:39
  95.0 3.8 %collective-permute-start.17 = (f32[8,128]{1,0:T(8,128)S(1)}, f32[8,128]{1,0:T(8,128)S(1)}, u32[]{:S(2)}, u32[]{:S(2)}) collective-permute-start(f32[8,128]{1,0:T(8,128)S(1)} %add.123), channel_id=1, source_target_pairs={{0,8},{4,12},{8,0},{12,4},{16,24},{20,28},{24,16},{28,20},{1,9},{5... | collective-permute-start | bytes 12296 | tf_op jit(solution)/shard_map/ppermute | solution.py:39
  98.8 6.4 %collective-permute-start.18 = (f32[8,128]{1,0:T(8,128)S(1)}, f32[8,128]{1,0:T(8,128)S(1)}, u32[]{:S(2)}, u32[]{:S(2)}) collective-permute-start(f32[8,128]{1,0:T(8,128)S(1)} %add.124), channel_id=1, source_target_pairs={{0,16},{4,20},{8,24},{12,28},{16,0},{20,4},{24,8},{28,12},{1,17},{... | collective-permute-start | bytes 12296 | tf_op jit(solution)/shard_map/ppermute | solution.py:39
  107.6 17.4 %collective-permute-start.24 = (f16[64,1024]{1,0:T(8,128)(2,1)S(1)}, f16[64,1024]{1,0:T(8,128)(2,1)S(1)}, u32[]{:S(2)}, u32[]{:S(2)}) collective-permute-start(f16[64,1024]{1,0:T(8,128)(2,1)S(1)} %get-tuple-element.29), channel_id=1, source_target_pairs={{0,24},{4,28},{8,0},{12,4},{16,8},{20,12},{24,16},{28,20},{1,25},{... | collective-permute-start | bytes 393224 | tf_op jit(solution)/shard_map/ppermute | solution.py:35
  108.4 17.0 %collective-permute-start.23 = (f16[64,1024]{1,0:T(8,128)(2,1)S(1)}, f16[64,1024]{1,0:T(8,128)(2,1)S(1)}, u32[]{:S(2)}, u32[]{:S(2)}) collective-permute-start(f16[64,1024]{1,0:T(8,128)(2,1)S(1)} %get-tuple-element.30), channel_id=1, source_target_pairs={{0,8},{4,12},{8,16},{12,20},{16,24},{20,28},{24,0},{28,4},{1,9},{5... | collective-permute-start | bytes 393224 | tf_op jit(solution)/shard_map/ppermute | solution.py:35
  110.2 17.5 %collective-permute-start.22 = (f16[64,1024]{1,0:T(8,128)(2,1)S(1)}, f16[64,1024]{1,0:T(8,128)(2,1)}, u32[]{:S(2)}, u32[]{:S(2)}) collective-permute-start(f16[64,1024]{1,0:T(8,128)(2,1)S(1)} %get-tuple-element.31), channel_id=1, source_target_pairs={{0,20},{4,24},{8,28},{12,0},{16,4},{20,8},{24,12},{28,16},{1,21},{... | collective-permute-start | bytes 393224 | tf_op jit(solution)/shard_map/ppermute | solution.py:35
  111.1 16.8 %collective-permute-start.21 = (f16[64,1024]{1,0:T(8,128)(2,1)S(1)}, f16[64,1024]{1,0:T(8,128)(2,1)}, u32[]{:S(2)}, u32[]{:S(2)}) collective-permute-start(f16[64,1024]{1,0:T(8,128)(2,1)S(1)} %get-tuple-element.32), channel_id=1, source_target_pairs={{0,12},{4,16},{8,20},{12,24},{16,28},{20,0},{24,4},{28,8},{1,13},{... | collective-permute-start | bytes 393224 | tf_op jit(solution)/shard_map/ppermute | solution.py:35
  113.5 14.4 %collective-permute-start.20 = (f16[64,1024]{1,0:T(8,128)(2,1)S(1)}, f16[64,1024]{1,0:T(8,128)(2,1)}, u32[]{:S(2)}, u32[]{:S(2)}) collective-permute-start(f16[64,1024]{1,0:T(8,128)(2,1)S(1)} %get-tuple-element.33), channel_id=1, source_target_pairs={{0,16},{4,20},{8,24},{12,28},{16,0},{20,4},{24,8},{28,12},{1,17},{... | collective-permute-start | bytes 393224 | tf_op jit(solution)/shard_map/ppermute | solution.py:35
  125.0 11.2 %collective-permute-start.25 = (f16[64,1024]{1,0:T(8,128)(2,1)S(1)}, f16[64,1024]{1,0:T(8,128)(2,1)S(1)}, u32[]{:S(2)}, u32[]{:S(2)}) collective-permute-start(f16[64,1024]{1,0:T(8,128)(2,1)S(1)} %get-tuple-element.27), channel_id=1, source_target_pairs={{0,4},{4,8},{8,12},{12,16},{16,20},{20,24},{24,28},{28,0},{1,5},{5... | collective-permute-start | bytes 393224 | tf_op jit(solution)/shard_map/ppermute | solution.py:35
  125.4 10.7 %collective-permute-start.26 = (f16[64,1024]{1,0:T(8,128)(2,1)S(1)}, f16[64,1024]{1,0:T(8,128)(2,1)S(1)}, u32[]{:S(2)}, u32[]{:S(2)}) collective-permute-start(f16[64,1024]{1,0:T(8,128)(2,1)S(1)} %get-tuple-element.28), channel_id=1, source_target_pairs={{0,28},{4,0},{8,4},{12,8},{16,12},{20,16},{24,20},{28,24},{1,29},{... | collective-permute-start | bytes 393224 | tf_op jit(solution)/shard_map/ppermute | solution.py:35
  (3 other events, 7.0 us)

commit v4 on v3

--- a/solution.py
+++ b/solution.py
@@ -186,7 +186,7 @@
     near[3] = shifted(near[1], -2)
     near[5] = shifted(near[7], 2)
     far = []
-    for block in near:
+    for k, block in enumerate(near):
         far.append(swapped(block))
 
     message = (PLANE_N, 2 * TILES, LANES)
@@ -224,20 +224,25 @@
     )
     arrived = swapped(other_part)
     loss_sum = loss_sum + swapped(loss_sum)
-    for bit in (1, 2):
-        loss_sum = loss_sum + across(loss_sum, bit)
-    crossed = across(loss_sum, 4)
-    mean_loss = ((rows_loss + (loss_sum + crossed)) * (1.0 / (2 * ROWS * 256)))[0, 0]
+    loss_sum = loss_sum + across(loss_sum, 1)
+    apart = {}
+    for bits in (4, 2, 6):
+        apart[bits] = across(loss_sum, bits)
+    loss_sum = (loss_sum + apart[4]) + (apart[2] + apart[6])
+    mean_loss = ((rows_loss + loss_sum) * (1.0 / (2 * ROWS * 256)))[0, 0]
 
     text_part = lax.dot_general(weights, image_all, TN, preferred_element_type=f32)
     text_part = (WIRE_SCALE * text_part).astype(f16).reshape(PLANE_N, ROWS, width)
     text_back = exchanged(text_part, PLANE)
     factor = logit_scale[0] * (0.5 / WIRE_SCALE)
-    image_part = [
-        near_part[k * ROWS : (k + 1) * ROWS] + arrived[k * ROWS : (k + 1) * ROWS]
-        for k in range(LINE_Z)
-    ]
-    leaving = [part.astype(f16) for part in image_part]
+    leaving = {}
+    near_rest, arrived_rest = lax.optimization_barrier((near_part, arrived))
+    for parts_of, blocks in (
+        ((near_part, arrived), FAR_FIRST[:3]), ((near_rest, arrived_rest), FAR_FIRST[3:])
+    ):
+        for k in blocks:
+            here, there = (part[k * ROWS : (k + 1) * ROWS] for part in parts_of)
+            leaving[k] = (here + there).astype(f16)
     back = {}
     for k in FAR_FIRST:
         back[k] = shifted(leaving[k], k)
@@ -245,11 +250,11 @@
     for k in range(1, PLANE_N):
         text_sum = text_sum + text_back[k].astype(f32)
     text_grad = factor * text_sum
-    image_sum = image_part[0]
-    for k in FAR_FIRST[:5]:
+    image_sum = near_part[:ROWS] + arrived[:ROWS]
+    for k in FAR_FIRST[:3]:
         image_sum = image_sum + back[k].astype(f32)
     image_sum = lax.optimization_barrier(image_sum)
-    for k in FAR_FIRST[5:]:
+    for k in FAR_FIRST[3:]:
         image_sum = image_sum + back[k].astype(f32)
     image_grad = factor * image_sum
     return (mean_loss, image_grad, text_grad)

time: 137 us -> 152 us (1.11)
  starting transfers between devices: 51.4 us -> 60.7 us
  waiting for transfers between devices: 33.9 us -> 37.8 us
    ppermute x3 -> x4, waiting for transfers between devices: 10.8 us -> 4.75 us  [across(): return lax.ppermute(array, 'z', [(k, k ^ bit) for k in range(LINE_Z)])]
    ppermute x14, starting transfers between devices: 27.3 us -> 32.5 us  [shifted(): lax.ppermute(array, 'z', [(k, (k + by) % LINE_Z) for k in range(LINE_Z)])]
    all_to_all x2, waiting for transfers between devices: 7.34 us -> 12 us  [exchanged(): return lax.all_to_all(message, axis, 0, 0, tiled=True)]
    ppermute x3 -> x4, starting transfers between devices: 1.73 us -> 6.02 us  [across(): return lax.ppermute(array, 'z', [(k, k ^ bit) for k in range(LINE_Z)])]
    ppermute x10, waiting for transfers between devices: 1.75 us -> 4.62 us  [swapped(): return lax.ppermute(array, 'c', [(0, 1), (1, 0)])]
    ppermute x14, waiting for transfers between devices: 14 us -> 16.4 us  [shifted(): lax.ppermute(array, 'z', [(k, (k + by) % LINE_Z) for k in range(LINE_Z)])]
  transfers between devices with their start and end apart: 29 -> 30, of which waited for: 12 -> 12; matrix products, arithmetic and copies ran while one was open for 7% -> 4% of each run, Pallas kernels for 0% -> 0%
where the time goes in v4:
time: 152 us
  starting transfers between devices  60.7 us (40%)
  waiting for transfers between devices  37.8 us (25%)
  blocking collectives  26.3 us (17%)
  Pallas kernels  9.57 us (6%)
  other arithmetic  7.3 us (5%)
  local copies, waits for them, and re-layouts  4.69 us (3%)
  matrix products  3.75 us (2%)
    ppermute x14, starting transfers between devices, shifted(): lax.ppermute(array, 'z', [(k, (k + by) % LINE_Z) for k in range(LINE_Z)])  32.5 us
    all_to_all x2, blocking collectives, exchanged(): return lax.all_to_all(message, axis, 0, 0, tiled=True)  26.3 us
    ppermute x14, waiting for transfers between devices, shifted(): lax.ppermute(array, 'z', [(k, (k + by) % LINE_Z) for k in range(LINE_Z)])  16.4 us
    all_to_all x2, starting transfers between devices, exchanged(): return lax.all_to_all(message, axis, 0, 0, tiled=True)  12.1 us
    all_to_all x2, waiting for transfers between devices, exchanged(): return lax.all_to_all(message, axis, 0, 0, tiled=True)  12 us
    ppermute x10, starting transfers between devices, swapped(): return lax.ppermute(array, 'c', [(0, 1), (1, 0)])  10 us
    pallas_call x3, Pallas kernels, call(): pl.pallas_call(kernel, out_shape=[jax.ShapeDtypeStruct(*o) for o in outs]...  9.57 us
    ppermute x4, starting transfers between devices, across(): return lax.ppermute(array, 'z', [(k, k ^ bit) for k in range(LINE_Z)])  6.02 us
  transfers between devices with their start and end apart: 30, of which 12 were waited for; matrix products, arithmetic and copies ran while one was open for 4% of the time, Pallas kernels for 0%

profile of v4, /device:TPU:1, one launch (start us, length us, event | category | flops | bytes accessed | tf_op | source)
XLA Modules:
  0.0 151.5 jit_solution(8155969225773595461)
XLA Ops:
  0.6 2.6 %broadcast_in_dim.2 = bf16[16,64,1024]{2,1,0:T(8,128)(2,1)} broadcast(bf16[64,1024]{1,0:T(8,128)(2,1)} %own_text.1), dimensions={1,2} | broadcast | bytes 2228224 | tf_op jit(solution)/shard_map/broadcast_in_dim | solution.py:181
  3.2 7.7 %all-to-all-start = ((bf16[16,64,1024]{2,1,0:T(8,128)(2,1)}), bf16[16,64,1024]{2,1,0:T(8,128)(2,1)S(1)}, u32[]{:S(2)}, u32[]{:S(2)}) async-start(bf16[16,64,1024]{2,1,0:T(8,128)(2,1)} %broadcast_in_dim.2), calls=%async_computation | async-start | bytes 4194304 | tf_op jit(solution)/shard_map/all_to_all | solution.py:31
  12.0 3.0 %collective-permute-start.6 = (bf16[64,1024]{1,0:T(8,128)(2,1)S(1)}, bf16[64,1024]{1,0:T(8,128)(2,1)S(1)}, u32[]{:S(2)}, u32[]{:S(2)}) collective-permute-start(bf16[64,1024]{1,0:T(8,128)(2,1)S(1)} %constant_dynamic-slice_fusion.refs_0_), channel_id=1, source_target_pairs={{0,8},{4,12},{8,16},{12,20},{16,24},{20,28},{24,0},{28,4},{1,9},{5... | collective-permute-start | bytes 393224 | tf_op jit(solution)/shard_map/ppermute | solution.py:35
  15.0 1.6 %collective-permute-start.4 = (bf16[64,1024]{1,0:T(8,128)(2,1)S(1)}, bf16[64,1024]{1,0:T(8,128)(2,1)S(1)}, u32[]{:S(2)}, u32[]{:S(2)}) collective-permute-start(bf16[64,1024]{1,0:T(8,128)(2,1)S(1)} %constant_dynamic-slice_fusion.refs_0_), channel_id=1, source_target_pairs={{0,4},{4,8},{8,12},{12,16},{16,20},{20,24},{24,28},{28,0},{1,5},{5... | collective-permute-start | bytes 393224 | tf_op jit(solution)/shard_map/ppermute | solution.py:35
  16.6 4.2 %collective-permute-start.3 = (bf16[64,1024]{1,0:T(8,128)(2,1)S(1)}, bf16[64,1024]{1,0:T(8,128)(2,1)S(1)}, u32[]{:S(2)}, u32[]{:S(2)}) collective-permute-start(bf16[64,1024]{1,0:T(8,128)(2,1)S(1)} %constant_dynamic-slice_fusion.refs_0_), channel_id=1, source_target_pairs={{0,16},{4,20},{8,24},{12,28},{16,0},{20,4},{24,8},{28,12},{1,17},{... | collective-permute-start | bytes 393224 | tf_op jit(solution)/shard_map/ppermute | solution.py:35
  20.9 1.9 %collective-permute-start = (bf16[64,1024]{1,0:T(8,128)(2,1)S(1)}, bf16[64,1024]{1,0:T(8,128)(2,1)S(1)}, u32[]{:S(2)}, u32[]{:S(2)}) collective-permute-start(bf16[64,1024]{1,0:T(8,128)(2,1)S(1)} %constant_dynamic-slice_fusion.refs_0_), channel_id=1, source_target_pairs={{0,28},{4,0},{8,4},{12,8},{16,12},{20,16},{24,20},{28,24},{1,29},{... | collective-permute-start | bytes 393224 | tf_op jit(solution)/shard_map/ppermute | solution.py:35
  24.0 1.5 collective-permute-start.13
  25.5 1.5 %collective-permute-done.4.refs_7_ = bf16[64,1024]{1,0:T(8,128)(2,1)S(1)} collective-permute-done((bf16[64,1024]{1,0:T(8,128)(2,1)S(1)}, bf16[64,1024]{1,0:T(8,128)(2,1)S(1)}, u32[]{:S(2)}, u32[]{:S(2)}) %collective-permute-start.4) | collective-permute-done | bytes 131104 | tf_op jit(solution)/shard_map/ppermute | solution.py:35
  27.7 4.4 %collective-permute-done.3.refs_4_ = bf16[64,1024]{1,0:T(8,128)(2,1)S(1)} collective-permute-done((bf16[64,1024]{1,0:T(8,128)(2,1)S(1)}, bf16[64,1024]{1,0:T(8,128)(2,1)S(1)}, u32[]{:S(2)}, u32[]{:S(2)}) %collective-permute-start.3) | collective-permute-done | bytes 131104 | tf_op jit(solution)/shard_map/ppermute | solution.py:35
  32.1 4.6 %collective-permute-start.5 = (bf16[64,1024]{1,0:T(8,128)(2,1)S(1)}, bf16[64,1024]{1,0:T(8,128)(2,1)}, u32[]{:S(2)}, u32[]{:S(2)}) collective-permute-start(bf16[64,1024]{1,0:T(8,128)(2,1)S(1)} %collective-permute-done.4.refs_7_), channel_id=1, source_target_pairs={{0,8},{4,12},{8,16},{12,20},{16,24},{20,28},{24,0},{28,4},{1,9},{5... | collective-permute-start | bytes 393224 | tf_op jit(solution)/shard_map/ppermute | solution.py:35
  40.4 1.5 collective-permute-start.12
  42.0 1.9 %collective-permute-start.10 = (bf16[64,1024]{1,0:T(8,128)(2,1)}, bf16[64,1024]{1,0:T(8,128)(2,1)}, u32[]{:S(2)}, u32[]{:S(2)}) collective-permute-start(bf16[64,1024]{1,0:T(8,128)(2,1)} %collective-permute-done.2.refs_3_), channel_id=1, source_target_pairs={{0,2},{2,0},{1,3},{3,1},{4,6},{6,4},{5,7},{7,5},{8,10},{10,8},{9,1... | collective-permute-start | bytes 393224 | tf_op jit(solution)/shard_map/ppermute | solution.py:43
  46.2 4.8 %shard_map.58 = (f32[1024,1024]{1,0:T(8,128)S(1)}, bf16[1024,1024]{1,0:T(8,128)(2,1)S(1)}, f32[16,8,128]{2,1,0:T(8,128)S(1)}, f32[8,128]{1,0:T(8,128)S(1)}, f32[8,128]{1,0:T(8,128)S(1)}) custom-call(s32[3]{0:T(128)S(1)} %pad_add_fusion.pos, f32[1]{0:T(128)S(6)} %copy.6.scale, bf16[64,1024]{1,0:T(8,128)(2,1)S(1)} %copy-done.3, ...), custom_call_target="tpu_custom_call" | custom-call | tf_op jit(solution)/shard_map/pallas_call | solution.py:162
  50.9 13.5 %all_to_all.20.heard = f32[16,8,128]{2,1,0:T(8,128)S(1)} all-to-all(f32[16,8,128]{2,1,0:T(8,128)S(1)} %get-tuple-element.18), channel_id=1, replica_groups=mesh['xh'=2,'y'=4,'z'=8,'c'=2,'xl'=2] {'z','c'}, dimensions={0} | all-to-all | bytes 131072 | tf_op jit(solution)/shard_map/all_to_all | solution.py:31
  65.1 12.8 %all_to_all.21.heard = f32[16,16,128]{2,1,0:T(8,128)S(1)} all-to-all(f32[16,16,128]{2,1,0:T(8,128)S(1)} %get-tuple-element.22), channel_id=1, replica_groups=mesh['xh'=2,'y'=4,'z'=8,'c'=2,'xl'=2] {'xh','y','xl'}, dimensions={0} | all-to-all | bytes 262144 | tf_op jit(solution)/shard_map/all_to_all | solution.py:31
  78.0 4.1 %shard_map.60 = (bf16[1024,1024]{1,0:T(8,128)(2,1)S(1)}, f32[512,1024]{1,0:T(8,128)S(1)}, f32[512,1024]{1,0:T(8,128)S(1)}, f32[8,128]{1,0:T(8,128)S(1)}, f32[8,128]{1,0:T(8,128)S(1)}) custom-call(s32[3]{0:T(128)S(1)} %pad_add_fusion.pos, f32[1024,1024]{1,0:T(8,128)S(1)} %get-tuple-element.17.scores, f32[16,128]{1,0:T(8,128)S(1)} %get-tuple-element.21.row_lse, ...), custom_call_target="tpu_custom_call" | custom-call | tf_op jit(solution)/shard_map/pallas_call | solution.py:162
  82.1 3.7 %multiply_convert_fusion = f16[1024,1024]{1,0:T(8,128)(2,1)} fusion(bf16[1024,1024]{1,0:T(8,128)(2,1)S(1)} %get-tuple-element.29, bf16[1024,1024]{1,0:T(8,128)(2,1)S(1)} %get-tuple-element.30), kind=kOutput, calls=%fused_computation | convolution fusion | flops 2149580800 | bytes 6291456 | tf_op jit(solution)/shard_map/dot_general | solution.py:234
  85.9 4.4 %all-to-all-start.3 = ((f16[16,64,1024]{2,1,0:T(8,128)(2,1)}), f16[16,64,1024]{2,1,0:T(8,128)(2,1)}, u32[]{:S(2)}, u32[]{:S(2)}) async-start(f16[16,64,1024]{2,1,0:T(8,128)(2,1)} %bitcast.6), calls=%async_computation.3 | async-start | bytes 4194304 | tf_op jit(solution)/shard_map/all_to_all | solution.py:31
  90.3 1.6 %collective-permute-start.20 = (f32[512,1024]{1,0:T(8,128)}, f32[512,1024]{1,0:T(8,128)}, u32[]{:S(2)}, u32[]{:S(2)}) collective-permute-start(f32[512,1024]{1,0:T(8,128)} %copy-done.6), channel_id=1, source_target_pairs={{0,2},{2,0},{1,3},{3,1},{4,6},{6,4},{5,7},{7,5},{8,10},{10,8},{9,1... | collective-permute-start | bytes 6291464 | tf_op jit(solution)/shard_map/ppermute | solution.py:43
  92.0 4.0 %collective-permute-done.15 = f32[8,128]{1,0:T(8,128)S(1)} collective-permute-done((f32[8,128]{1,0:T(8,128)S(1)}, f32[8,128]{1,0:T(8,128)S(1)}, u32[]{:S(2)}, u32[]{:S(2)}) %collective-permute-start.15) | collective-permute-done | bytes 4128 | tf_op jit(solution)/shard_map/ppermute | solution.py:43
  96.4 2.5 %collective-permute-done.16 = f32[8,128]{1,0:T(8,128)S(1)} collective-permute-done((f32[8,128]{1,0:T(8,128)S(1)}, f32[8,128]{1,0:T(8,128)S(1)}, u32[]{:S(2)}, u32[]{:S(2)}) %collective-permute-start.16) | collective-permute-done | bytes 4128 | tf_op jit(solution)/shard_map/ppermute | solution.py:39
  100.1 4.5 %collective-permute-start.17 = (f32[8,128]{1,0:T(8,128)S(1)}, f32[8,128]{1,0:T(8,128)S(1)}, u32[]{:S(2)}, u32[]{:S(2)}) collective-permute-start(f32[8,128]{1,0:T(8,128)S(1)} %add.126), channel_id=1, source_target_pairs={{0,16},{4,20},{8,24},{12,28},{16,0},{20,4},{24,8},{28,12},{1,17},{... | collective-permute-start | bytes 12296 | tf_op jit(solution)/shard_map/ppermute | solution.py:39
  104.6 2.2 %collective-permute-done.17 = f32[8,128]{1,0:T(8,128)S(1)} collective-permute-done((f32[8,128]{1,0:T(8,128)S(1)}, f32[8,128]{1,0:T(8,128)S(1)}, u32[]{:S(2)}, u32[]{:S(2)}) %collective-permute-start.17) | collective-permute-done | bytes 4128 | tf_op jit(solution)/shard_map/ppermute | solution.py:39
  107.4 12.0 %all-to-all-done.3 = f16[16,64,1024]{2,1,0:T(8,128)(2,1)} async-done(((f16[16,64,1024]{2,1,0:T(8,128)(2,1)}), f16[16,64,1024]{2,1,0:T(8,128)(2,1)}, u32[]{:S(2)}, u32[]{:S(2)}) %all-to-all-start.3) | async-done | bytes 2097184 | tf_op jit(solution)/shard_map/all_to_all | solution.py:31
  119.4 2.7 %fusion.6 = f32[64,1024]{1,0:T(8,128)} fusion(f16[16,64,1024]{2,1,0:T(8,128)(2,1)} %all-to-all-done.3, f32[]{:T(128)} %bitcast.5), kind=kLoop, calls=%fused_computation.12 | loop fusion | flops 2097152 | bytes 2359300 | tf_op jit(solution)/shard_map/mul | solution.py:252
  123.4 3.9 %collective-permute-start.23 = (f16[64,1024]{1,0:T(8,128)(2,1)S(1)}, f16[64,1024]{1,0:T(8,128)(2,1)S(1)}, u32[]{:S(2)}, u32[]{:S(2)}) collective-permute-start(f16[64,1024]{1,0:T(8,128)(2,1)S(1)} %get-tuple-element.36), channel_id=1, source_target_pairs={{0,20},{4,24},{8,28},{12,0},{16,4},{20,8},{24,12},{28,16},{1,21},{... | collective-permute-start | bytes 393224 | tf_op jit(solution)/shard_map/ppermute | solution.py:35
  127.3 1.4 add_convert_fusion.3
  128.8 2.2 %collective-permute-start.24 = (f16[64,1024]{1,0:T(8,128)(2,1)S(1)}, f16[64,1024]{1,0:T(8,128)(2,1)S(1)}, u32[]{:S(2)}, u32[]{:S(2)}) collective-permute-start(f16[64,1024]{1,0:T(8,128)(2,1)S(1)} %get-tuple-element.31), channel_id=1, source_target_pairs={{0,8},{4,12},{8,16},{12,20},{16,24},{20,28},{24,0},{28,4},{1,9},{5... | collective-permute-start | bytes 393224 | tf_op jit(solution)/shard_map/ppermute | solution.py:35
  130.9 2.1 %collective-permute-start.27 = (f16[64,1024]{1,0:T(8,128)(2,1)S(1)}, f16[64,1024]{1,0:T(8,128)(2,1)S(1)}, u32[]{:S(2)}, u32[]{:S(2)}) collective-permute-start(f16[64,1024]{1,0:T(8,128)(2,1)S(1)} %get-tuple-element.32), channel_id=1, source_target_pairs={{0,28},{4,0},{8,4},{12,8},{16,12},{20,16},{24,20},{28,24},{1,29},{... | collective-permute-start | bytes 393224 | tf_op jit(solution)/shard_map/ppermute | solution.py:35
  134.3 5.7 %collective-permute-start.25 = (f16[64,1024]{1,0:T(8,128)(2,1)S(1)}, f16[64,1024]{1,0:T(8,128)(2,1)S(1)}, u32[]{:S(2)}, u32[]{:S(2)}) collective-permute-start(f16[64,1024]{1,0:T(8,128)(2,1)S(1)} %get-tuple-element.34), channel_id=1, source_target_pairs={{0,24},{4,28},{8,0},{12,4},{16,8},{20,12},{24,16},{28,20},{1,25},{... | collective-permute-start | bytes 393224 | tf_op jit(solution)/shard_map/ppermute | solution.py:35
  140.1 1.4 collective-permute-done.22
  143.3 7.4 %collective-permute-done.26 = f16[64,1024]{1,0:T(8,128)(2,1)S(1)} collective-permute-done((f16[64,1024]{1,0:T(8,128)(2,1)S(1)}, f16[64,1024]{1,0:T(8,128)(2,1)S(1)}, u32[]{:S(2)}, u32[]{:S(2)}) %collective-permute-start.26) | collective-permute-done | bytes 131104 | tf_op jit(solution)/shard_map/ppermute | solution.py:35
  (60 shorter events, 16.5 us)
Async XLA Ops:
  3.2 42.0 %copy-start.3 = (bf16[64,1024]{1,0:T(8,128)(2,1)S(1)}, bf16[64,1024]{1,0:T(8,128)(2,1)}, u32[]{:S(2)}) copy-start(bf16[64,1024]{1,0:T(8,128)(2,1)} %own_text.1) | copy-start | bytes 393220
  3.2 42.0 %all-to-all-start = ((bf16[16,64,1024]{2,1,0:T(8,128)(2,1)}), bf16[16,64,1024]{2,1,0:T(8,128)(2,1)S(1)}, u32[]{:S(2)}, u32[]{:S(2)}) async-start(bf16[16,64,1024]{2,1,0:T(8,128)(2,1)} %broadcast_in_dim.2), calls=%async_computation | async-start | bytes 4194304 | tf_op jit(solution)/shard_map/all_to_all | solution.py:31
  11.0 11.8 %collective-permute-start.7 = (bf16[64,1024]{1,0:T(8,128)(2,1)S(1)}, bf16[64,1024]{1,0:T(8,128)(2,1)S(1)}, u32[]{:S(2)}, u32[]{:S(2)}) collective-permute-start(bf16[64,1024]{1,0:T(8,128)(2,1)S(1)} %constant_dynamic-slice_fusion.refs_0_), channel_id=1, source_target_pairs={{0,2},{2,0},{1,3},{3,1},{4,6},{6,4},{5,7},{7,5},{8,10},{10,8},{9,1... | collective-permute-start | bytes 393224 | tf_op jit(solution)/shard_map/ppermute | solution.py:43
  12.0 12.0 %collective-permute-start.6 = (bf16[64,1024]{1,0:T(8,128)(2,1)S(1)}, bf16[64,1024]{1,0:T(8,128)(2,1)S(1)}, u32[]{:S(2)}, u32[]{:S(2)}) collective-permute-start(bf16[64,1024]{1,0:T(8,128)(2,1)S(1)} %constant_dynamic-slice_fusion.refs_0_), channel_id=1, source_target_pairs={{0,8},{4,12},{8,16},{12,20},{16,24},{20,28},{24,0},{28,4},{1,9},{5... | collective-permute-start | bytes 393224 | tf_op jit(solution)/shard_map/ppermute | solution.py:35
  15.0 12.0 %collective-permute-start.4 = (bf16[64,1024]{1,0:T(8,128)(2,1)S(1)}, bf16[64,1024]{1,0:T(8,128)(2,1)S(1)}, u32[]{:S(2)}, u32[]{:S(2)}) collective-permute-start(bf16[64,1024]{1,0:T(8,128)(2,1)S(1)} %constant_dynamic-slice_fusion.refs_0_), channel_id=1, source_target_pairs={{0,4},{4,8},{8,12},{12,16},{16,20},{20,24},{24,28},{28,0},{1,5},{5... | collective-permute-start | bytes 393224 | tf_op jit(solution)/shard_map/ppermute | solution.py:35
  16.6 15.4 %collective-permute-start.3 = (bf16[64,1024]{1,0:T(8,128)(2,1)S(1)}, bf16[64,1024]{1,0:T(8,128)(2,1)S(1)}, u32[]{:S(2)}, u32[]{:S(2)}) collective-permute-start(bf16[64,1024]{1,0:T(8,128)(2,1)S(1)} %constant_dynamic-slice_fusion.refs_0_), channel_id=1, source_target_pairs={{0,16},{4,20},{8,24},{12,28},{16,0},{20,4},{24,8},{28,12},{1,17},{... | collective-permute-start | bytes 393224 | tf_op jit(solution)/shard_map/ppermute | solution.py:35
  20.9 15.8 %collective-permute-start = (bf16[64,1024]{1,0:T(8,128)(2,1)S(1)}, bf16[64,1024]{1,0:T(8,128)(2,1)S(1)}, u32[]{:S(2)}, u32[]{:S(2)}) collective-permute-start(bf16[64,1024]{1,0:T(8,128)(2,1)S(1)} %constant_dynamic-slice_fusion.refs_0_), channel_id=1, source_target_pairs={{0,28},{4,0},{8,4},{12,8},{16,12},{20,16},{24,20},{28,24},{1,29},{... | collective-permute-start | bytes 393224 | tf_op jit(solution)/shard_map/ppermute | solution.py:35
  22.8 14.6 %collective-permute-start.1 = (bf16[64,1024]{1,0:T(8,128)(2,1)S(1)}, bf16[64,1024]{1,0:T(8,128)(2,1)S(1)}, u32[]{:S(2)}, u32[]{:S(2)}) collective-permute-start(bf16[64,1024]{1,0:T(8,128)(2,1)S(1)} %constant_dynamic-slice_fusion.refs_0_), channel_id=1, source_target_pairs={{0,24},{4,28},{8,0},{12,4},{16,8},{20,12},{24,16},{28,20},{1,25},{... | collective-permute-start | bytes 393224 | tf_op jit(solution)/shard_map/ppermute | solution.py:35
  24.0 14.6 %collective-permute-start.13 = (bf16[64,1024]{1,0:T(8,128)(2,1)S(1)}, bf16[64,1024]{1,0:T(8,128)(2,1)S(1)}, u32[]{:S(2)}, u32[]{:S(2)}) collective-permute-start(bf16[64,1024]{1,0:T(8,128)(2,1)S(1)} %collective-permute-done.6.refs_6_), channel_id=1, source_target_pairs={{0,2},{2,0},{1,3},{3,1},{4,6},{6,4},{5,7},{7,5},{8,10},{10,8},{9,1... | collective-permute-start | bytes 393224 | tf_op jit(solution)/shard_map/ppermute | solution.py:43
  27.0 11.6 %collective-permute-start.14 = (bf16[64,1024]{1,0:T(8,128)(2,1)S(1)}, bf16[64,1024]{1,0:T(8,128)(2,1)S(1)}, u32[]{:S(2)}, u32[]{:S(2)}) collective-permute-start(bf16[64,1024]{1,0:T(8,128)(2,1)S(1)} %collective-permute-done.4.refs_7_), channel_id=1, source_target_pairs={{0,2},{2,0},{1,3},{3,1},{4,6},{6,4},{5,7},{7,5},{8,10},{10,8},{9,1... | collective-permute-start | bytes 393224 | tf_op jit(solution)/shard_map/ppermute | solution.py:43
  32.1 8.3 %collective-permute-start.5 = (bf16[64,1024]{1,0:T(8,128)(2,1)S(1)}, bf16[64,1024]{1,0:T(8,128)(2,1)}, u32[]{:S(2)}, u32[]{:S(2)}) collective-permute-start(bf16[64,1024]{1,0:T(8,128)(2,1)S(1)} %collective-permute-done.4.refs_7_), channel_id=1, source_target_pairs={{0,8},{4,12},{8,16},{12,20},{16,24},{20,28},{24,0},{28,4},{1,9},{5... | collective-permute-start | bytes 393224 | tf_op jit(solution)/shard_map/ppermute | solution.py:35
  36.7 5.3 %collective-permute-start.2 = (bf16[64,1024]{1,0:T(8,128)(2,1)S(1)}, bf16[64,1024]{1,0:T(8,128)(2,1)}, u32[]{:S(2)}, u32[]{:S(2)}) collective-permute-start(bf16[64,1024]{1,0:T(8,128)(2,1)S(1)} %collective-permute-done.refs_1_), channel_id=1, source_target_pairs={{0,24},{4,28},{8,0},{12,4},{16,8},{20,12},{24,16},{28,20},{1,25},{... | collective-permute-start | bytes 393224 | tf_op jit(solution)/shard_map/ppermute | solution.py:35
  37.3 7.3 %collective-permute-start.8 = (bf16[64,1024]{1,0:T(8,128)(2,1)S(1)}, bf16[64,1024]{1,0:T(8,128)(2,1)}, u32[]{:S(2)}, u32[]{:S(2)}) collective-permute-start(bf16[64,1024]{1,0:T(8,128)(2,1)S(1)} %collective-permute-done.refs_1_), channel_id=1, source_target_pairs={{0,2},{2,0},{1,3},{3,1},{4,6},{6,4},{5,7},{7,5},{8,10},{10,8},{9,1... | collective-permute-start | bytes 393224 | tf_op jit(solution)/shard_map/ppermute | solution.py:43
  38.5 6.1 %collective-permute-start.11 = (bf16[64,1024]{1,0:T(8,128)(2,1)S(1)}, bf16[64,1024]{1,0:T(8,128)(2,1)}, u32[]{:S(2)}, u32[]{:S(2)}) collective-permute-start(bf16[64,1024]{1,0:T(8,128)(2,1)S(1)} %collective-permute-done.3.refs_4_), channel_id=1, source_target_pairs={{0,2},{2,0},{1,3},{3,1},{4,6},{6,4},{5,7},{7,5},{8,10},{10,8},{9,1... | collective-permute-start | bytes 393224 | tf_op jit(solution)/shard_map/ppermute | solution.py:43
  39.3 5.4 %collective-permute-start.9 = (bf16[64,1024]{1,0:T(8,128)(2,1)S(1)}, bf16[64,1024]{1,0:T(8,128)(2,1)}, u32[]{:S(2)}, u32[]{:S(2)}) collective-permute-start(bf16[64,1024]{1,0:T(8,128)(2,1)S(1)} %collective-permute-done.1.refs_2_), channel_id=1, source_target_pairs={{0,2},{2,0},{1,3},{3,1},{4,6},{6,4},{5,7},{7,5},{8,10},{10,8},{9,1... | collective-permute-start | bytes 393224 | tf_op jit(solution)/shard_map/ppermute | solution.py:43
  40.4 4.2 %collective-permute-start.12 = (bf16[64,1024]{1,0:T(8,128)(2,1)}, bf16[64,1024]{1,0:T(8,128)(2,1)}, u32[]{:S(2)}, u32[]{:S(2)}) collective-permute-start(bf16[64,1024]{1,0:T(8,128)(2,1)} %collective-permute-done.5.refs_5_), channel_id=1, source_target_pairs={{0,2},{2,0},{1,3},{3,1},{4,6},{6,4},{5,7},{7,5},{8,10},{10,8},{9,1... | collective-permute-start | bytes 393224 | tf_op jit(solution)/shard_map/ppermute | solution.py:43
  42.0 3.3 %collective-permute-start.10 = (bf16[64,1024]{1,0:T(8,128)(2,1)}, bf16[64,1024]{1,0:T(8,128)(2,1)}, u32[]{:S(2)}, u32[]{:S(2)}) collective-permute-start(bf16[64,1024]{1,0:T(8,128)(2,1)} %collective-permute-done.2.refs_3_), channel_id=1, source_target_pairs={{0,2},{2,0},{1,3},{3,1},{4,6},{6,4},{5,7},{7,5},{8,10},{10,8},{9,1... | collective-permute-start | bytes 393224 | tf_op jit(solution)/shard_map/ppermute | solution.py:43
  85.9 33.5 %all-to-all-start.3 = ((f16[16,64,1024]{2,1,0:T(8,128)(2,1)}), f16[16,64,1024]{2,1,0:T(8,128)(2,1)}, u32[]{:S(2)}, u32[]{:S(2)}) async-start(f16[16,64,1024]{2,1,0:T(8,128)(2,1)} %bitcast.6), calls=%async_computation.3 | async-start | bytes 4194304 | tf_op jit(solution)/shard_map/all_to_all | solution.py:31
  90.3 31.8 %copy-start.2 = (f32[512,1024]{1,0:T(8,128)S(1)}, f32[512,1024]{1,0:T(8,128)}, u32[]{:S(2)}) copy-start(f32[512,1024]{1,0:T(8,128)} %copy-done.1) | copy-start | bytes 6291460
  90.3 31.8 %collective-permute-start.20 = (f32[512,1024]{1,0:T(8,128)}, f32[512,1024]{1,0:T(8,128)}, u32[]{:S(2)}, u32[]{:S(2)}) collective-permute-start(f32[512,1024]{1,0:T(8,128)} %copy-done.6), channel_id=1, source_target_pairs={{0,2},{2,0},{1,3},{3,1},{4,6},{6,4},{5,7},{7,5},{8,10},{10,8},{9,1... | collective-permute-start | bytes 6291464 | tf_op jit(solution)/shard_map/ppermute | solution.py:43
  91.9 4.1 %collective-permute-start.15 = (f32[8,128]{1,0:T(8,128)S(1)}, f32[8,128]{1,0:T(8,128)S(1)}, u32[]{:S(2)}, u32[]{:S(2)}) collective-permute-start(f32[8,128]{1,0:T(8,128)S(1)} %get-tuple-element.24), channel_id=1, source_target_pairs={{0,2},{2,0},{1,3},{3,1},{4,6},{6,4},{5,7},{7,5},{8,10},{10,8},{9,1... | collective-permute-start | bytes 12296 | tf_op jit(solution)/shard_map/ppermute | solution.py:43
  96.1 2.9 %collective-permute-start.16 = (f32[8,128]{1,0:T(8,128)S(1)}, f32[8,128]{1,0:T(8,128)S(1)}, u32[]{:S(2)}, u32[]{:S(2)}) collective-permute-start(f32[8,128]{1,0:T(8,128)S(1)} %add.125), channel_id=1, source_target_pairs={{0,4},{4,0},{8,12},{12,8},{16,20},{20,16},{24,28},{28,24},{1,5},{5... | collective-permute-start | bytes 12296 | tf_op jit(solution)/shard_map/ppermute | solution.py:39
  98.9 5.7 %collective-permute-start.19 = (f32[8,128]{1,0:T(8,128)S(1)}, f32[8,128]{1,0:T(8,128)S(1)}, u32[]{:S(2)}, u32[]{:S(2)}) collective-permute-start(f32[8,128]{1,0:T(8,128)S(1)} %add.126), channel_id=1, source_target_pairs={{0,24},{4,28},{8,16},{12,20},{16,8},{20,12},{24,0},{28,4},{1,25},{... | collective-permute-start | bytes 12296 | tf_op jit(solution)/shard_map/ppermute | solution.py:39
  99.5 5.1 %collective-permute-start.18 = (f32[8,128]{1,0:T(8,128)S(1)}, f32[8,128]{1,0:T(8,128)S(1)}, u32[]{:S(2)}, u32[]{:S(2)}) collective-permute-start(f32[8,128]{1,0:T(8,128)S(1)} %add.126), channel_id=1, source_target_pairs={{0,8},{4,12},{8,0},{12,4},{16,24},{20,28},{24,16},{28,20},{1,9},{5... | collective-permute-start | bytes 12296 | tf_op jit(solution)/shard_map/ppermute | solution.py:39
  100.1 6.8 %collective-permute-start.17 = (f32[8,128]{1,0:T(8,128)S(1)}, f32[8,128]{1,0:T(8,128)S(1)}, u32[]{:S(2)}, u32[]{:S(2)}) collective-permute-start(f32[8,128]{1,0:T(8,128)S(1)} %add.126), channel_id=1, source_target_pairs={{0,16},{4,20},{8,24},{12,28},{16,0},{20,4},{24,8},{28,12},{1,17},{... | collective-permute-start | bytes 12296 | tf_op jit(solution)/shard_map/ppermute | solution.py:39
  123.3 9.6 %collective-permute-start.21 = (f16[64,1024]{1,0:T(8,128)(2,1)S(1)}, f16[64,1024]{1,0:T(8,128)(2,1)S(1)}, u32[]{:S(2)}, u32[]{:S(2)}) collective-permute-start(f16[64,1024]{1,0:T(8,128)(2,1)S(1)} %get-tuple-element.35), channel_id=1, source_target_pairs={{0,16},{4,20},{8,24},{12,28},{16,0},{20,4},{24,8},{28,12},{1,17},{... | collective-permute-start | bytes 393224 | tf_op jit(solution)/shard_map/ppermute | solution.py:35
  123.4 10.9 %collective-permute-start.23 = (f16[64,1024]{1,0:T(8,128)(2,1)S(1)}, f16[64,1024]{1,0:T(8,128)(2,1)S(1)}, u32[]{:S(2)}, u32[]{:S(2)}) collective-permute-start(f16[64,1024]{1,0:T(8,128)(2,1)S(1)} %get-tuple-element.36), channel_id=1, source_target_pairs={{0,20},{4,24},{8,28},{12,0},{16,4},{20,8},{24,12},{28,16},{1,21},{... | collective-permute-start | bytes 393224 | tf_op jit(solution)/shard_map/ppermute | solution.py:35
  127.3 14.1 %collective-permute-start.22 = (f16[64,1024]{1,0:T(8,128)(2,1)S(1)}, f16[64,1024]{1,0:T(8,128)(2,1)S(1)}, u32[]{:S(2)}, u32[]{:S(2)}) collective-permute-start(f16[64,1024]{1,0:T(8,128)(2,1)S(1)} %get-tuple-element.37), channel_id=1, source_target_pairs={{0,12},{4,16},{8,20},{12,24},{16,28},{20,0},{24,4},{28,8},{1,13},{... | collective-permute-start | bytes 393224 | tf_op jit(solution)/shard_map/ppermute | solution.py:35
  128.8 14.6 %collective-permute-start.24 = (f16[64,1024]{1,0:T(8,128)(2,1)S(1)}, f16[64,1024]{1,0:T(8,128)(2,1)S(1)}, u32[]{:S(2)}, u32[]{:S(2)}) collective-permute-start(f16[64,1024]{1,0:T(8,128)(2,1)S(1)} %get-tuple-element.31), channel_id=1, source_target_pairs={{0,8},{4,12},{8,16},{12,20},{16,24},{20,28},{24,0},{28,4},{1,9},{5... | collective-permute-start | bytes 393224 | tf_op jit(solution)/shard_map/ppermute | solution.py:35
  130.9 12.4 %collective-permute-start.27 = (f16[64,1024]{1,0:T(8,128)(2,1)S(1)}, f16[64,1024]{1,0:T(8,128)(2,1)S(1)}, u32[]{:S(2)}, u32[]{:S(2)}) collective-permute-start(f16[64,1024]{1,0:T(8,128)(2,1)S(1)} %get-tuple-element.32), channel_id=1, source_target_pairs={{0,28},{4,0},{8,4},{12,8},{16,12},{20,16},{24,20},{28,24},{1,29},{... | collective-permute-start | bytes 393224 | tf_op jit(solution)/shard_map/ppermute | solution.py:35
  133.0 17.7 %collective-permute-start.26 = (f16[64,1024]{1,0:T(8,128)(2,1)S(1)}, f16[64,1024]{1,0:T(8,128)(2,1)S(1)}, u32[]{:S(2)}, u32[]{:S(2)}) collective-permute-start(f16[64,1024]{1,0:T(8,128)(2,1)S(1)} %get-tuple-element.33), channel_id=1, source_target_pairs={{0,4},{4,8},{8,12},{12,16},{16,20},{20,24},{24,28},{28,0},{1,5},{5... | collective-permute-start | bytes 393224 | tf_op jit(solution)/shard_map/ppermute | solution.py:35
  134.3 16.4 %collective-permute-start.25 = (f16[64,1024]{1,0:T(8,128)(2,1)S(1)}, f16[64,1024]{1,0:T(8,128)(2,1)S(1)}, u32[]{:S(2)}, u32[]{:S(2)}) collective-permute-start(f16[64,1024]{1,0:T(8,128)(2,1)S(1)} %get-tuple-element.34), channel_id=1, source_target_pairs={{0,24},{4,28},{8,0},{12,4},{16,8},{20,12},{24,16},{28,20},{1,25},{... | collective-permute-start | bytes 393224 | tf_op jit(solution)/shard_map/ppermute | solution.py:35
  (5 other events, 19.4 us)

commit v5 on v3

--- a/solution.py
+++ b/solution.py
@@ -224,10 +224,12 @@
     )
     arrived = swapped(other_part)
     loss_sum = loss_sum + swapped(loss_sum)
-    for bit in (1, 2):
-        loss_sum = loss_sum + across(loss_sum, bit)
-    crossed = across(loss_sum, 4)
-    mean_loss = ((rows_loss + (loss_sum + crossed)) * (1.0 / (2 * ROWS * 256)))[0, 0]
+    loss_sum = loss_sum + across(loss_sum, 1)
+    apart = {}
+    for bits in (4, 2, 6):
+        apart[bits] = across(loss_sum, bits)
+    loss_sum = (loss_sum + apart[4]) + (apart[2] + apart[6])
+    mean_loss = ((rows_loss + loss_sum) * (1.0 / (2 * ROWS * 256)))[0, 0]
 
     text_part = lax.dot_general(weights, image_all, TN, preferred_element_type=f32)
     text_part = (WIRE_SCALE * text_part).astype(f16).reshape(PLANE_N, ROWS, width)

time: 137 us -> 137 us (level)
  waiting for transfers between devices: 33.9 us -> 26.2 us
  starting transfers between devices: 51.4 us -> 58.6 us
    ppermute x3 -> x4, waiting for transfers between devices: 10.8 us -> 3.95 us  [across(): return lax.ppermute(array, 'z', [(k, k ^ bit) for k in range(LINE_Z)])]
    ppermute x3 -> x4, starting transfers between devices: 1.73 us -> 6.02 us  [across(): return lax.ppermute(array, 'z', [(k, k ^ bit) for k in range(LINE_Z)])]
    ppermute x14, starting transfers between devices: 27.3 us -> 30.3 us  [shifted(): lax.ppermute(array, 'z', [(k, (k + by) % LINE_Z) for k in range(LINE_Z)])]
  transfers between devices with their start and end apart: 29 -> 30, of which waited for: 12 -> 10; matrix products, arithmetic and copies ran while one was open for 7% -> 7% of each run, Pallas kernels for 0% -> 0%
where the time goes in v5:
time: 137 us
  starting transfers between devices  58.6 us (43%)
  blocking collectives  26.3 us (19%)
  waiting for transfers between devices  26.2 us (19%)
  Pallas kernels  8.8 us (6%)
  other arithmetic  6.68 us (5%)
  local copies, waits for them, and re-layouts  4.67 us (3%)
  matrix products  3.77 us (3%)
  between operations  1.42 us (1%)
    ppermute x14, starting transfers between devices, shifted(): lax.ppermute(array, 'z', [(k, (k + by) % LINE_Z) for k in range(LINE_Z)])  30.3 us
    all_to_all x2, blocking collectives, exchanged(): return lax.all_to_all(message, axis, 0, 0, tiled=True)  26.3 us
    ppermute x14, waiting for transfers between devices, shifted(): lax.ppermute(array, 'z', [(k, (k + by) % LINE_Z) for k in range(LINE_Z)])  13.5 us
    all_to_all x2, starting transfers between devices, exchanged(): return lax.all_to_all(message, axis, 0, 0, tiled=True)  12.3 us
    ppermute x10, starting transfers between devices, swapped(): return lax.ppermute(array, 'c', [(0, 1), (1, 0)])  10 us
    pallas_call x3, Pallas kernels, call(): pl.pallas_call(kernel, out_shape=[jax.ShapeDtypeStruct(*o) for o in outs]...  8.8 us
    all_to_all x2, waiting for transfers between devices, exchanged(): return lax.all_to_all(message, axis, 0, 0, tiled=True)  6.99 us
    ppermute x4, starting transfers between devices, across(): return lax.ppermute(array, 'z', [(k, k ^ bit) for k in range(LINE_Z)])  6.02 us
  transfers between devices with their start and end apart: 30, of which 10 were waited for; matrix products, arithmetic and copies ran while one was open for 7% of the time, Pallas kernels for 0%

profile of v5, /device:TPU:1, one launch (start us, length us, event | category | flops | bytes accessed | tf_op | source)
XLA Modules:
  0.0 136.5 jit_solution(14287042059228377864)
XLA Ops:
  0.6 2.6 %broadcast_in_dim.2 = bf16[16,64,1024]{2,1,0:T(8,128)(2,1)} broadcast(bf16[64,1024]{1,0:T(8,128)(2,1)} %own_text.1), dimensions={1,2} | broadcast | bytes 2228224 | tf_op jit(solution)/shard_map/broadcast_in_dim | solution.py:181
  3.2 7.7 %all-to-all-start = ((bf16[16,64,1024]{2,1,0:T(8,128)(2,1)}), bf16[16,64,1024]{2,1,0:T(8,128)(2,1)S(1)}, u32[]{:S(2)}, u32[]{:S(2)}) async-start(bf16[16,64,1024]{2,1,0:T(8,128)(2,1)} %broadcast_in_dim.2), calls=%async_computation | async-start | bytes 4194304 | tf_op jit(solution)/shard_map/all_to_all | solution.py:31
  12.0 3.0 %collective-permute-start.6 = (bf16[64,1024]{1,0:T(8,128)(2,1)S(1)}, bf16[64,1024]{1,0:T(8,128)(2,1)S(1)}, u32[]{:S(2)}, u32[]{:S(2)}) collective-permute-start(bf16[64,1024]{1,0:T(8,128)(2,1)S(1)} %constant_dynamic-slice_fusion.refs_0_), channel_id=1, source_target_pairs={{0,8},{4,12},{8,16},{12,20},{16,24},{20,28},{24,0},{28,4},{1,9},{5... | collective-permute-start | bytes 393224 | tf_op jit(solution)/shard_map/ppermute | solution.py:35
  15.0 1.6 %collective-permute-start.4 = (bf16[64,1024]{1,0:T(8,128)(2,1)S(1)}, bf16[64,1024]{1,0:T(8,128)(2,1)S(1)}, u32[]{:S(2)}, u32[]{:S(2)}) collective-permute-start(bf16[64,1024]{1,0:T(8,128)(2,1)S(1)} %constant_dynamic-slice_fusion.refs_0_), channel_id=1, source_target_pairs={{0,4},{4,8},{8,12},{12,16},{16,20},{20,24},{24,28},{28,0},{1,5},{5... | collective-permute-start | bytes 393224 | tf_op jit(solution)/shard_map/ppermute | solution.py:35
  16.6 4.2 %collective-permute-start.3 = (bf16[64,1024]{1,0:T(8,128)(2,1)S(1)}, bf16[64,1024]{1,0:T(8,128)(2,1)S(1)}, u32[]{:S(2)}, u32[]{:S(2)}) collective-permute-start(bf16[64,1024]{1,0:T(8,128)(2,1)S(1)} %constant_dynamic-slice_fusion.refs_0_), channel_id=1, source_target_pairs={{0,16},{4,20},{8,24},{12,28},{16,0},{20,4},{24,8},{28,12},{1,17},{... | collective-permute-start | bytes 393224 | tf_op jit(solution)/shard_map/ppermute | solution.py:35
  20.8 1.9 %collective-permute-start = (bf16[64,1024]{1,0:T(8,128)(2,1)S(1)}, bf16[64,1024]{1,0:T(8,128)(2,1)S(1)}, u32[]{:S(2)}, u32[]{:S(2)}) collective-permute-start(bf16[64,1024]{1,0:T(8,128)(2,1)S(1)} %constant_dynamic-slice_fusion.refs_0_), channel_id=1, source_target_pairs={{0,28},{4,0},{8,4},{12,8},{16,12},{20,16},{24,20},{28,24},{1,29},{... | collective-permute-start | bytes 393224 | tf_op jit(solution)/shard_map/ppermute | solution.py:35
  22.8 1.2 collective-permute-start.1
  24.0 1.5 %collective-permute-start.13 = (bf16[64,1024]{1,0:T(8,128)(2,1)S(1)}, bf16[64,1024]{1,0:T(8,128)(2,1)S(1)}, u32[]{:S(2)}, u32[]{:S(2)}) collective-permute-start(bf16[64,1024]{1,0:T(8,128)(2,1)S(1)} %collective-permute-done.6.refs_6_), channel_id=1, source_target_pairs={{0,2},{2,0},{1,3},{3,1},{4,6},{6,4},{5,7},{7,5},{8,10},{10,8},{9,1... | collective-permute-start | bytes 393224 | tf_op jit(solution)/shard_map/ppermute | solution.py:43
  25.5 1.5 %collective-permute-done.4.refs_7_ = bf16[64,1024]{1,0:T(8,128)(2,1)S(1)} collective-permute-done((bf16[64,1024]{1,0:T(8,128)(2,1)S(1)}, bf16[64,1024]{1,0:T(8,128)(2,1)S(1)}, u32[]{:S(2)}, u32[]{:S(2)}) %collective-permute-start.4) | collective-permute-done | bytes 131104 | tf_op jit(solution)/shard_map/ppermute | solution.py:35
  27.6 4.4 %collective-permute-done.3.refs_4_ = bf16[64,1024]{1,0:T(8,128)(2,1)S(1)} collective-permute-done((bf16[64,1024]{1,0:T(8,128)(2,1)S(1)}, bf16[64,1024]{1,0:T(8,128)(2,1)S(1)}, u32[]{:S(2)}, u32[]{:S(2)}) %collective-permute-start.3) | collective-permute-done | bytes 131104 | tf_op jit(solution)/shard_map/ppermute | solution.py:35
  32.1 4.6 %collective-permute-start.5 = (bf16[64,1024]{1,0:T(8,128)(2,1)S(1)}, bf16[64,1024]{1,0:T(8,128)(2,1)}, u32[]{:S(2)}, u32[]{:S(2)}) collective-permute-start(bf16[64,1024]{1,0:T(8,128)(2,1)S(1)} %collective-permute-done.4.refs_7_), channel_id=1, source_target_pairs={{0,8},{4,12},{8,16},{12,20},{16,24},{20,28},{24,0},{28,4},{1,9},{5... | collective-permute-start | bytes 393224 | tf_op jit(solution)/shard_map/ppermute | solution.py:35
  40.4 1.5 %collective-permute-start.12 = (bf16[64,1024]{1,0:T(8,128)(2,1)}, bf16[64,1024]{1,0:T(8,128)(2,1)}, u32[]{:S(2)}, u32[]{:S(2)}) collective-permute-start(bf16[64,1024]{1,0:T(8,128)(2,1)} %collective-permute-done.5.refs_5_), channel_id=1, source_target_pairs={{0,2},{2,0},{1,3},{3,1},{4,6},{6,4},{5,7},{7,5},{8,10},{10,8},{9,1... | collective-permute-start | bytes 393224 | tf_op jit(solution)/shard_map/ppermute | solution.py:43
  42.0 1.9 %collective-permute-start.10 = (bf16[64,1024]{1,0:T(8,128)(2,1)}, bf16[64,1024]{1,0:T(8,128)(2,1)}, u32[]{:S(2)}, u32[]{:S(2)}) collective-permute-start(bf16[64,1024]{1,0:T(8,128)(2,1)} %collective-permute-done.2.refs_3_), channel_id=1, source_target_pairs={{0,2},{2,0},{1,3},{3,1},{4,6},{6,4},{5,7},{7,5},{8,10},{10,8},{9,1... | collective-permute-start | bytes 393224 | tf_op jit(solution)/shard_map/ppermute | solution.py:43
  46.2 4.8 %shard_map.58 = (f32[1024,1024]{1,0:T(8,128)S(1)}, bf16[1024,1024]{1,0:T(8,128)(2,1)S(1)}, f32[16,8,128]{2,1,0:T(8,128)S(1)}, f32[8,128]{1,0:T(8,128)S(1)}, f32[8,128]{1,0:T(8,128)S(1)}) custom-call(s32[3]{0:T(128)S(1)} %pad_add_fusion.pos, f32[1]{0:T(128)S(6)} %copy.6.scale, bf16[64,1024]{1,0:T(8,128)(2,1)S(1)} %copy-done.3, ...), custom_call_target="tpu_custom_call" | custom-call | tf_op jit(solution)/shard_map/pallas_call | solution.py:162
  50.9 13.5 %all_to_all.20.heard = f32[16,8,128]{2,1,0:T(8,128)S(1)} all-to-all(f32[16,8,128]{2,1,0:T(8,128)S(1)} %get-tuple-element.16), channel_id=1, replica_groups=mesh['xh'=2,'y'=4,'z'=8,'c'=2,'xl'=2] {'z','c'}, dimensions={0} | all-to-all | bytes 131072 | tf_op jit(solution)/shard_map/all_to_all | solution.py:31
  65.1 12.8 %all_to_all.21.heard = f32[16,16,128]{2,1,0:T(8,128)S(1)} all-to-all(f32[16,16,128]{2,1,0:T(8,128)S(1)} %get-tuple-element.20), channel_id=1, replica_groups=mesh['xh'=2,'y'=4,'z'=8,'c'=2,'xl'=2] {'xh','y','xl'}, dimensions={0} | all-to-all | bytes 262144 | tf_op jit(solution)/shard_map/all_to_all | solution.py:31
  78.0 3.3 %shard_map.60 = (bf16[1024,1024]{1,0:T(8,128)(2,1)S(1)}, f32[512,1024]{1,0:T(8,128)S(1)}, f32[512,1024]{1,0:T(8,128)}, f32[8,128]{1,0:T(8,128)S(1)}, f32[8,128]{1,0:T(8,128)S(1)}) custom-call(s32[3]{0:T(128)S(1)} %pad_add_fusion.pos, f32[1024,1024]{1,0:T(8,128)S(1)} %get-tuple-element.15.scores, f32[16,128]{1,0:T(8,128)S(1)} %get-tuple-element.19.row_lse, ...), custom_call_target="tpu_custom_call" | custom-call | tf_op jit(solution)/shard_map/pallas_call | solution.py:162
  81.3 1.6 %collective-permute-start.20 = (f32[512,1024]{1,0:T(8,128)}, f32[512,1024]{1,0:T(8,128)}, u32[]{:S(2)}, u32[]{:S(2)}) collective-permute-start(f32[512,1024]{1,0:T(8,128)} %get-tuple-element.24), channel_id=1, source_target_pairs={{0,2},{2,0},{1,3},{3,1},{4,6},{6,4},{5,7},{7,5},{8,10},{10,8},{9,1... | collective-permute-start | bytes 6291464 | tf_op jit(solution)/shard_map/ppermute | solution.py:43
  83.0 3.8 %multiply_convert_fusion = f16[1024,1024]{1,0:T(8,128)(2,1)} fusion(bf16[1024,1024]{1,0:T(8,128)(2,1)S(1)} %get-tuple-element.25, bf16[1024,1024]{1,0:T(8,128)(2,1)S(1)} %get-tuple-element.26), kind=kOutput, calls=%fused_computation | convolution fusion | flops 2149580800 | bytes 6291456 | tf_op jit(solution)/shard_map/dot_general | solution.py:234
  86.7 4.6 %all-to-all-start.3 = ((f16[16,64,1024]{2,1,0:T(8,128)(2,1)}), f16[16,64,1024]{2,1,0:T(8,128)(2,1)}, u32[]{:S(2)}, u32[]{:S(2)}) async-start(f16[16,64,1024]{2,1,0:T(8,128)(2,1)} %bitcast.18), calls=%async_computation.3 | async-start | bytes 4194304 | tf_op jit(solution)/shard_map/all_to_all | solution.py:31
  92.9 2.1 %collective-permute-done.16 = f32[8,128]{1,0:T(8,128)S(1)} collective-permute-done((f32[8,128]{1,0:T(8,128)S(1)}, f32[8,128]{1,0:T(8,128)S(1)}, u32[]{:S(2)}, u32[]{:S(2)}) %collective-permute-start.16) | collective-permute-done | bytes 4128 | tf_op jit(solution)/shard_map/ppermute | solution.py:39
  96.2 4.5 %collective-permute-start.17 = (f32[8,128]{1,0:T(8,128)S(1)}, f32[8,128]{1,0:T(8,128)S(1)}, u32[]{:S(2)}, u32[]{:S(2)}) collective-permute-start(f32[8,128]{1,0:T(8,128)S(1)} %add.126), channel_id=1, source_target_pairs={{0,16},{4,20},{8,24},{12,28},{16,0},{20,4},{24,8},{28,12},{1,17},{... | collective-permute-start | bytes 12296 | tf_op jit(solution)/shard_map/ppermute | solution.py:39
  100.7 1.8 %collective-permute-done.17 = f32[8,128]{1,0:T(8,128)S(1)} collective-permute-done((f32[8,128]{1,0:T(8,128)S(1)}, f32[8,128]{1,0:T(8,128)S(1)}, u32[]{:S(2)}, u32[]{:S(2)}) %collective-permute-start.17) | collective-permute-done | bytes 4128 | tf_op jit(solution)/shard_map/ppermute | solution.py:39
  103.1 1.9 %fusion.1 = (f16[64,1024]{1,0:T(8,128)(2,1)S(1)}, f16[64,1024]{1,0:T(8,128)(2,1)S(1)}, f16[64,1024]{1,0:T(8,128)(2,1)S(1)}, f16[64,1024]{1,0:T(8,128)(2,1)S(1)},...) fusion(f32[512,1024]{1,0:T(8,128)} %collective-permute-done.20, ...), kind=kLoop, calls=%fused_computation.4 | loop fusion | flops 917504 | bytes 4587520 | tf_op jit(solution)/shard_map/convert_element_type | solution.py:242
  104.9 3.0 %collective-permute-start.25 = (f16[64,1024]{1,0:T(8,128)(2,1)S(1)}, f16[64,1024]{1,0:T(8,128)(2,1)S(1)}, u32[]{:S(2)}, u32[]{:S(2)}) collective-permute-start(f16[64,1024]{1,0:T(8,128)(2,1)S(1)} %get-tuple-element.29), channel_id=1, source_target_pairs={{0,24},{4,28},{8,0},{12,4},{16,8},{20,12},{24,16},{28,20},{1,25},{... | collective-permute-start | bytes 393224 | tf_op jit(solution)/shard_map/ppermute | solution.py:35
  108.0 3.1 %collective-permute-start.23 = (f16[64,1024]{1,0:T(8,128)(2,1)S(1)}, f16[64,1024]{1,0:T(8,128)(2,1)}, u32[]{:S(2)}, u32[]{:S(2)}) collective-permute-start(f16[64,1024]{1,0:T(8,128)(2,1)S(1)} %get-tuple-element.31), channel_id=1, source_target_pairs={{0,20},{4,24},{8,28},{12,0},{16,4},{20,8},{24,12},{28,16},{1,21},{... | collective-permute-start | bytes 393224 | tf_op jit(solution)/shard_map/ppermute | solution.py:35
  111.2 4.0 %collective-permute-start.21 = (f16[64,1024]{1,0:T(8,128)(2,1)S(1)}, f16[64,1024]{1,0:T(8,128)(2,1)}, u32[]{:S(2)}, u32[]{:S(2)}) collective-permute-start(f16[64,1024]{1,0:T(8,128)(2,1)S(1)} %get-tuple-element.33), channel_id=1, source_target_pairs={{0,16},{4,20},{8,24},{12,28},{16,0},{20,4},{24,8},{28,12},{1,17},{... | collective-permute-start | bytes 393224 | tf_op jit(solution)/shard_map/ppermute | solution.py:35
  115.3 7.0 %all-to-all-done.3 = f16[16,64,1024]{2,1,0:T(8,128)(2,1)} async-done(((f16[16,64,1024]{2,1,0:T(8,128)(2,1)}), f16[16,64,1024]{2,1,0:T(8,128)(2,1)}, u32[]{:S(2)}, u32[]{:S(2)}) %all-to-all-start.3) | async-done | bytes 2097184 | tf_op jit(solution)/shard_map/all_to_all | solution.py:31
  122.3 2.7 %fusion.12 = f32[64,1024]{1,0:T(8,128)} fusion(f16[16,64,1024]{2,1,0:T(8,128)(2,1)} %all-to-all-done.3, f32[]{:T(128)} %bitcast.5), kind=kLoop, calls=%fused_computation.22 | loop fusion | flops 2097152 | bytes 2359300 | tf_op jit(solution)/shard_map/mul | solution.py:249
  125.4 2.3 %collective-permute-start.27 = (f16[64,1024]{1,0:T(8,128)(2,1)S(1)}, f16[64,1024]{1,0:T(8,128)(2,1)S(1)}, u32[]{:S(2)}, u32[]{:S(2)}) collective-permute-start(f16[64,1024]{1,0:T(8,128)(2,1)S(1)} %get-tuple-element.28), channel_id=1, source_target_pairs={{0,28},{4,0},{8,4},{12,8},{16,12},{20,16},{24,20},{28,24},{1,29},{... | collective-permute-start | bytes 393224 | tf_op jit(solution)/shard_map/ppermute | solution.py:35
  127.8 1.2 fusion.11
  129.0 6.7 %collective-permute-done.26 = f16[64,1024]{1,0:T(8,128)(2,1)S(1)} collective-permute-done((f16[64,1024]{1,0:T(8,128)(2,1)S(1)}, f16[64,1024]{1,0:T(8,128)(2,1)S(1)}, u32[]{:S(2)}, u32[]{:S(2)}) %collective-permute-start.26) | collective-permute-done | bytes 131104 | tf_op jit(solution)/shard_map/ppermute | solution.py:35
  (57 shorter events, 12.5 us)
Async XLA Ops:
  3.2 42.0 %copy-start.3 = (bf16[64,1024]{1,0:T(8,128)(2,1)S(1)}, bf16[64,1024]{1,0:T(8,128)(2,1)}, u32[]{:S(2)}) copy-start(bf16[64,1024]{1,0:T(8,128)(2,1)} %own_text.1) | copy-start | bytes 393220
  3.2 42.0 %all-to-all-start = ((bf16[16,64,1024]{2,1,0:T(8,128)(2,1)}), bf16[16,64,1024]{2,1,0:T(8,128)(2,1)S(1)}, u32[]{:S(2)}, u32[]{:S(2)}) async-start(bf16[16,64,1024]{2,1,0:T(8,128)(2,1)} %broadcast_in_dim.2), calls=%async_computation | async-start | bytes 4194304 | tf_op jit(solution)/shard_map/all_to_all | solution.py:31
  11.0 11.8 %collective-permute-start.7 = (bf16[64,1024]{1,0:T(8,128)(2,1)S(1)}, bf16[64,1024]{1,0:T(8,128)(2,1)S(1)}, u32[]{:S(2)}, u32[]{:S(2)}) collective-permute-start(bf16[64,1024]{1,0:T(8,128)(2,1)S(1)} %constant_dynamic-slice_fusion.refs_0_), channel_id=1, source_target_pairs={{0,2},{2,0},{1,3},{3,1},{4,6},{6,4},{5,7},{7,5},{8,10},{10,8},{9,1... | collective-permute-start | bytes 393224 | tf_op jit(solution)/shard_map/ppermute | solution.py:43
  12.0 12.0 %collective-permute-start.6 = (bf16[64,1024]{1,0:T(8,128)(2,1)S(1)}, bf16[64,1024]{1,0:T(8,128)(2,1)S(1)}, u32[]{:S(2)}, u32[]{:S(2)}) collective-permute-start(bf16[64,1024]{1,0:T(8,128)(2,1)S(1)} %constant_dynamic-slice_fusion.refs_0_), channel_id=1, source_target_pairs={{0,8},{4,12},{8,16},{12,20},{16,24},{20,28},{24,0},{28,4},{1,9},{5... | collective-permute-start | bytes 393224 | tf_op jit(solution)/shard_map/ppermute | solution.py:35
  15.0 12.0 %collective-permute-start.4 = (bf16[64,1024]{1,0:T(8,128)(2,1)S(1)}, bf16[64,1024]{1,0:T(8,128)(2,1)S(1)}, u32[]{:S(2)}, u32[]{:S(2)}) collective-permute-start(bf16[64,1024]{1,0:T(8,128)(2,1)S(1)} %constant_dynamic-slice_fusion.refs_0_), channel_id=1, source_target_pairs={{0,4},{4,8},{8,12},{12,16},{16,20},{20,24},{24,28},{28,0},{1,5},{5... | collective-permute-start | bytes 393224 | tf_op jit(solution)/shard_map/ppermute | solution.py:35
  16.6 15.4 %collective-permute-start.3 = (bf16[64,1024]{1,0:T(8,128)(2,1)S(1)}, bf16[64,1024]{1,0:T(8,128)(2,1)S(1)}, u32[]{:S(2)}, u32[]{:S(2)}) collective-permute-start(bf16[64,1024]{1,0:T(8,128)(2,1)S(1)} %constant_dynamic-slice_fusion.refs_0_), channel_id=1, source_target_pairs={{0,16},{4,20},{8,24},{12,28},{16,0},{20,4},{24,8},{28,12},{1,17},{... | collective-permute-start | bytes 393224 | tf_op jit(solution)/shard_map/ppermute | solution.py:35
  20.8 15.8 %collective-permute-start = (bf16[64,1024]{1,0:T(8,128)(2,1)S(1)}, bf16[64,1024]{1,0:T(8,128)(2,1)S(1)}, u32[]{:S(2)}, u32[]{:S(2)}) collective-permute-start(bf16[64,1024]{1,0:T(8,128)(2,1)S(1)} %constant_dynamic-slice_fusion.refs_0_), channel_id=1, source_target_pairs={{0,28},{4,0},{8,4},{12,8},{16,12},{20,16},{24,20},{28,24},{1,29},{... | collective-permute-start | bytes 393224 | tf_op jit(solution)/shard_map/ppermute | solution.py:35
  22.8 14.6 %collective-permute-start.1 = (bf16[64,1024]{1,0:T(8,128)(2,1)S(1)}, bf16[64,1024]{1,0:T(8,128)(2,1)S(1)}, u32[]{:S(2)}, u32[]{:S(2)}) collective-permute-start(bf16[64,1024]{1,0:T(8,128)(2,1)S(1)} %constant_dynamic-slice_fusion.refs_0_), channel_id=1, source_target_pairs={{0,24},{4,28},{8,0},{12,4},{16,8},{20,12},{24,16},{28,20},{1,25},{... | collective-permute-start | bytes 393224 | tf_op jit(solution)/shard_map/ppermute | solution.py:35
  24.0 14.6 %collective-permute-start.13 = (bf16[64,1024]{1,0:T(8,128)(2,1)S(1)}, bf16[64,1024]{1,0:T(8,128)(2,1)S(1)}, u32[]{:S(2)}, u32[]{:S(2)}) collective-permute-start(bf16[64,1024]{1,0:T(8,128)(2,1)S(1)} %collective-permute-done.6.refs_6_), channel_id=1, source_target_pairs={{0,2},{2,0},{1,3},{3,1},{4,6},{6,4},{5,7},{7,5},{8,10},{10,8},{9,1... | collective-permute-start | bytes 393224 | tf_op jit(solution)/shard_map/ppermute | solution.py:43
  27.0 11.6 %collective-permute-start.14 = (bf16[64,1024]{1,0:T(8,128)(2,1)S(1)}, bf16[64,1024]{1,0:T(8,128)(2,1)S(1)}, u32[]{:S(2)}, u32[]{:S(2)}) collective-permute-start(bf16[64,1024]{1,0:T(8,128)(2,1)S(1)} %collective-permute-done.4.refs_7_), channel_id=1, source_target_pairs={{0,2},{2,0},{1,3},{3,1},{4,6},{6,4},{5,7},{7,5},{8,10},{10,8},{9,1... | collective-permute-start | bytes 393224 | tf_op jit(solution)/shard_map/ppermute | solution.py:43
  32.1 8.3 %collective-permute-start.5 = (bf16[64,1024]{1,0:T(8,128)(2,1)S(1)}, bf16[64,1024]{1,0:T(8,128)(2,1)}, u32[]{:S(2)}, u32[]{:S(2)}) collective-permute-start(bf16[64,1024]{1,0:T(8,128)(2,1)S(1)} %collective-permute-done.4.refs_7_), channel_id=1, source_target_pairs={{0,8},{4,12},{8,16},{12,20},{16,24},{20,28},{24,0},{28,4},{1,9},{5... | collective-permute-start | bytes 393224 | tf_op jit(solution)/shard_map/ppermute | solution.py:35
  36.7 5.3 %collective-permute-start.2 = (bf16[64,1024]{1,0:T(8,128)(2,1)S(1)}, bf16[64,1024]{1,0:T(8,128)(2,1)}, u32[]{:S(2)}, u32[]{:S(2)}) collective-permute-start(bf16[64,1024]{1,0:T(8,128)(2,1)S(1)} %collective-permute-done.refs_1_), channel_id=1, source_target_pairs={{0,24},{4,28},{8,0},{12,4},{16,8},{20,12},{24,16},{28,20},{1,25},{... | collective-permute-start | bytes 393224 | tf_op jit(solution)/shard_map/ppermute | solution.py:35
  37.3 7.3 %collective-permute-start.8 = (bf16[64,1024]{1,0:T(8,128)(2,1)S(1)}, bf16[64,1024]{1,0:T(8,128)(2,1)}, u32[]{:S(2)}, u32[]{:S(2)}) collective-permute-start(bf16[64,1024]{1,0:T(8,128)(2,1)S(1)} %collective-permute-done.refs_1_), channel_id=1, source_target_pairs={{0,2},{2,0},{1,3},{3,1},{4,6},{6,4},{5,7},{7,5},{8,10},{10,8},{9,1... | collective-permute-start | bytes 393224 | tf_op jit(solution)/shard_map/ppermute | solution.py:43
  38.5 6.1 %collective-permute-start.11 = (bf16[64,1024]{1,0:T(8,128)(2,1)S(1)}, bf16[64,1024]{1,0:T(8,128)(2,1)}, u32[]{:S(2)}, u32[]{:S(2)}) collective-permute-start(bf16[64,1024]{1,0:T(8,128)(2,1)S(1)} %collective-permute-done.3.refs_4_), channel_id=1, source_target_pairs={{0,2},{2,0},{1,3},{3,1},{4,6},{6,4},{5,7},{7,5},{8,10},{10,8},{9,1... | collective-permute-start | bytes 393224 | tf_op jit(solution)/shard_map/ppermute | solution.py:43
  39.3 5.4 %collective-permute-start.9 = (bf16[64,1024]{1,0:T(8,128)(2,1)S(1)}, bf16[64,1024]{1,0:T(8,128)(2,1)}, u32[]{:S(2)}, u32[]{:S(2)}) collective-permute-start(bf16[64,1024]{1,0:T(8,128)(2,1)S(1)} %collective-permute-done.1.refs_2_), channel_id=1, source_target_pairs={{0,2},{2,0},{1,3},{3,1},{4,6},{6,4},{5,7},{7,5},{8,10},{10,8},{9,1... | collective-permute-start | bytes 393224 | tf_op jit(solution)/shard_map/ppermute | solution.py:43
  40.4 4.2 %collective-permute-start.12 = (bf16[64,1024]{1,0:T(8,128)(2,1)}, bf16[64,1024]{1,0:T(8,128)(2,1)}, u32[]{:S(2)}, u32[]{:S(2)}) collective-permute-start(bf16[64,1024]{1,0:T(8,128)(2,1)} %collective-permute-done.5.refs_5_), channel_id=1, source_target_pairs={{0,2},{2,0},{1,3},{3,1},{4,6},{6,4},{5,7},{7,5},{8,10},{10,8},{9,1... | collective-permute-start | bytes 393224 | tf_op jit(solution)/shard_map/ppermute | solution.py:43
  42.0 3.3 %collective-permute-start.10 = (bf16[64,1024]{1,0:T(8,128)(2,1)}, bf16[64,1024]{1,0:T(8,128)(2,1)}, u32[]{:S(2)}, u32[]{:S(2)}) collective-permute-start(bf16[64,1024]{1,0:T(8,128)(2,1)} %collective-permute-done.2.refs_3_), channel_id=1, source_target_pairs={{0,2},{2,0},{1,3},{3,1},{4,6},{6,4},{5,7},{7,5},{8,10},{10,8},{9,1... | collective-permute-start | bytes 393224 | tf_op jit(solution)/shard_map/ppermute | solution.py:43
  81.3 21.7 %collective-permute-start.20 = (f32[512,1024]{1,0:T(8,128)}, f32[512,1024]{1,0:T(8,128)}, u32[]{:S(2)}, u32[]{:S(2)}) collective-permute-start(f32[512,1024]{1,0:T(8,128)} %get-tuple-element.24), channel_id=1, source_target_pairs={{0,2},{2,0},{1,3},{3,1},{4,6},{6,4},{5,7},{7,5},{8,10},{10,8},{9,1... | collective-permute-start | bytes 6291464 | tf_op jit(solution)/shard_map/ppermute | solution.py:43
  86.7 16.4 %copy-start.2 = (f32[512,1024]{1,0:T(8,128)S(1)}, f32[512,1024]{1,0:T(8,128)}, u32[]{:S(2)}) copy-start(f32[512,1024]{1,0:T(8,128)} %copy-done.1) | copy-start | bytes 6291460
  86.7 35.5 %all-to-all-start.3 = ((f16[16,64,1024]{2,1,0:T(8,128)(2,1)}), f16[16,64,1024]{2,1,0:T(8,128)(2,1)}, u32[]{:S(2)}, u32[]{:S(2)}) async-start(f16[16,64,1024]{2,1,0:T(8,128)(2,1)} %bitcast.18), calls=%async_computation.3 | async-start | bytes 4194304 | tf_op jit(solution)/shard_map/all_to_all | solution.py:31
  91.3 1.3 collective-permute-start.15
  92.6 2.5 %collective-permute-start.16 = (f32[8,128]{1,0:T(8,128)S(1)}, f32[8,128]{1,0:T(8,128)S(1)}, u32[]{:S(2)}, u32[]{:S(2)}) collective-permute-start(f32[8,128]{1,0:T(8,128)S(1)} %add.125), channel_id=1, source_target_pairs={{0,4},{4,0},{8,12},{12,8},{16,20},{20,16},{24,28},{28,24},{1,5},{5... | collective-permute-start | bytes 12296 | tf_op jit(solution)/shard_map/ppermute | solution.py:39
  95.0 5.7 %collective-permute-start.19 = (f32[8,128]{1,0:T(8,128)S(1)}, f32[8,128]{1,0:T(8,128)S(1)}, u32[]{:S(2)}, u32[]{:S(2)}) collective-permute-start(f32[8,128]{1,0:T(8,128)S(1)} %add.126), channel_id=1, source_target_pairs={{0,24},{4,28},{8,16},{12,20},{16,8},{20,12},{24,0},{28,4},{1,25},{... | collective-permute-start | bytes 12296 | tf_op jit(solution)/shard_map/ppermute | solution.py:39
  95.6 5.1 %collective-permute-start.18 = (f32[8,128]{1,0:T(8,128)S(1)}, f32[8,128]{1,0:T(8,128)S(1)}, u32[]{:S(2)}, u32[]{:S(2)}) collective-permute-start(f32[8,128]{1,0:T(8,128)S(1)} %add.126), channel_id=1, source_target_pairs={{0,8},{4,12},{8,0},{12,4},{16,24},{20,28},{24,16},{28,20},{1,9},{5... | collective-permute-start | bytes 12296 | tf_op jit(solution)/shard_map/ppermute | solution.py:39
  96.2 6.4 %collective-permute-start.17 = (f32[8,128]{1,0:T(8,128)S(1)}, f32[8,128]{1,0:T(8,128)S(1)}, u32[]{:S(2)}, u32[]{:S(2)}) collective-permute-start(f32[8,128]{1,0:T(8,128)S(1)} %add.126), channel_id=1, source_target_pairs={{0,16},{4,20},{8,24},{12,28},{16,0},{20,4},{24,8},{28,12},{1,17},{... | collective-permute-start | bytes 12296 | tf_op jit(solution)/shard_map/ppermute | solution.py:39
  104.9 20.0 %collective-permute-start.25 = (f16[64,1024]{1,0:T(8,128)(2,1)S(1)}, f16[64,1024]{1,0:T(8,128)(2,1)S(1)}, u32[]{:S(2)}, u32[]{:S(2)}) collective-permute-start(f16[64,1024]{1,0:T(8,128)(2,1)S(1)} %get-tuple-element.29), channel_id=1, source_target_pairs={{0,24},{4,28},{8,0},{12,4},{16,8},{20,12},{24,16},{28,20},{1,25},{... | collective-permute-start | bytes 393224 | tf_op jit(solution)/shard_map/ppermute | solution.py:35
  108.0 17.5 %collective-permute-start.24 = (f16[64,1024]{1,0:T(8,128)(2,1)S(1)}, f16[64,1024]{1,0:T(8,128)(2,1)S(1)}, u32[]{:S(2)}, u32[]{:S(2)}) collective-permute-start(f16[64,1024]{1,0:T(8,128)(2,1)S(1)} %get-tuple-element.30), channel_id=1, source_target_pairs={{0,8},{4,12},{8,16},{12,20},{16,24},{20,28},{24,0},{28,4},{1,9},{5... | collective-permute-start | bytes 393224 | tf_op jit(solution)/shard_map/ppermute | solution.py:35
  108.0 19.8 %collective-permute-start.23 = (f16[64,1024]{1,0:T(8,128)(2,1)S(1)}, f16[64,1024]{1,0:T(8,128)(2,1)}, u32[]{:S(2)}, u32[]{:S(2)}) collective-permute-start(f16[64,1024]{1,0:T(8,128)(2,1)S(1)} %get-tuple-element.31), channel_id=1, source_target_pairs={{0,20},{4,24},{8,28},{12,0},{16,4},{20,8},{24,12},{28,16},{1,21},{... | collective-permute-start | bytes 393224 | tf_op jit(solution)/shard_map/ppermute | solution.py:35
  111.1 16.7 %collective-permute-start.22 = (f16[64,1024]{1,0:T(8,128)(2,1)S(1)}, f16[64,1024]{1,0:T(8,128)(2,1)}, u32[]{:S(2)}, u32[]{:S(2)}) collective-permute-start(f16[64,1024]{1,0:T(8,128)(2,1)S(1)} %get-tuple-element.32), channel_id=1, source_target_pairs={{0,12},{4,16},{8,20},{12,24},{16,28},{20,0},{24,4},{28,8},{1,13},{... | collective-permute-start | bytes 393224 | tf_op jit(solution)/shard_map/ppermute | solution.py:35
  111.2 16.5 %collective-permute-start.21 = (f16[64,1024]{1,0:T(8,128)(2,1)S(1)}, f16[64,1024]{1,0:T(8,128)(2,1)}, u32[]{:S(2)}, u32[]{:S(2)}) collective-permute-start(f16[64,1024]{1,0:T(8,128)(2,1)S(1)} %get-tuple-element.33), channel_id=1, source_target_pairs={{0,16},{4,20},{8,24},{12,28},{16,0},{20,4},{24,8},{28,12},{1,17},{... | collective-permute-start | bytes 393224 | tf_op jit(solution)/shard_map/ppermute | solution.py:35
  125.0 10.8 %collective-permute-start.26 = (f16[64,1024]{1,0:T(8,128)(2,1)S(1)}, f16[64,1024]{1,0:T(8,128)(2,1)S(1)}, u32[]{:S(2)}, u32[]{:S(2)}) collective-permute-start(f16[64,1024]{1,0:T(8,128)(2,1)S(1)} %get-tuple-element.27), channel_id=1, source_target_pairs={{0,4},{4,8},{8,12},{12,16},{16,20},{20,24},{24,28},{28,0},{1,5},{5... | collective-permute-start | bytes 393224 | tf_op jit(solution)/shard_map/ppermute | solution.py:35
  125.4 10.3 %collective-permute-start.27 = (f16[64,1024]{1,0:T(8,128)(2,1)S(1)}, f16[64,1024]{1,0:T(8,128)(2,1)S(1)}, u32[]{:S(2)}, u32[]{:S(2)}) collective-permute-start(f16[64,1024]{1,0:T(8,128)(2,1)S(1)} %get-tuple-element.28), channel_id=1, source_target_pairs={{0,28},{4,0},{8,4},{12,8},{16,12},{20,16},{24,20},{28,24},{1,29},{... | collective-permute-start | bytes 393224 | tf_op jit(solution)/shard_map/ppermute | solution.py:35
  (4 other events, 17.3 us)

commit v6 on v5

--- a/solution.py
+++ b/solution.py
@@ -181,10 +181,8 @@
         jnp.broadcast_to(text_embed[None], (PLANE_N, ROWS, width)), PLANE
     ).reshape(BLOCK, width)
     near = [own_image] + [None] * (LINE_Z - 1)
-    for k, by in ((1, -1), (7, 1), (2, -2), (6, 2), (4, 4)):
-        near[k] = shifted(own_image, by)
-    near[3] = shifted(near[1], -2)
-    near[5] = shifted(near[7], 2)
+    for k in FAR_FIRST:
+        near[k] = shifted(own_image, -k)
     far = []
     for block in near:
         far.append(swapped(block))

time: 137 us -> 143 us (1.044)
  waiting for transfers between devices: 26.2 us -> 30.6 us
  local copies, waits for them, and re-layouts: 4.67 us -> 6.24 us
    ppermute x14, waiting for transfers between devices: 13.5 us -> 17.9 us  [shifted(): lax.ppermute(array, 'z', [(k, (k + by) % LINE_Z) for k in range(LINE_Z)])]
    unnamed x12 -> x16, local copies, waits for them, and re-layouts: 1.58 us -> 3.14 us
  transfers between devices with their start and end apart: 30 -> 30, of which waited for: 10 -> 8; matrix products, arithmetic and copies ran while one was open for 7% -> 7% of each run, Pallas kernels for 0% -> 0%
where the time goes in v6:
time: 143 us
  starting transfers between devices  58.2 us (41%)
  waiting for transfers between devices  30.6 us (21%)
  blocking collectives  26.8 us (19%)
  Pallas kernels  8.78 us (6%)
  other arithmetic  6.68 us (5%)
  local copies, waits for them, and re-layouts  6.24 us (4%)
  matrix products  3.78 us (3%)
    ppermute x14, starting transfers between devices, shifted(): lax.ppermute(array, 'z', [(k, (k + by) % LINE_Z) for k in range(LINE_Z)])  30.5 us
    all_to_all x2, blocking collectives, exchanged(): return lax.all_to_all(message, axis, 0, 0, tiled=True)  26.8 us
    ppermute x14, waiting for transfers between devices, shifted(): lax.ppermute(array, 'z', [(k, (k + by) % LINE_Z) for k in range(LINE_Z)])  17.9 us
    all_to_all x2, starting transfers between devices, exchanged(): return lax.all_to_all(message, axis, 0, 0, tiled=True)  12.3 us
    ppermute x10, starting transfers between devices, swapped(): return lax.ppermute(array, 'c', [(0, 1), (1, 0)])  9.46 us
    pallas_call x3, Pallas kernels, call(): pl.pallas_call(kernel, out_shape=[jax.ShapeDtypeStruct(*o) for o in outs]...  8.78 us
    all_to_all x2, waiting for transfers between devices, exchanged(): return lax.all_to_all(message, axis, 0, 0, tiled=True)  6.99 us
    ppermute x4, starting transfers between devices, across(): return lax.ppermute(array, 'z', [(k, k ^ bit) for k in range(LINE_Z)])  6.01 us
  transfers between devices with their start and end apart: 30, of which 8 were waited for; matrix products, arithmetic and copies ran while one was open for 7% of the time, Pallas kernels for 0%

profile of v6, /device:TPU:1, one launch (start us, length us, event | category | flops | bytes accessed | tf_op | source)
XLA Modules:
  0.0 142.5 jit_solution(5329347999093620052)
XLA Ops:
  0.6 2.6 %broadcast_in_dim.2 = bf16[16,64,1024]{2,1,0:T(8,128)(2,1)} broadcast(bf16[64,1024]{1,0:T(8,128)(2,1)} %own_text.1), dimensions={1,2} | broadcast | bytes 2228224 | tf_op jit(solution)/shard_map/broadcast_in_dim | solution.py:181
  3.2 7.7 %all-to-all-start = ((bf16[16,64,1024]{2,1,0:T(8,128)(2,1)}), bf16[16,64,1024]{2,1,0:T(8,128)(2,1)S(1)}, u32[]{:S(2)}, u32[]{:S(2)}) async-start(bf16[16,64,1024]{2,1,0:T(8,128)(2,1)} %broadcast_in_dim.2), calls=%async_computation | async-start | bytes 4194304 | tf_op jit(solution)/shard_map/all_to_all | solution.py:31
  12.0 1.6 %collective-permute-start.6 = (bf16[64,1024]{1,0:T(8,128)(2,1)S(1)}, bf16[64,1024]{1,0:T(8,128)(2,1)S(1)}, u32[]{:S(2)}, u32[]{:S(2)}) collective-permute-start(bf16[64,1024]{1,0:T(8,128)(2,1)S(1)} %constant_dynamic-slice_fusion.refs_0_), channel_id=1, source_target_pairs={{0,4},{4,8},{8,12},{12,16},{16,20},{20,24},{24,28},{28,0},{1,5},{5... | collective-permute-start | bytes 393224 | tf_op jit(solution)/shard_map/ppermute | solution.py:35
  13.6 3.0 %collective-permute-start.5 = (bf16[64,1024]{1,0:T(8,128)(2,1)S(1)}, bf16[64,1024]{1,0:T(8,128)(2,1)S(1)}, u32[]{:S(2)}, u32[]{:S(2)}) collective-permute-start(bf16[64,1024]{1,0:T(8,128)(2,1)S(1)} %constant_dynamic-slice_fusion.refs_0_), channel_id=1, source_target_pairs={{0,8},{4,12},{8,16},{12,20},{16,24},{20,28},{24,0},{28,4},{1,9},{5... | collective-permute-start | bytes 393224 | tf_op jit(solution)/shard_map/ppermute | solution.py:35
  16.6 3.8 %collective-permute-start.4 = (bf16[64,1024]{1,0:T(8,128)(2,1)S(1)}, bf16[64,1024]{1,0:T(8,128)(2,1)S(1)}, u32[]{:S(2)}, u32[]{:S(2)}) collective-permute-start(bf16[64,1024]{1,0:T(8,128)(2,1)S(1)} %constant_dynamic-slice_fusion.refs_0_), channel_id=1, source_target_pairs={{0,12},{4,16},{8,20},{12,24},{16,28},{20,0},{24,4},{28,8},{1,13},{... | collective-permute-start | bytes 393224 | tf_op jit(solution)/shard_map/ppermute | solution.py:35
  20.9 4.5 %collective-permute-start.2 = (bf16[64,1024]{1,0:T(8,128)(2,1)S(1)}, bf16[64,1024]{1,0:T(8,128)(2,1)S(1)}, u32[]{:S(2)}, u32[]{:S(2)}) collective-permute-start(bf16[64,1024]{1,0:T(8,128)(2,1)S(1)} %constant_dynamic-slice_fusion.refs_0_), channel_id=1, source_target_pairs={{0,20},{4,24},{8,28},{12,0},{16,4},{20,8},{24,12},{28,16},{1,21},{... | collective-permute-start | bytes 393224 | tf_op jit(solution)/shard_map/ppermute | solution.py:35
  25.3 2.4 %collective-permute-start.1 = (bf16[64,1024]{1,0:T(8,128)(2,1)S(1)}, bf16[64,1024]{1,0:T(8,128)(2,1)S(1)}, u32[]{:S(2)}, u32[]{:S(2)}) collective-permute-start(bf16[64,1024]{1,0:T(8,128)(2,1)S(1)} %constant_dynamic-slice_fusion.refs_0_), channel_id=1, source_target_pairs={{0,24},{4,28},{8,0},{12,4},{16,8},{20,12},{24,16},{28,20},{1,25},{... | collective-permute-start | bytes 393224 | tf_op jit(solution)/shard_map/ppermute | solution.py:35
  27.7 1.7 %collective-permute-start = (bf16[64,1024]{1,0:T(8,128)(2,1)S(1)}, bf16[64,1024]{1,0:T(8,128)(2,1)}, u32[]{:S(2)}, u32[]{:S(2)}) collective-permute-start(bf16[64,1024]{1,0:T(8,128)(2,1)S(1)} %constant_dynamic-slice_fusion.refs_0_), channel_id=1, source_target_pairs={{0,28},{4,0},{8,4},{12,8},{16,12},{20,16},{24,20},{28,24},{1,29},{... | collective-permute-start | bytes 393224 | tf_op jit(solution)/shard_map/ppermute | solution.py:35
  29.4 7.9 %collective-permute-done.4.refs_5_ = bf16[64,1024]{1,0:T(8,128)(2,1)S(1)} collective-permute-done((bf16[64,1024]{1,0:T(8,128)(2,1)S(1)}, bf16[64,1024]{1,0:T(8,128)(2,1)S(1)}, u32[]{:S(2)}, u32[]{:S(2)}) %collective-permute-start.4) | collective-permute-done | bytes 131104 | tf_op jit(solution)/shard_map/ppermute | solution.py:35
  37.3 2.1 %collective-permute-start.14 = (bf16[64,1024]{1,0:T(8,128)(2,1)S(1)}, bf16[64,1024]{1,0:T(8,128)(2,1)S(1)}, u32[]{:S(2)}, u32[]{:S(2)}) collective-permute-start(bf16[64,1024]{1,0:T(8,128)(2,1)S(1)} %collective-permute-done.6.refs_7_), channel_id=1, source_target_pairs={{0,2},{2,0},{1,3},{3,1},{4,6},{6,4},{5,7},{7,5},{8,10},{10,8},{9,1... | collective-permute-start | bytes 393224 | tf_op jit(solution)/shard_map/ppermute | solution.py:43
  39.4 3.1 %collective-permute-start.12 = (bf16[64,1024]{1,0:T(8,128)(2,1)S(1)}, bf16[64,1024]{1,0:T(8,128)(2,1)}, u32[]{:S(2)}, u32[]{:S(2)}) collective-permute-start(bf16[64,1024]{1,0:T(8,128)(2,1)S(1)} %collective-permute-done.4.refs_5_), channel_id=1, source_target_pairs={{0,2},{2,0},{1,3},{3,1},{4,6},{6,4},{5,7},{7,5},{8,10},{10,8},{9,1... | collective-permute-start | bytes 393224 | tf_op jit(solution)/shard_map/ppermute | solution.py:43
  42.4 3.2 %collective-permute-done.1.refs_2_ = bf16[64,1024]{1,0:T(8,128)(2,1)S(1)} collective-permute-done((bf16[64,1024]{1,0:T(8,128)(2,1)S(1)}, bf16[64,1024]{1,0:T(8,128)(2,1)S(1)}, u32[]{:S(2)}, u32[]{:S(2)}) %collective-permute-start.1) | collective-permute-done | bytes 131104 | tf_op jit(solution)/shard_map/ppermute | solution.py:35
  51.7 4.7 %shard_map.58 = (f32[1024,1024]{1,0:T(8,128)S(1)}, bf16[1024,1024]{1,0:T(8,128)(2,1)S(1)}, f32[16,8,128]{2,1,0:T(8,128)S(1)}, f32[8,128]{1,0:T(8,128)S(1)}, f32[8,128]{1,0:T(8,128)S(1)}) custom-call(s32[3]{0:T(128)S(1)} %pad_add_fusion.pos, f32[1]{0:T(128)S(6)} %copy.6.scale, bf16[64,1024]{1,0:T(8,128)(2,1)S(1)} %copy-done.3, ...), custom_call_target="tpu_custom_call" | custom-call | tf_op jit(solution)/shard_map/pallas_call | solution.py:162
  56.4 13.2 %all_to_all.20.heard = f32[16,8,128]{2,1,0:T(8,128)S(1)} all-to-all(f32[16,8,128]{2,1,0:T(8,128)S(1)} %get-tuple-element.16), channel_id=1, replica_groups=mesh['xh'=2,'y'=4,'z'=8,'c'=2,'xl'=2] {'z','c'}, dimensions={0} | all-to-all | bytes 131072 | tf_op jit(solution)/shard_map/all_to_all | solution.py:31
  70.4 13.6 %all_to_all.21.heard = f32[16,16,128]{2,1,0:T(8,128)S(1)} all-to-all(f32[16,16,128]{2,1,0:T(8,128)S(1)} %get-tuple-element.20), channel_id=1, replica_groups=mesh['xh'=2,'y'=4,'z'=8,'c'=2,'xl'=2] {'xh','y','xl'}, dimensions={0} | all-to-all | bytes 262144 | tf_op jit(solution)/shard_map/all_to_all | solution.py:31
  84.0 3.3 %shard_map.60 = (bf16[1024,1024]{1,0:T(8,128)(2,1)S(1)}, f32[512,1024]{1,0:T(8,128)S(1)}, f32[512,1024]{1,0:T(8,128)}, f32[8,128]{1,0:T(8,128)S(1)}, f32[8,128]{1,0:T(8,128)S(1)}) custom-call(s32[3]{0:T(128)S(1)} %pad_add_fusion.pos, f32[1024,1024]{1,0:T(8,128)S(1)} %get-tuple-element.15.scores, f32[16,128]{1,0:T(8,128)S(1)} %get-tuple-element.19.row_lse, ...), custom_call_target="tpu_custom_call" | custom-call | tf_op jit(solution)/shard_map/pallas_call | solution.py:162
  87.3 1.6 %collective-permute-start.20 = (f32[512,1024]{1,0:T(8,128)}, f32[512,1024]{1,0:T(8,128)}, u32[]{:S(2)}, u32[]{:S(2)}) collective-permute-start(f32[512,1024]{1,0:T(8,128)} %get-tuple-element.24), channel_id=1, source_target_pairs={{0,2},{2,0},{1,3},{3,1},{4,6},{6,4},{5,7},{7,5},{8,10},{10,8},{9,1... | collective-permute-start | bytes 6291464 | tf_op jit(solution)/shard_map/ppermute | solution.py:43
  89.0 3.8 %multiply_convert_fusion = f16[1024,1024]{1,0:T(8,128)(2,1)} fusion(bf16[1024,1024]{1,0:T(8,128)(2,1)S(1)} %get-tuple-element.25, bf16[1024,1024]{1,0:T(8,128)(2,1)S(1)} %get-tuple-element.26), kind=kOutput, calls=%fused_computation | convolution fusion | flops 2149580800 | bytes 6291456 | tf_op jit(solution)/shard_map/dot_general | solution.py:232
  92.7 4.6 %all-to-all-start.3 = ((f16[16,64,1024]{2,1,0:T(8,128)(2,1)}), f16[16,64,1024]{2,1,0:T(8,128)(2,1)}, u32[]{:S(2)}, u32[]{:S(2)}) async-start(f16[16,64,1024]{2,1,0:T(8,128)(2,1)} %bitcast.18), calls=%async_computation.3 | async-start | bytes 4194304 | tf_op jit(solution)/shard_map/all_to_all | solution.py:31
  97.4 1.2 collective-permute-done.15
  98.9 2.1 %collective-permute-done.16 = f32[8,128]{1,0:T(8,128)S(1)} collective-permute-done((f32[8,128]{1,0:T(8,128)S(1)}, f32[8,128]{1,0:T(8,128)S(1)}, u32[]{:S(2)}, u32[]{:S(2)}) %collective-permute-start.16) | collective-permute-done | bytes 4128 | tf_op jit(solution)/shard_map/ppermute | solution.py:39
  102.2 4.5 %collective-permute-start.17 = (f32[8,128]{1,0:T(8,128)S(1)}, f32[8,128]{1,0:T(8,128)S(1)}, u32[]{:S(2)}, u32[]{:S(2)}) collective-permute-start(f32[8,128]{1,0:T(8,128)S(1)} %add.126), channel_id=1, source_target_pairs={{0,16},{4,20},{8,24},{12,28},{16,0},{20,4},{24,8},{28,12},{1,17},{... | collective-permute-start | bytes 12296 | tf_op jit(solution)/shard_map/ppermute | solution.py:39
  106.7 1.8 %collective-permute-done.17 = f32[8,128]{1,0:T(8,128)S(1)} collective-permute-done((f32[8,128]{1,0:T(8,128)S(1)}, f32[8,128]{1,0:T(8,128)S(1)}, u32[]{:S(2)}, u32[]{:S(2)}) %collective-permute-start.17) | collective-permute-done | bytes 4128 | tf_op jit(solution)/shard_map/ppermute | solution.py:39
  109.1 1.9 %fusion.1 = (f16[64,1024]{1,0:T(8,128)(2,1)S(1)}, f16[64,1024]{1,0:T(8,128)(2,1)S(1)}, f16[64,1024]{1,0:T(8,128)(2,1)S(1)}, f16[64,1024]{1,0:T(8,128)(2,1)S(1)},...) fusion(f32[512,1024]{1,0:T(8,128)} %collective-permute-done.20, ...), kind=kLoop, calls=%fused_computation.4 | loop fusion | flops 917504 | bytes 4587520 | tf_op jit(solution)/shard_map/convert_element_type | solution.py:240
  110.9 3.0 %collective-permute-start.25 = (f16[64,1024]{1,0:T(8,128)(2,1)S(1)}, f16[64,1024]{1,0:T(8,128)(2,1)S(1)}, u32[]{:S(2)}, u32[]{:S(2)}) collective-permute-start(f16[64,1024]{1,0:T(8,128)(2,1)S(1)} %get-tuple-element.29), channel_id=1, source_target_pairs={{0,24},{4,28},{8,0},{12,4},{16,8},{20,12},{24,16},{28,20},{1,25},{... | collective-permute-start | bytes 393224 | tf_op jit(solution)/shard_map/ppermute | solution.py:35
  114.0 3.1 %collective-permute-start.23 = (f16[64,1024]{1,0:T(8,128)(2,1)S(1)}, f16[64,1024]{1,0:T(8,128)(2,1)}, u32[]{:S(2)}, u32[]{:S(2)}) collective-permute-start(f16[64,1024]{1,0:T(8,128)(2,1)S(1)} %get-tuple-element.31), channel_id=1, source_target_pairs={{0,20},{4,24},{8,28},{12,0},{16,4},{20,8},{24,12},{28,16},{1,21},{... | collective-permute-start | bytes 393224 | tf_op jit(solution)/shard_map/ppermute | solution.py:35
  117.2 4.0 %collective-permute-start.21 = (f16[64,1024]{1,0:T(8,128)(2,1)S(1)}, f16[64,1024]{1,0:T(8,128)(2,1)}, u32[]{:S(2)}, u32[]{:S(2)}) collective-permute-start(f16[64,1024]{1,0:T(8,128)(2,1)S(1)} %get-tuple-element.33), channel_id=1, source_target_pairs={{0,16},{4,20},{8,24},{12,28},{16,0},{20,4},{24,8},{28,12},{1,17},{... | collective-permute-start | bytes 393224 | tf_op jit(solution)/shard_map/ppermute | solution.py:35
  121.3 7.0 %all-to-all-done.3 = f16[16,64,1024]{2,1,0:T(8,128)(2,1)} async-done(((f16[16,64,1024]{2,1,0:T(8,128)(2,1)}), f16[16,64,1024]{2,1,0:T(8,128)(2,1)}, u32[]{:S(2)}, u32[]{:S(2)}) %all-to-all-start.3) | async-done | bytes 2097184 | tf_op jit(solution)/shard_map/all_to_all | solution.py:31
  128.3 2.7 %fusion.12 = f32[64,1024]{1,0:T(8,128)} fusion(f16[16,64,1024]{2,1,0:T(8,128)(2,1)} %all-to-all-done.3, f32[]{:T(128)} %bitcast.5), kind=kLoop, calls=%fused_computation.22 | loop fusion | flops 2097152 | bytes 2359300 | tf_op jit(solution)/shard_map/mul | solution.py:247
  131.4 2.3 %collective-permute-start.27 = (f16[64,1024]{1,0:T(8,128)(2,1)S(1)}, f16[64,1024]{1,0:T(8,128)(2,1)S(1)}, u32[]{:S(2)}, u32[]{:S(2)}) collective-permute-start(f16[64,1024]{1,0:T(8,128)(2,1)S(1)} %get-tuple-element.28), channel_id=1, source_target_pairs={{0,28},{4,0},{8,4},{12,8},{16,12},{20,16},{24,20},{28,24},{1,29},{... | collective-permute-start | bytes 393224 | tf_op jit(solution)/shard_map/ppermute | solution.py:35
  133.8 1.2 fusion.11
  135.0 6.7 %collective-permute-done.26 = f16[64,1024]{1,0:T(8,128)(2,1)S(1)} collective-permute-done((f16[64,1024]{1,0:T(8,128)(2,1)S(1)}, f16[64,1024]{1,0:T(8,128)(2,1)S(1)}, u32[]{:S(2)}, u32[]{:S(2)}) %collective-permute-start.26) | collective-permute-done | bytes 131104 | tf_op jit(solution)/shard_map/ppermute | solution.py:35
  (61 shorter events, 11.1 us)
Async XLA Ops:
  3.2 46.7 %copy-start.3 = (bf16[64,1024]{1,0:T(8,128)(2,1)S(1)}, bf16[64,1024]{1,0:T(8,128)(2,1)}, u32[]{:S(2)}) copy-start(bf16[64,1024]{1,0:T(8,128)(2,1)} %own_text.1) | copy-start | bytes 393220
  3.2 46.7 %all-to-all-start = ((bf16[16,64,1024]{2,1,0:T(8,128)(2,1)}), bf16[16,64,1024]{2,1,0:T(8,128)(2,1)S(1)}, u32[]{:S(2)}, u32[]{:S(2)}) async-start(bf16[16,64,1024]{2,1,0:T(8,128)(2,1)} %broadcast_in_dim.2), calls=%async_computation | async-start | bytes 4194304 | tf_op jit(solution)/shard_map/all_to_all | solution.py:31
  11.0 9.9 %collective-permute-start.7 = (bf16[64,1024]{1,0:T(8,128)(2,1)S(1)}, bf16[64,1024]{1,0:T(8,128)(2,1)S(1)}, u32[]{:S(2)}, u32[]{:S(2)}) collective-permute-start(bf16[64,1024]{1,0:T(8,128)(2,1)S(1)} %constant_dynamic-slice_fusion.refs_0_), channel_id=1, source_target_pairs={{0,2},{2,0},{1,3},{3,1},{4,6},{6,4},{5,7},{7,5},{8,10},{10,8},{9,1... | collective-permute-start | bytes 393224 | tf_op jit(solution)/shard_map/ppermute | solution.py:43
  12.0 13.3 %collective-permute-start.6 = (bf16[64,1024]{1,0:T(8,128)(2,1)S(1)}, bf16[64,1024]{1,0:T(8,128)(2,1)S(1)}, u32[]{:S(2)}, u32[]{:S(2)}) collective-permute-start(bf16[64,1024]{1,0:T(8,128)(2,1)S(1)} %constant_dynamic-slice_fusion.refs_0_), channel_id=1, source_target_pairs={{0,4},{4,8},{8,12},{12,16},{16,20},{20,24},{24,28},{28,0},{1,5},{5... | collective-permute-start | bytes 393224 | tf_op jit(solution)/shard_map/ppermute | solution.py:35
  13.6 14.1 %collective-permute-start.5 = (bf16[64,1024]{1,0:T(8,128)(2,1)S(1)}, bf16[64,1024]{1,0:T(8,128)(2,1)S(1)}, u32[]{:S(2)}, u32[]{:S(2)}) collective-permute-start(bf16[64,1024]{1,0:T(8,128)(2,1)S(1)} %constant_dynamic-slice_fusion.refs_0_), channel_id=1, source_target_pairs={{0,8},{4,12},{8,16},{12,20},{16,24},{20,28},{24,0},{28,4},{1,9},{5... | collective-permute-start | bytes 393224 | tf_op jit(solution)/shard_map/ppermute | solution.py:35
  16.6 20.7 %collective-permute-start.4 = (bf16[64,1024]{1,0:T(8,128)(2,1)S(1)}, bf16[64,1024]{1,0:T(8,128)(2,1)S(1)}, u32[]{:S(2)}, u32[]{:S(2)}) collective-permute-start(bf16[64,1024]{1,0:T(8,128)(2,1)S(1)} %constant_dynamic-slice_fusion.refs_0_), channel_id=1, source_target_pairs={{0,12},{4,16},{8,20},{12,24},{16,28},{20,0},{24,4},{28,8},{1,13},{... | collective-permute-start | bytes 393224 | tf_op jit(solution)/shard_map/ppermute | solution.py:35
  20.4 19.0 %collective-permute-start.3 = (bf16[64,1024]{1,0:T(8,128)(2,1)S(1)}, bf16[64,1024]{1,0:T(8,128)(2,1)S(1)}, u32[]{:S(2)}, u32[]{:S(2)}) collective-permute-start(bf16[64,1024]{1,0:T(8,128)(2,1)S(1)} %constant_dynamic-slice_fusion.refs_0_), channel_id=1, source_target_pairs={{0,16},{4,20},{8,24},{12,28},{16,0},{20,4},{24,8},{28,12},{1,17},{... | collective-permute-start | bytes 393224 | tf_op jit(solution)/shard_map/ppermute | solution.py:35
  20.9 18.5 %collective-permute-start.2 = (bf16[64,1024]{1,0:T(8,128)(2,1)S(1)}, bf16[64,1024]{1,0:T(8,128)(2,1)S(1)}, u32[]{:S(2)}, u32[]{:S(2)}) collective-permute-start(bf16[64,1024]{1,0:T(8,128)(2,1)S(1)} %constant_dynamic-slice_fusion.refs_0_), channel_id=1, source_target_pairs={{0,20},{4,24},{8,28},{12,0},{16,4},{20,8},{24,12},{28,16},{1,21},{... | collective-permute-start | bytes 393224 | tf_op jit(solution)/shard_map/ppermute | solution.py:35
  25.3 20.3 %collective-permute-start.1 = (bf16[64,1024]{1,0:T(8,128)(2,1)S(1)}, bf16[64,1024]{1,0:T(8,128)(2,1)S(1)}, u32[]{:S(2)}, u32[]{:S(2)}) collective-permute-start(bf16[64,1024]{1,0:T(8,128)(2,1)S(1)} %constant_dynamic-slice_fusion.refs_0_), channel_id=1, source_target_pairs={{0,24},{4,28},{8,0},{12,4},{16,8},{20,12},{24,16},{28,20},{1,25},{... | collective-permute-start | bytes 393224 | tf_op jit(solution)/shard_map/ppermute | solution.py:35
  27.7 18.5 %collective-permute-start = (bf16[64,1024]{1,0:T(8,128)(2,1)S(1)}, bf16[64,1024]{1,0:T(8,128)(2,1)}, u32[]{:S(2)}, u32[]{:S(2)}) collective-permute-start(bf16[64,1024]{1,0:T(8,128)(2,1)S(1)} %constant_dynamic-slice_fusion.refs_0_), channel_id=1, source_target_pairs={{0,28},{4,0},{8,4},{12,8},{16,12},{20,16},{24,20},{28,24},{1,29},{... | collective-permute-start | bytes 393224 | tf_op jit(solution)/shard_map/ppermute | solution.py:35
  37.3 9.4 %collective-permute-start.14 = (bf16[64,1024]{1,0:T(8,128)(2,1)S(1)}, bf16[64,1024]{1,0:T(8,128)(2,1)S(1)}, u32[]{:S(2)}, u32[]{:S(2)}) collective-permute-start(bf16[64,1024]{1,0:T(8,128)(2,1)S(1)} %collective-permute-done.6.refs_7_), channel_id=1, source_target_pairs={{0,2},{2,0},{1,3},{3,1},{4,6},{6,4},{5,7},{7,5},{8,10},{10,8},{9,1... | collective-permute-start | bytes 393224 | tf_op jit(solution)/shard_map/ppermute | solution.py:43
  39.4 8.1 %collective-permute-start.13 = (bf16[64,1024]{1,0:T(8,128)(2,1)S(1)}, bf16[64,1024]{1,0:T(8,128)(2,1)S(1)}, u32[]{:S(2)}, u32[]{:S(2)}) collective-permute-start(bf16[64,1024]{1,0:T(8,128)(2,1)S(1)} %collective-permute-done.5.refs_6_), channel_id=1, source_target_pairs={{0,2},{2,0},{1,3},{3,1},{4,6},{6,4},{5,7},{7,5},{8,10},{10,8},{9,1... | collective-permute-start | bytes 393224 | tf_op jit(solution)/shard_map/ppermute | solution.py:43
  39.4 9.9 %collective-permute-start.12 = (bf16[64,1024]{1,0:T(8,128)(2,1)S(1)}, bf16[64,1024]{1,0:T(8,128)(2,1)}, u32[]{:S(2)}, u32[]{:S(2)}) collective-permute-start(bf16[64,1024]{1,0:T(8,128)(2,1)S(1)} %collective-permute-done.4.refs_5_), channel_id=1, source_target_pairs={{0,2},{2,0},{1,3},{3,1},{4,6},{6,4},{5,7},{7,5},{8,10},{10,8},{9,1... | collective-permute-start | bytes 393224 | tf_op jit(solution)/shard_map/ppermute | solution.py:43
  45.7 3.6 %collective-permute-start.11 = (bf16[64,1024]{1,0:T(8,128)(2,1)S(1)}, bf16[64,1024]{1,0:T(8,128)(2,1)}, u32[]{:S(2)}, u32[]{:S(2)}) collective-permute-start(bf16[64,1024]{1,0:T(8,128)(2,1)S(1)} %collective-permute-done.3.refs_4_), channel_id=1, source_target_pairs={{0,2},{2,0},{1,3},{3,1},{4,6},{6,4},{5,7},{7,5},{8,10},{10,8},{9,1... | collective-permute-start | bytes 393224 | tf_op jit(solution)/shard_map/ppermute | solution.py:43
  46.3 3.0 %collective-permute-start.10 = (bf16[64,1024]{1,0:T(8,128)(2,1)S(1)}, bf16[64,1024]{1,0:T(8,128)(2,1)}, u32[]{:S(2)}, u32[]{:S(2)}) collective-permute-start(bf16[64,1024]{1,0:T(8,128)(2,1)S(1)} %collective-permute-done.2.refs_3_), channel_id=1, source_target_pairs={{0,2},{2,0},{1,3},{3,1},{4,6},{6,4},{5,7},{7,5},{8,10},{10,8},{9,1... | collective-permute-start | bytes 393224 | tf_op jit(solution)/shard_map/ppermute | solution.py:43
  47.4 1.9 %collective-permute-start.9 = (bf16[64,1024]{1,0:T(8,128)(2,1)S(1)}, bf16[64,1024]{1,0:T(8,128)(2,1)}, u32[]{:S(2)}, u32[]{:S(2)}) collective-permute-start(bf16[64,1024]{1,0:T(8,128)(2,1)S(1)} %collective-permute-done.1.refs_2_), channel_id=1, source_target_pairs={{0,2},{2,0},{1,3},{3,1},{4,6},{6,4},{5,7},{7,5},{8,10},{10,8},{9,1... | collective-permute-start | bytes 393224 | tf_op jit(solution)/shard_map/ppermute | solution.py:43
  48.1 1.8 %collective-permute-start.8 = (bf16[64,1024]{1,0:T(8,128)(2,1)}, bf16[64,1024]{1,0:T(8,128)(2,1)}, u32[]{:S(2)}, u32[]{:S(2)}) collective-permute-start(bf16[64,1024]{1,0:T(8,128)(2,1)} %collective-permute-done.refs_1_), channel_id=1, source_target_pairs={{0,2},{2,0},{1,3},{3,1},{4,6},{6,4},{5,7},{7,5},{8,10},{10,8},{9,1... | collective-permute-start | bytes 393224 | tf_op jit(solution)/shard_map/ppermute | solution.py:43
  87.3 21.7 %collective-permute-start.20 = (f32[512,1024]{1,0:T(8,128)}, f32[512,1024]{1,0:T(8,128)}, u32[]{:S(2)}, u32[]{:S(2)}) collective-permute-start(f32[512,1024]{1,0:T(8,128)} %get-tuple-element.24), channel_id=1, source_target_pairs={{0,2},{2,0},{1,3},{3,1},{4,6},{6,4},{5,7},{7,5},{8,10},{10,8},{9,1... | collective-permute-start | bytes 6291464 | tf_op jit(solution)/shard_map/ppermute | solution.py:43
  92.7 16.3 %copy-start.2 = (f32[512,1024]{1,0:T(8,128)S(1)}, f32[512,1024]{1,0:T(8,128)}, u32[]{:S(2)}) copy-start(f32[512,1024]{1,0:T(8,128)} %copy-done.1) | copy-start | bytes 6291460
  92.7 35.5 %all-to-all-start.3 = ((f16[16,64,1024]{2,1,0:T(8,128)(2,1)}), f16[16,64,1024]{2,1,0:T(8,128)(2,1)}, u32[]{:S(2)}, u32[]{:S(2)}) async-start(f16[16,64,1024]{2,1,0:T(8,128)(2,1)} %bitcast.18), calls=%async_computation.3 | async-start | bytes 4194304 | tf_op jit(solution)/shard_map/all_to_all | solution.py:31
  97.3 1.3 collective-permute-start.15
  98.6 2.5 %collective-permute-start.16 = (f32[8,128]{1,0:T(8,128)S(1)}, f32[8,128]{1,0:T(8,128)S(1)}, u32[]{:S(2)}, u32[]{:S(2)}) collective-permute-start(f32[8,128]{1,0:T(8,128)S(1)} %add.125), channel_id=1, source_target_pairs={{0,4},{4,0},{8,12},{12,8},{16,20},{20,16},{24,28},{28,24},{1,5},{5... | collective-permute-start | bytes 12296 | tf_op jit(solution)/shard_map/ppermute | solution.py:39
  101.0 5.7 %collective-permute-start.19 = (f32[8,128]{1,0:T(8,128)S(1)}, f32[8,128]{1,0:T(8,128)S(1)}, u32[]{:S(2)}, u32[]{:S(2)}) collective-permute-start(f32[8,128]{1,0:T(8,128)S(1)} %add.126), channel_id=1, source_target_pairs={{0,24},{4,28},{8,16},{12,20},{16,8},{20,12},{24,0},{28,4},{1,25},{... | collective-permute-start | bytes 12296 | tf_op jit(solution)/shard_map/ppermute | solution.py:39
  101.6 5.1 %collective-permute-start.18 = (f32[8,128]{1,0:T(8,128)S(1)}, f32[8,128]{1,0:T(8,128)S(1)}, u32[]{:S(2)}, u32[]{:S(2)}) collective-permute-start(f32[8,128]{1,0:T(8,128)S(1)} %add.126), channel_id=1, source_target_pairs={{0,8},{4,12},{8,0},{12,4},{16,24},{20,28},{24,16},{28,20},{1,9},{5... | collective-permute-start | bytes 12296 | tf_op jit(solution)/shard_map/ppermute | solution.py:39
  102.2 6.4 %collective-permute-start.17 = (f32[8,128]{1,0:T(8,128)S(1)}, f32[8,128]{1,0:T(8,128)S(1)}, u32[]{:S(2)}, u32[]{:S(2)}) collective-permute-start(f32[8,128]{1,0:T(8,128)S(1)} %add.126), channel_id=1, source_target_pairs={{0,16},{4,20},{8,24},{12,28},{16,0},{20,4},{24,8},{28,12},{1,17},{... | collective-permute-start | bytes 12296 | tf_op jit(solution)/shard_map/ppermute | solution.py:39
  110.9 20.1 %collective-permute-start.25 = (f16[64,1024]{1,0:T(8,128)(2,1)S(1)}, f16[64,1024]{1,0:T(8,128)(2,1)S(1)}, u32[]{:S(2)}, u32[]{:S(2)}) collective-permute-start(f16[64,1024]{1,0:T(8,128)(2,1)S(1)} %get-tuple-element.29), channel_id=1, source_target_pairs={{0,24},{4,28},{8,0},{12,4},{16,8},{20,12},{24,16},{28,20},{1,25},{... | collective-permute-start | bytes 393224 | tf_op jit(solution)/shard_map/ppermute | solution.py:35
  114.0 17.5 %collective-permute-start.24 = (f16[64,1024]{1,0:T(8,128)(2,1)S(1)}, f16[64,1024]{1,0:T(8,128)(2,1)S(1)}, u32[]{:S(2)}, u32[]{:S(2)}) collective-permute-start(f16[64,1024]{1,0:T(8,128)(2,1)S(1)} %get-tuple-element.30), channel_id=1, source_target_pairs={{0,8},{4,12},{8,16},{12,20},{16,24},{20,28},{24,0},{28,4},{1,9},{5... | collective-permute-start | bytes 393224 | tf_op jit(solution)/shard_map/ppermute | solution.py:35
  114.0 19.8 %collective-permute-start.23 = (f16[64,1024]{1,0:T(8,128)(2,1)S(1)}, f16[64,1024]{1,0:T(8,128)(2,1)}, u32[]{:S(2)}, u32[]{:S(2)}) collective-permute-start(f16[64,1024]{1,0:T(8,128)(2,1)S(1)} %get-tuple-element.31), channel_id=1, source_target_pairs={{0,20},{4,24},{8,28},{12,0},{16,4},{20,8},{24,12},{28,16},{1,21},{... | collective-permute-start | bytes 393224 | tf_op jit(solution)/shard_map/ppermute | solution.py:35
  117.1 16.7 %collective-permute-start.22 = (f16[64,1024]{1,0:T(8,128)(2,1)S(1)}, f16[64,1024]{1,0:T(8,128)(2,1)}, u32[]{:S(2)}, u32[]{:S(2)}) collective-permute-start(f16[64,1024]{1,0:T(8,128)(2,1)S(1)} %get-tuple-element.32), channel_id=1, source_target_pairs={{0,12},{4,16},{8,20},{12,24},{16,28},{20,0},{24,4},{28,8},{1,13},{... | collective-permute-start | bytes 393224 | tf_op jit(solution)/shard_map/ppermute | solution.py:35
  117.2 16.5 %collective-permute-start.21 = (f16[64,1024]{1,0:T(8,128)(2,1)S(1)}, f16[64,1024]{1,0:T(8,128)(2,1)}, u32[]{:S(2)}, u32[]{:S(2)}) collective-permute-start(f16[64,1024]{1,0:T(8,128)(2,1)S(1)} %get-tuple-element.33), channel_id=1, source_target_pairs={{0,16},{4,20},{8,24},{12,28},{16,0},{20,4},{24,8},{28,12},{1,17},{... | collective-permute-start | bytes 393224 | tf_op jit(solution)/shard_map/ppermute | solution.py:35
  131.0 10.8 %collective-permute-start.26 = (f16[64,1024]{1,0:T(8,128)(2,1)S(1)}, f16[64,1024]{1,0:T(8,128)(2,1)S(1)}, u32[]{:S(2)}, u32[]{:S(2)}) collective-permute-start(f16[64,1024]{1,0:T(8,128)(2,1)S(1)} %get-tuple-element.27), channel_id=1, source_target_pairs={{0,4},{4,8},{8,12},{12,16},{16,20},{20,24},{24,28},{28,0},{1,5},{5... | collective-permute-start | bytes 393224 | tf_op jit(solution)/shard_map/ppermute | solution.py:35
  131.4 10.3 %collective-permute-start.27 = (f16[64,1024]{1,0:T(8,128)(2,1)S(1)}, f16[64,1024]{1,0:T(8,128)(2,1)S(1)}, u32[]{:S(2)}, u32[]{:S(2)}) collective-permute-start(f16[64,1024]{1,0:T(8,128)(2,1)S(1)} %get-tuple-element.28), channel_id=1, source_target_pairs={{0,28},{4,0},{8,4},{12,8},{16,12},{20,16},{24,20},{28,24},{1,29},{... | collective-permute-start | bytes 393224 | tf_op jit(solution)/shard_map/ppermute | solution.py:35
  (6 other events, 18.9 us)
